TPU v7x, 256 devices: a whole 4x4x8 slice. The times are simulated.
256 devices in a mesh: tm: 8 (over x_lo, y), lat: 16 (over z, x_hi), ens: 2 (over core).
Axes of the slice: x: 4 (x_hi: 2, x_lo: 2; x = x_hi * 2 + x_lo), y: 4, z: 8, core: 2. Of those that a mesh axis runs over, the one named last changes fastest.
Arguments:
- increment: float32 [8, 8, 256, 1440], P('tm', None, 'lat'), may hold values from -6 to 6
- wind_lon: float32 [8, 8, 256, 1440], P('tm', None, 'lat'), may hold values from -0.45 to 0.45
- wind_lat: float32 [8, 8, 256, 1440], P('tm', None, 'lat'), may hold values from -0.45 to 0.45
- model_precision: float32 [8], replicated, may hold values from 0.5 to 4
- perturbations: float32 [32, 8, 256, 1440], P('ens', 'tm', 'lat'), may hold values from -0.14478652 to 0.14478652
- obs_rows: int32 [8, 512], P('tm', 'lat'), may hold values from 0 to 127
- obs_jacobian: float32 [8, 512, 16, 1440], P('tm', 'lat'), may hold values from -0.15625 to 0.15625
- obs_values: float32 [8, 512, 16], P('tm', 'lat'), may hold values from -6 to 6
- obs_precision: float32 [8, 512, 16], P('tm', 'lat'), may hold values from 0.5 to 2
- obs_counts: int32 [8, 512], P('tm', 'lat'), may hold values from 1 to 16
Outputs:
- grad_state: float32 [8, 8, 256, 1440], P('tm', None, 'lat')
- forcing_step: float32 [8, 256, 1440], P('tm', 'lat')
Inputs may be any that keep to these rules, and one draw needn't show every extreme that they name: `obs_rows`: block j of band b reads level r // 16 and latitude b * 16 + r % 16, where r is its entry; several blocks may read the same row. `obs_counts`: only the first count slots of a block hold observations.
All inputs are finite; a program needn't handle non-finite values.
Results may differ from a plain program's by a relative error of at most 0.0003.
Values sent between devices are 32-bit elements; how exact they have to be, the bound alone decides.
No kernel may reach another device: no remote copies, remote signals or barrier semaphores. Data moves between devices by JAX's collectives and lax.ppermute only.
A program may use at most 64 MiB of HBM per device.

v0:
```python
import jax
import jax.numpy as jnp
from jax import lax
from jax.sharding import Mesh
from jax.sharding import PartitionSpec as P

MEM = 32
STEPS = 4
TM = ("tm_0", "tm_1")
LAT = ("lat_0", "lat_1")
TM_LAT = ("tm_0", "tm_1", "lat_0", "lat_1")


def shifted(value, axis, steps):
    count = lax.axis_size(axis)
    leading, last = (max(0, -steps), min(count, count - steps))
    return lax.ppermute(value, axis, [(source, source + steps) for source in range(leading, last)])


def padded(value, sides, width):
    for axis, dim in sides:
        peers, length = (lax.axis_size(axis), value.shape[dim])
        up = [(i, (i + 1) % peers) for i in range(peers - 1)]
        down = [(j, i) for i, j in up]
        last = lax.slice_in_dim(value, length - width, length, axis=dim)
        leading = lax.slice_in_dim(value, 0, width, axis=dim)
        before = lax.ppermute(last, axis, up)
        after = lax.ppermute(leading, axis, down)
        value = jnp.concatenate([before, value, after], axis=dim)
    return value


def in_blocks(value, dim, peers):
    shape = value.shape
    pieces = value.reshape(*shape[:dim], peers, shape[dim] // peers, *shape[dim + 1 :])
    return jnp.moveaxis(pieces, dim, 0)


def sent_and_summed(value, axis, dim):
    peers = lax.axis_size(axis)
    pieces = lax.all_to_all(in_blocks(value, dim, peers), axis, 0, 0, tiled=True)
    return jnp.sum(pieces, axis=0)


def by_axis(value, axes):
    for axis in axes:
        value = lax.psum(value, axis)
    return value


def from_everyone(value, axis):
    peers = lax.axis_size(axis)
    return lax.all_to_all(
        jnp.broadcast_to(value[None], (peers, *value.shape)), axis, 0, 0, tiled=True
    )


def taken_together(value, axis):
    return from_everyone(value, axis).sum(axis=0)


def coefficients(wind_lon, wind_lat):
    center = 1.0 - wind_lon * wind_lon - wind_lat * wind_lat
    plus_lon = 0.5 * (wind_lon * wind_lon - wind_lon)
    minus_lon = 0.5 * (wind_lon * wind_lon + wind_lon)
    plus_lat = 0.5 * (wind_lat * wind_lat - wind_lat)
    minus_lat = 0.5 * (wind_lat * wind_lat + wind_lat)
    return (center, plus_lon, minus_lon, plus_lat, minus_lat)


def trim_coefs(coefs, first, last):
    return tuple((item[:, first:last] for item in coefs))


def advect_inner(field, coefs):
    center, plus_lon, minus_lon, plus_lat, minus_lat = trim_coefs(coefs, 1, coefs[0].shape[1] - 1)
    middle = field[:, 1:-1]
    return (
        center * middle
        + plus_lon * jnp.roll(middle, -1, 2)
        + minus_lon * jnp.roll(middle, 1, 2)
        + plus_lat * field[:, 2:]
        + minus_lat * field[:, :-2]
    )


def adjoint_inner(field, coefs):
    center, plus_lon, minus_lon, plus_lat, minus_lat = coefs
    middle = field[:, 1:-1]
    inner_plus = plus_lon[:, 1:-1]
    inner_minus = minus_lon[:, 1:-1]
    from_south = (plus_lat * field)[:, :-2]
    from_north = (minus_lat * field)[:, 2:]
    return (
        center[:, 1:-1] * middle
        + jnp.roll(inner_plus * middle, 1, 2)
        + jnp.roll(inner_minus * middle, -1, 2)
        + from_south
        + from_north
    )


def on_device(
    increment,
    wind_lon,
    wind_lat,
    model_precision,
    perturbations,
    obs_rows,
    obs_jacobian,
    obs_values,
    obs_precision,
    obs_counts,
):
    highest = lax.Precision.HIGHEST
    level_prec = model_precision[:, None, None]
    band_rows = increment.shape[2]
    next_increment = shifted(increment[0], TM, -1)
    stacked = jnp.stack([increment[0], wind_lon[0], wind_lat[0]])
    widened = padded(stacked, ((LAT, 2),), STEPS)
    wide_coefs = coefficients(widened[1], widened[2])
    width = widened.shape[2]
    field = widened[0]
    for repeat in range(STEPS):
        field = advect_inner(field, trim_coefs(wide_coefs, repeat, width - repeat))
    prior = shifted(field, TM, 1)
    mismatch = level_prec * (increment[0] - prior)
    not_last = (lax.axis_index(TM) < lax.axis_size(TM) - 1).astype(jnp.float32)
    later = not_last * (level_prec * (next_increment - field))
    levels, lat_rows, lon_cells = field.shape
    flat = field.reshape(levels * lat_rows, lon_cells)
    row_ids = jnp.arange(levels * lat_rows, dtype=jnp.int32)
    onehot = (obs_rows[0][:, None] == row_ids[None, :]).astype(jnp.float32)
    picked = jnp.dot(onehot, flat, precision=highest)
    jacobian = obs_jacobian[0]
    evolved = jnp.einsum("jon,jn->jo", jacobian, picked, precision=highest)
    slots = jnp.arange(jacobian.shape[1], dtype=jnp.int32)
    used = (slots[None, :] < obs_counts[0][:, None]).astype(jnp.float32)
    weighted = obs_precision[0] * (evolved - obs_values[0]) * used
    force = jnp.einsum("jon,jo->jn", jacobian, weighted, precision=highest)
    placed = jnp.dot(onehot.T, force, precision=highest).reshape(levels, lat_rows, lon_cells)
    adjoint = placed - later
    forcing = adjoint
    spread = padded(adjoint[None], ((LAT, 2),), STEPS)[0]
    for repeat in range(STEPS):
        spread = adjoint_inner(spread, trim_coefs(wide_coefs, repeat, width - repeat))
        if repeat + 1 < STEPS:
            offset = STEPS - repeat - 1
            forcing = forcing + spread[:, offset : offset + band_rows]
    adjoint = spread
    grad_state = (adjoint + mismatch)[None]
    reduced = sent_and_summed(forcing, TM, 0)
    local_coef = jnp.einsum("mlan,lan->m", perturbations, reduced, precision=highest)
    member_coef = by_axis(local_coef, TM_LAT)
    partial_sum = jnp.einsum("m,mlan->lan", member_coef, perturbations, precision=highest)
    combined = taken_together(partial_sum, "ens")
    forcing_step = -combined / (MEM - 1.0)
    return (grad_state, forcing_step)


def solution(mesh):
    torus = Mesh(
        mesh.devices.reshape(2, 4, 8, 2, mesh.shape["ens"]),
        ("tm_0", "tm_1", "lat_0", "lat_1", "ens"),
    )
    in_specs = (
        P(TM, None, LAT, None),
        P(TM, None, LAT, None),
        P(TM, None, LAT, None),
        P(),
        P("ens", TM, LAT, None),
        P(TM, LAT),
        P(TM, LAT, None, None),
        P(TM, LAT, None),
        P(TM, LAT, None),
        P(TM, LAT),
    )
    out_specs = (P(TM, None, LAT, None), P(TM, LAT, None))
    return jax.shard_map(
        on_device, mesh=torus, in_specs=in_specs, out_specs=out_specs, check_vma=False
    )
```

profile of v0, /device:TPU:1, one launch (start us, length us, event | category | flops | bytes accessed | tf_op | source)
XLA Modules:
  0.0 161.9 jit_solution(10306627762371642672)
XLA Ops:
  0.7 1.3 constant_dynamic-update-slice_fusion.2
  3.4 1.4 copy-done.12
  4.8 1.2 fusion.58
  6.0 6.3 %collective-permute-start = (f32[3,8,4,1440]{3,2,1,0:T(4,128)}, f32[3,8,4,1440]{3,2,1,0:T(4,128)}, u32[]{:S(2)}, u32[]{:S(2)}) collective-permute-start(f32[3,8,4,1440]{3,2,1,0:T(4,128)} %get-tuple-element.7), channel_id=1, source_target_pairs={{0,2},{2,4},{4,6},{6,8},{8,10},{10,12},{12,14},{14,16},{16,18},{18... | collective-permute-start | bytes 1658888 | tf_op jit(solution)/shard_map/ppermute | solution.py:27
  12.3 1.3 collective-permute-start.1
  13.6 1.3 collective-permute-start.2
  14.9 21.5 %collective-permute-done = f32[3,8,4,1440]{3,2,1,0:T(4,128)} collective-permute-done((f32[3,8,4,1440]{3,2,1,0:T(4,128)}, f32[3,8,4,1440]{3,2,1,0:T(4,128)}, u32[]{:S(2)}, u32[]{:S(2)}) %collective-permute-start) | collective-permute-done | bytes 552992 | tf_op jit(solution)/shard_map/ppermute | solution.py:27
  36.4 2.6 %pad_maximum_fusion = f32[3,8,24,1440]{3,2,1,0:T(8,128)S(1)} fusion(f32[3,8,4,1440]{3,2,1,0:T(4,128)} %collective-permute-done.1, f32[3,8,16,1440]{3,2,1,0:T(8,128)} %copy-done.12, f32[3,8,4,1440]{3,2,1,0:T(4,128)} %collective-permute-done), kind=kLoop, calls=%fused_computation | loop fusion | flops 1658880 | bytes 6635520 | tf_op jit(solution)/shard_map/concatenate | solution.py:29
  40.6 2.8 %fusion.61 = (f32[8,22,1440]{2,1,0:T(8,128)}, f32[8,22,1440]{2,1,0:T(8,128)S(1)}, f32[8,22,1440]{2,1,0:T(8,128)}) fusion(f32[8,24,1440]{2,1,0:T(8,128)S(1)} %get-tuple-element.2, f32[8,24,1440]{2,1,0:T(8,128)S(1)} %slice_bitcast_fusion, f32[8,24,1440]{2,1,0:T(8,128)S(1)} %get-tuple-element.3, f32[8,22,1439]{2,1,0:T(8,128)S(1)} %get-tuple-element.41, ...), kind=kLoop, calls=%fused_computation.122 | loop fusion | flops 2787840 | bytes 13178880 | tf_op jit(solution)/shard_map/slice | solution.py:72
  43.9 2.8 %fusion.60 = (f32[8,20,1440]{2,1,0:T(8,128)}, f32[8,20,1440]{2,1,0:T(8,128)S(1)}, f32[8,20,1440]{2,1,0:T(8,128)}) fusion(f32[8,24,1440]{2,1,0:T(8,128)S(1)} %get-tuple-element.2, f32[8,22,1440]{2,1,0:T(8,128)S(1)} %get-tuple-element.23, f32[8,24,1440]{2,1,0:T(8,128)S(1)} %get-tuple-element.3, f32[8,20,1439]{2,1,0:T(8,128)S(1)} %get-tuple-element.37, ...), kind=kLoop, calls=%fused_computation.121 | loop fusion | flops 2534400 | bytes 11980800 | tf_op jit(solution)/shard_map/slice | solution.py:72
  47.3 2.7 %fusion.59 = (f32[8,18,1440]{2,1,0:T(8,128)}, f32[8,18,1440]{2,1,0:T(8,128)S(1)}, f32[8,18,1440]{2,1,0:T(8,128)}) fusion(f32[8,24,1440]{2,1,0:T(8,128)S(1)} %get-tuple-element.2, f32[8,20,1440]{2,1,0:T(8,128)S(1)} %get-tuple-element.18, f32[8,24,1440]{2,1,0:T(8,128)S(1)} %get-tuple-element.3, f32[8,18,1439]{2,1,0:T(8,128)S(1)} %get-tuple-element.33, ...), kind=kLoop, calls=%fused_computation.120 | loop fusion | flops 2280960 | bytes 10782720 | tf_op jit(solution)/shard_map/slice | solution.py:72
  50.5 1.1 fusion.42
  52.9 3.6 %fusion.2 = f32[32,1,16]{2,1,0:T(1,128)S(1)} fusion(f32[1,32,16,1440]{3,2,1,0:T(8,128)S(1)} %copy-done, f32[32,1440,1]{1,0,2:T(8,128)S(1)} %convolution_bitcast_fusion), kind=kOutput, calls=%fused_computation.3 | convolution fusion | flops 8847360 | bytes 3135488 | tf_op jit(solution)/shard_map/jon,jn->jo/dot_general | solution.py:136
  56.7 1.8 %fusion = f32[32,1,1440]{2,1,0:T(1,128)S(1)} fusion(f32[32,16,1]{1,2,0:T(1,128)S(1)} %copy.20, f32[1,32,16,1440]{3,2,1,0:T(8,128)S(1)} %copy-done), kind=kOutput, calls=%fused_computation.1 | convolution fusion | flops 8847360 | bytes 3135488 | tf_op jit(solution)/shard_map/jon,jo->jn/dot_general | solution.py:140
  59.7 1.3 multiply_subtract_fusion.4
  61.1 5.6 %collective-permute-start.3 = (f32[1,8,4,1440]{3,2,1,0:T(4,128)S(1)}, f32[1,8,4,1440]{3,2,1,0:T(4,128)S(1)}, u32[]{:S(2)}, u32[]{:S(2)}) collective-permute-start(f32[1,8,4,1440]{3,2,1,0:T(4,128)S(1)} %get-tuple-element.43), channel_id=1, source_target_pairs={{0,2},{2,4},{4,6},{6,8},{8,10},{10,12},{12,14},{14,16},{16,18},{18... | collective-permute-start | bytes 552968 | tf_op jit(solution)/shard_map/ppermute | solution.py:27
  66.7 1.4 collective-permute-start.4
  68.2 4.1 %collective-permute-start.5 = (f32[8,16,1440]{2,1,0:T(8,128)S(1)}, f32[8,16,1440]{2,1,0:T(8,128)}, u32[]{:S(2)}, u32[]{:S(2)}) collective-permute-start(f32[8,16,1440]{2,1,0:T(8,128)S(1)} %copy-done.14), channel_id=1, source_target_pairs={{0,32},{32,64},{64,96},{96,128},{128,160},{160,192},{192,224},{1,3... | collective-permute-start | bytes 2211848 | tf_op jit(solution)/shard_map/ppermute | solution.py:17
  72.3 3.7 %collective-permute-done.4 = f32[1,8,4,1440]{3,2,1,0:T(4,128)S(1)} collective-permute-done((f32[1,8,4,1440]{3,2,1,0:T(4,128)S(1)}, f32[1,8,4,1440]{3,2,1,0:T(4,128)S(1)}, u32[]{:S(2)}, u32[]{:S(2)}) %collective-permute-start.4) | collective-permute-done | bytes 184352 | tf_op jit(solution)/shard_map/ppermute | solution.py:28
  85.3 1.9 %fusion.37 = (f32[8,1,16,1440]{3,2,1,0:T(8,128)}, f32[8,16,1440]{2,1,0:T(8,128)}, f32[8,16,1440]{2,1,0:T(8,128)}) fusion(f32[8,20,1440]{2,1,0:T(8,128)S(1)} %fusion.14, f32[8,16,1440]{2,1,0:T(8,128)S(1)} %multiply_subtract_fusion.4, f32[8,22,1440]{2,1,0:T(8,128)S(1)} %fusion.16, f32[8,18,1440]{2,1,0:T(8,128)S(1)} %fusion.12, ...), kind=kLoop, calls=%fused_computation.78 | loop fusion | flops 921600 | bytes 6635520 | tf_op jit(solution)/shard_map/reshape | solution.py:35
  87.2 5.9 %all-to-all-start = ((f32[8,1,16,1440]{3,2,1,0:T(8,128)}), f32[8,1,16,1440]{3,2,1,0:T(8,128)}, u32[]{:S(2)}, u32[]{:S(2)}) async-start(f32[8,1,16,1440]{3,2,1,0:T(8,128)} %get-tuple-element.9), calls=%async_computation | async-start | bytes 1572864 | tf_op jit(solution)/shard_map/all_to_all | solution.py:41
  94.0 1.4 slice.515
  95.5 3.8 %fusion.40 = f32[1,8,16,1440]{3,2,1,0:T(8,128)} fusion(f32[8,18,1440]{2,1,0:T(8,128)S(1)} %fusion.12, f32[8,18,1440]{2,1,0:T(8,128)} %get-tuple-element.14, f32[8,18,1440]{2,1,0:T(8,128)} %get-tuple-element.12, f32[8,16,1439]{2,1,0:T(8,128)S(1)} %bitcast.83, f32[8,16,1]{2,1,0:T(8,128)S(1)} %slice.513, f32[8,16,1]{2,1,0:T(8,128)S(1)} %slice.516, ...), kind=kLoop, calls=%fused_computation.83 | loop fusion | flops 2211840 | bytes 8110112 | tf_op jit(solution)/shard_map/broadcast_in_dim | solution.py:151
  99.3 3.3 %all-to-all-done = f32[8,1,16,1440]{3,2,1,0:T(8,128)} async-done(((f32[8,1,16,1440]{3,2,1,0:T(8,128)}), f32[8,1,16,1440]{3,2,1,0:T(8,128)}, u32[]{:S(2)}, u32[]{:S(2)}) %all-to-all-start) | async-done | bytes 737312 | tf_op jit(solution)/shard_map/all_to_all | solution.py:41
  102.5 1.2 reduce_sum.18
  103.7 3.9 %fusion.33 = f32[16]{0:T(128)S(1)} fusion(f32[16,16,1440]{2,1,0:T(8,128)} %bitcast.78, f32[16,1440,1]{1,0,2:T(8,128)S(1)} %bitcast.85), kind=kOutput, calls=%fused_computation.75 | convolution fusion | flops 4423680 | bytes 1566784 | tf_op jit(solution)/shard_map/mlan,lan->m/dot_general | solution.py:153
  107.6 6.3 %psum.28 = f32[16]{0:T(128)S(1)} all-reduce(f32[16]{0:T(128)S(1)} %fusion.33), channel_id=1, replica_groups=mesh['tm_0'=2,'tm_1'=4,'lat_0'=8,'lat_1'=2,'ens'=2] {'tm_0'}, use_global_device_ids=true, to_apply=%region_1.2 | all-reduce | flops 16 | bytes 128 | tf_op jit(solution)/shard_map/psum | solution.py:47
  113.9 7.4 %psum.29 = f32[16]{0:T(128)S(1)} all-reduce(f32[16]{0:T(128)S(1)} %psum.28), channel_id=1, replica_groups=mesh['tm_0'=2,'tm_1'=4,'lat_0'=8,'lat_1'=2,'ens'=2] {'tm_1'}, use_global_device_ids=true, to_apply=%region_2.3 | all-reduce | flops 16 | bytes 128 | tf_op jit(solution)/shard_map/psum | solution.py:47
  121.4 18.9 %psum.30 = f32[16]{0:T(128)S(1)} all-reduce(f32[16]{0:T(128)S(1)} %psum.29), channel_id=1, replica_groups=mesh['tm_0'=2,'tm_1'=4,'lat_0'=8,'lat_1'=2,'ens'=2] {'lat_0'}, use_global_device_ids=true, to_apply=%region_3.4 | all-reduce | flops 16 | bytes 128 | tf_op jit(solution)/shard_map/psum | solution.py:47
  140.2 5.5 %psum.31 = f32[16]{0:T(128)S(1)} all-reduce(f32[16]{0:T(128)S(1)} %psum.30), channel_id=1, replica_groups=mesh['tm_0'=2,'tm_1'=4,'lat_0'=8,'lat_1'=2,'ens'=2] {'lat_1'}, use_global_device_ids=true, to_apply=%region_4.5 | all-reduce | flops 16 | bytes 128 | tf_op jit(solution)/shard_map/psum | solution.py:47
  145.8 3.1 %fusion.4 = f32[1,16,1440]{2,0,1:T(1,128)S(1)} fusion(f32[16,16,1440]{2,1,0:T(8,128)} %bitcast.79, f32[16]{0:T(128)S(1)} %psum.31), kind=kOutput, calls=%fused_computation.12 | convolution fusion | flops 4423680 | bytes 1566784 | tf_op jit(solution)/shard_map/m,mlan->lan/dot_general | solution.py:155
  148.9 12.4 %all_to_all.10 = f32[2,1,16,1440]{3,2,1,0:T(8,128)S(1)} all-to-all(f32[2,1,16,1440]{3,2,1,0:T(8,128)S(1)} %broadcast_in_dim.8), channel_id=1, replica_groups=mesh['tm_0'=2,'tm_1'=4,'lat_0'=8,'lat_1'=2,'ens'=2] {'ens'}, dimensions={0} | all-to-all | bytes 368640 | tf_op jit(solution)/shard_map/all_to_all | solution.py:53
  (97 shorter events, 17.8 us)
Async XLA Ops:
  0.6 52.2 %copy-start = (f32[1,32,16,1440]{3,2,1,0:T(8,128)S(1)}, f32[1,32,16,1440]{3,2,1,0:T(8,128)}, u32[]{:S(2)}) copy-start(f32[1,32,16,1440]{3,2,1,0:T(8,128)} %param.16) | copy-start | bytes 8847364
  0.6 1.5 copy-start.20
  3.4 1.4 copy-start.12
  6.0 30.4 %collective-permute-start = (f32[3,8,4,1440]{3,2,1,0:T(4,128)}, f32[3,8,4,1440]{3,2,1,0:T(4,128)}, u32[]{:S(2)}, u32[]{:S(2)}) collective-permute-start(f32[3,8,4,1440]{3,2,1,0:T(4,128)} %get-tuple-element.7), channel_id=1, source_target_pairs={{0,2},{2,4},{4,6},{6,8},{8,10},{10,12},{12,14},{14,16},{16,18},{18... | collective-permute-start | bytes 1658888 | tf_op jit(solution)/shard_map/ppermute | solution.py:27
  12.3 24.1 %collective-permute-start.1 = (f32[3,8,4,1440]{3,2,1,0:T(4,128)}, f32[3,8,4,1440]{3,2,1,0:T(4,128)}, u32[]{:S(2)}, u32[]{:S(2)}) collective-permute-start(f32[3,8,4,1440]{3,2,1,0:T(4,128)} %get-tuple-element.8), channel_id=1, source_target_pairs={{2,0},{4,2},{6,4},{8,6},{10,8},{12,10},{14,12},{16,14},{18,16},{20... | collective-permute-start | bytes 1658888 | tf_op jit(solution)/shard_map/ppermute | solution.py:28
  13.6 45.6 %collective-permute-start.2 = (f32[8,16,1440]{2,1,0:T(8,128)}, f32[8,16,1440]{2,1,0:T(8,128)}, u32[]{:S(2)}, u32[]{:S(2)}) collective-permute-start(f32[8,16,1440]{2,1,0:T(8,128)} %bitcast.14), channel_id=1, source_target_pairs={{32,0},{64,32},{96,64},{128,96},{160,128},{192,160},{224,192},{33,... | collective-permute-start | bytes 2211848 | tf_op jit(solution)/shard_map/ppermute | solution.py:17
  40.0 10.5 %copy-start.2 = (f32[8,24,1440]{2,1,0:T(8,128)}, f32[8,24,1440]{2,1,0:T(8,128)S(1)}, u32[]{:S(2)}) copy-start(f32[8,24,1440]{2,1,0:T(8,128)S(1)} %get-tuple-element.6) | copy-start | bytes 3317764
  40.0 10.5 %copy-start.4 = (f32[8,24,1440]{2,1,0:T(8,128)}, f32[8,24,1440]{2,1,0:T(8,128)S(1)}, u32[]{:S(2)}) copy-start(f32[8,24,1440]{2,1,0:T(8,128)S(1)} %get-tuple-element.4) | copy-start | bytes 3317764
  40.0 10.5 %copy-start.6 = (f32[8,24,1440]{2,1,0:T(8,128)}, f32[8,24,1440]{2,1,0:T(8,128)S(1)}, u32[]{:S(2)}) copy-start(f32[8,24,1440]{2,1,0:T(8,128)S(1)} %get-tuple-element.5) | copy-start | bytes 3317764
  40.0 10.5 %copy-start.8 = (f32[8,24,1440]{2,1,0:T(8,128)}, f32[8,24,1440]{2,1,0:T(8,128)S(1)}, u32[]{:S(2)}) copy-start(f32[8,24,1440]{2,1,0:T(8,128)S(1)} %get-tuple-element.2) | copy-start | bytes 3317764
  40.0 10.5 %copy-start.10 = (f32[8,24,1440]{2,1,0:T(8,128)}, f32[8,24,1440]{2,1,0:T(8,128)S(1)}, u32[]{:S(2)}) copy-start(f32[8,24,1440]{2,1,0:T(8,128)S(1)} %get-tuple-element.3) | copy-start | bytes 3317764
  50.5 2.0 %copy-start.24 = (s32[1,32]{1,0:T(1,128)S(1)}, s32[1,32]{1,0:T(1,128)}, u32[]{:S(2)}) copy-start(s32[1,32]{1,0:T(1,128)} %param.15) | copy-start | bytes 388
  52.9 3.7 %copy-start.22 = (f32[1,32,16]{1,2,0:T(8,128)S(1)}, f32[1,32,16]{1,2,0:T(8,128)}, u32[]{:S(2)}) copy-start(f32[1,32,16]{1,2,0:T(8,128)} %param.17) | copy-start | bytes 6148
  52.9 3.7 %copy-start.23 = (f32[1,32,16]{1,2,0:T(8,128)S(1)}, f32[1,32,16]{1,2,0:T(8,128)}, u32[]{:S(2)}) copy-start(f32[1,32,16]{1,2,0:T(8,128)} %param.18) | copy-start | bytes 6148
  52.9 3.7 %copy-start.26 = (s32[1,32]{1,0:T(1,128)S(1)}, s32[1,32]{1,0:T(1,128)}, u32[]{:S(2)}) copy-start(s32[1,32]{1,0:T(1,128)} %param.19) | copy-start | bytes 388
  56.7 2.5 %copy-start.25 = (f32[8]{0:T(128)S(1)}, f32[8]{0:T(128)}, u32[]{:S(2)}) copy-start(f32[8]{0:T(128)} %param.13) | copy-start | bytes 100
  58.5 1.1 copy-start.14
  61.1 11.2 %collective-permute-start.3 = (f32[1,8,4,1440]{3,2,1,0:T(4,128)S(1)}, f32[1,8,4,1440]{3,2,1,0:T(4,128)S(1)}, u32[]{:S(2)}, u32[]{:S(2)}) collective-permute-start(f32[1,8,4,1440]{3,2,1,0:T(4,128)S(1)} %get-tuple-element.43), channel_id=1, source_target_pairs={{0,2},{2,4},{4,6},{6,8},{8,10},{10,12},{12,14},{14,16},{16,18},{18... | collective-permute-start | bytes 552968 | tf_op jit(solution)/shard_map/ppermute | solution.py:27
  66.7 9.5 %copy-start.5 = (f32[8,24,1440]{2,1,0:T(8,128)S(1)}, f32[8,24,1440]{2,1,0:T(8,128)}, u32[]{:S(2)}) copy-start(f32[8,24,1440]{2,1,0:T(8,128)} %copy-done.4) | copy-start | bytes 3317764
  66.7 9.5 %copy-start.7 = (f32[8,24,1440]{2,1,0:T(8,128)S(1)}, f32[8,24,1440]{2,1,0:T(8,128)}, u32[]{:S(2)}) copy-start(f32[8,24,1440]{2,1,0:T(8,128)} %copy-done.6) | copy-start | bytes 3317764
  66.7 9.3 %collective-permute-start.4 = (f32[1,8,4,1440]{3,2,1,0:T(4,128)S(1)}, f32[1,8,4,1440]{3,2,1,0:T(4,128)S(1)}, u32[]{:S(2)}, u32[]{:S(2)}) collective-permute-start(f32[1,8,4,1440]{3,2,1,0:T(4,128)S(1)} %get-tuple-element.44), channel_id=1, source_target_pairs={{2,0},{4,2},{6,4},{8,6},{10,8},{12,10},{14,12},{16,14},{18,16},{20... | collective-permute-start | bytes 552968 | tf_op jit(solution)/shard_map/ppermute | solution.py:28
  68.2 27.3 %collective-permute-start.5 = (f32[8,16,1440]{2,1,0:T(8,128)S(1)}, f32[8,16,1440]{2,1,0:T(8,128)}, u32[]{:S(2)}, u32[]{:S(2)}) collective-permute-start(f32[8,16,1440]{2,1,0:T(8,128)S(1)} %copy-done.14), channel_id=1, source_target_pairs={{0,32},{32,64},{64,96},{96,128},{128,160},{160,192},{192,224},{1,3... | collective-permute-start | bytes 2211848 | tf_op jit(solution)/shard_map/ppermute | solution.py:17
  76.2 1.3 copy-start.11
  76.7 1.4 copy-start.3
  76.7 1.7 %copy-start.9 = (f32[8,24,1440]{2,1,0:T(8,128)S(1)}, f32[8,24,1440]{2,1,0:T(8,128)}, u32[]{:S(2)}) copy-start(f32[8,24,1440]{2,1,0:T(8,128)} %copy-done.8) | copy-start | bytes 3317764
  79.8 1.3 copy-start.15
  79.8 1.6 copy-start.16
  82.8 1.3 copy-start.17
  82.8 1.6 copy-start.18
  87.2 15.3 %all-to-all-start = ((f32[8,1,16,1440]{3,2,1,0:T(8,128)}), f32[8,1,16,1440]{3,2,1,0:T(8,128)}, u32[]{:S(2)}, u32[]{:S(2)}) async-start(f32[8,1,16,1440]{3,2,1,0:T(8,128)} %get-tuple-element.9), calls=%async_computation | async-start | bytes 1572864 | tf_op jit(solution)/shard_map/all_to_all | solution.py:41
  93.1 2.3 %copy-start.19 = (f32[8,16,1440]{2,1,0:T(8,128)S(1)}, f32[8,16,1440]{2,1,0:T(8,128)}, u32[]{:S(2)}) copy-start(f32[8,16,1440]{2,1,0:T(8,128)} %get-tuple-element.11) | copy-start | bytes 2211844
  140.2 21.7 %copy-start.1 = (f32[1,32,16,1440]{3,2,1,0:T(8,128)S(1)}, f32[1,32,16,1440]{3,2,1,0:T(8,128)}, u32[]{:S(2)}) copy-start(f32[1,32,16,1440]{3,2,1,0:T(8,128)} %param.16) | copy-start | bytes 8847364
  (2 other events, 2.0 us)
where the time goes:
time: 163 us; the launch traced here: 162 us
  blocking collectives  50.5 us (31%)
  waiting for transfers between devices  28.6 us (18%)
  starting transfers between devices  25.9 us (16%)
  other arithmetic  25.9 us (16%)
  local copies, waits for them, and re-layouts  16.4 us (10%)
  matrix products  13.4 us (8%)
    psum x4, blocking collectives, by_axis(): value = lax.psum(value, axis)  38.1 us
    ppermute x2, waiting for transfers between devices, padded(): before = lax.ppermute(last, axis, up)  21.5 us
    all_to_all x1, blocking collectives, from_everyone(): lax.all_to_all(jnp.broadcast_to(value[None], (peers, *value.shape)), axis...  12.4 us
    ppermute x2, starting transfers between devices, padded(): before = lax.ppermute(last, axis, up)  11.9 us
    unnamed x56, local copies, waits for them, and re-layouts  9.06 us
    slice x3, other arithmetic, trim_coefs(): return tuple((item[:, first:last] for item in coefs))  8.38 us
    all_to_all x1, starting transfers between devices, sent_and_summed(): lax.all_to_all(in_blocks(value, dim, peers), axis, 0, 0, tiled=True)  5.89 us
    ppermute x2, starting transfers between devices, shifted(): lax.ppermute(value, axis, [(source, source + steps) for source in range(l...  5.39 us
  transfers between devices with their start and end apart: 7, of which 3 were waited for; matrix products, arithmetic and copies ran while one was open for 22% of the time, Pallas kernels for 0%

commit v1 on v0

v1 whole, which is shorter than its diff:
```python
import jax
import jax.numpy as jnp
from jax import lax
from jax.experimental import pallas as pl
from jax.experimental.pallas import tpu as pltpu
from jax.sharding import Mesh
from jax.sharding import PartitionSpec as P

MEM = 32
STEPS = 4
LANES = 128
TM = ("tm_0", "tm_1")
LAT = ("lat_0", "lat_1")
ALL = ("tm_0", "tm_1", "lat_0", "lat_1", "ens")


def wrapped(value):
    lon = value.shape[-1]
    half = (-lon % LANES) // 2
    return jnp.concatenate([value, value[..., :half], value[..., lon - half :]], axis=-1)


def row_major(value):
    return wrapped(jnp.swapaxes(value, 0, 1))


def east(value):
    return pltpu.roll(value, value.shape[-1] - 1, 1)


def west(value):
    return pltpu.roll(value, 1, 1)


def forward_kernel(
    core_ref, rows_ref, prec_ref, inc_ref, lon_ref, lat_ref, halo_ref, next_ref, jac_ref, val_ref, oprec_ref,
    used_ref, end_ref, adj_ref, outer_ref, inner_ref, coef_ref, x0, x1, pk, wgt,
):
    core = core_ref[0]
    has_next = core_ref[1]
    blocks, slots, lons = jac_ref.shape
    own_at = 4 * (1 - core)
    x0[pl.ds(own_at, 12)] = inc_ref[...]
    x0[pl.ds(12 * core, 4)] = halo_ref[0:4]
    center, plon, mlon, plat, mlat = (coef_ref.at[i] for i in range(5))

    def fill(at, c, e):
        cc = c * c
        ee = e * e
        center[at] = 1.0 - cc - ee
        plon[at] = 0.5 * (cc - c)
        mlon[at] = 0.5 * (cc + c)
        plat[at] = 0.5 * (ee - e)
        mlat[at] = 0.5 * (ee + e)

    for r in range(12):
        fill(own_at + r, lon_ref[r], lat_ref[r])
    for r in range(3):
        fill(1 + 11 * core + r, halo_ref[4 + r], halo_ref[7 + r])
    ones = jnp.ones(x0.shape[1:], jnp.float32)

    @pl.when(core == 0)
    def _():
        plat[0] = ones

    @pl.when(core == 1)
    def _():
        mlat[15] = ones

    bufs = (x0, x1)
    for step in range(STEPS):
        src, dst = bufs[step % 2], bufs[(step + 1) % 2]
        for j in range(step + 1, 15 - step):
            f = src[j]
            dst[j] = (
                center[j] * f + plon[j] * east(f) + mlon[j] * west(f) + plat[j] * src[j + 1] + mlat[j] * src[j - 1]
            )
    field = bufs[STEPS % 2]
    prec = prec_ref[...] * has_next.astype(jnp.float32)
    for r in range(8):
        f = field[4 + r]
        end_ref[r] = f
        adj_ref[r] = prec * (f - next_ref[r])

    lane = lax.broadcasted_iota(jnp.int32, (slots, LANES), 1)
    for j in range(blocks):
        r = rows_ref[0, j]
        row = jnp.clip(r % 16 - 8 * core, 0, 7)
        pk[pl.ds(j, 1), :] = field[4 + row, pl.ds(r // 16, 1), :]
    ev = jnp.zeros((slots, LANES), jnp.float32)
    for j in range(blocks):
        total = jnp.sum(jac_ref[j] * pk[pl.ds(j, 1), 0:lons], axis=1, keepdims=True)
        ev = jnp.where(lane == j, total, ev)
    wgt[...] = oprec_ref[...] * (ev - val_ref[...]) * used_ref[...]
    for j in range(blocks):
        w = jnp.sum(jnp.where(lane == j, wgt[...], 0.0), axis=1, keepdims=True)
        force = jnp.sum(jac_ref[j] * w, axis=0, keepdims=True)
        pk[pl.ds(j, 1), 0:lons] = force
    lane32 = lax.broadcasted_iota(jnp.int32, (blocks, LANES), 1)
    tail = lons % LANES
    first = pk[:, 0:LANES]
    last = pk[:, lons - tail :]
    half = (LANES - tail) // 2
    pk[:, lons - tail :] = jnp.where(
        lane32 < tail, last, jnp.where(lane32 < tail + half, pltpu.roll(first, tail, 1), pltpu.roll(last, LANES - tail, 1))
    )
    for j in range(blocks):
        r = rows_ref[0, j]
        row = jnp.clip(r % 16 - 8 * core, 0, 7)
        lev = pl.ds(r // 16, 1)
        adj_ref[row, lev, :] = adj_ref[row, lev, :] + pk[pl.ds(j, 1), :]

    @pl.when(core == 0)
    def _():
        for r in range(4):
            outer_ref[r] = adj_ref[r] * mlat[7] if r == 3 else adj_ref[r]
            inner_ref[r] = adj_ref[4 + r]

    @pl.when(core == 1)
    def _():
        for r in range(4):
            outer_ref[r] = adj_ref[4 + r] * plat[8] if r == 0 else adj_ref[4 + r]
            inner_ref[r] = adj_ref[r]


def adjoint_kernel(core_ref, adj_ref, outer_ref, inner_ref, coef_ref, forcing_ref, start_ref, g0, g1):
    core = core_ref[0]
    lons = forcing_ref.shape[-1]
    center, plon, mlon, plat, mlat = (coef_ref.at[i] for i in range(5))
    g0[4:12] = adj_ref[...]
    g0[pl.ds(12 * core, 4)] = outer_ref[...]
    g0[pl.ds(12 * (1 - core), 4)] = inner_ref[...]
    bufs = (g0, g1)
    acc = [None] * 8
    for step in range(STEPS):
        src, dst = bufs[step % 2], bufs[(step + 1) % 2]
        for j in range(step + 1, 15 - step):
            g = src[j]
            out = (
                center[j] * g
                + west(plon[j] * g)
                + east(mlon[j] * g)
                + plat[j - 1] * src[j - 1]
                + mlat[j + 1] * src[j + 1]
            )
            if step + 1 < STEPS:
                dst[j] = out
            else:
                start_ref[j - 4] = out
            if 4 <= j < 12 and step + 1 < STEPS:
                acc[j - 4] = (src[j] if step == 0 else acc[j - 4]) + out
    for r in range(8):
        forcing_ref[:, r, :] = acc[r][:, 0:lons]


def product_kernel(core_ref, pieces_ref, own_ref, other_ref, out_ref):
    core = core_ref[0]
    forcing = jnp.sum(pieces_ref[...], axis=0)
    first = pl.multiple_of(8 * core, 8)
    lane = lax.broadcasted_iota(jnp.int32, (8, LANES), 1)
    members = own_ref.shape[0]
    vec = jnp.zeros((8, LANES), jnp.float32)
    for m in range(2 * members):
        ref, at = (own_ref, m) if m < members else (other_ref, m - members)
        col = jnp.sum(ref[at, 0, pl.ds(first, 8), :] * forcing, axis=1, keepdims=True)
        vec = jnp.where(lane == m, col, vec)
    vec = jnp.sum(vec, axis=0, keepdims=True)
    swapped = jnp.where(
        lane[0:1] < members, pltpu.roll(vec, LANES - members, 1), pltpu.roll(vec, members, 1)
    )
    vec = jnp.where(core == 0, vec, swapped)
    vec = jnp.where(lane[0:1] < 2 * members, vec, 0.0)
    out_ref[...] = jnp.broadcast_to(vec[None], out_ref.shape)


def step_kernel(core_ref, sums_ref, own_ref, other_ref, out_ref):
    core = core_ref[0]
    members = own_ref.shape[0]
    vec = jnp.sum(sums_ref[...], axis=0)
    swapped = jnp.where(
        lax.broadcasted_iota(jnp.int32, (1, LANES), 1) < members,
        pltpu.roll(vec, LANES - members, 1),
        pltpu.roll(vec, members, 1),
    )
    vec = jnp.where(core == 0, vec, swapped) * (-1.0 / (MEM - 1.0))
    wide = jnp.broadcast_to(vec, (8, LANES))
    lane = lax.broadcasted_iota(jnp.int32, (8, LANES), 1)
    coefs = [jnp.sum(jnp.where(lane == m, wide, 0.0), axis=1, keepdims=True) for m in range(2 * members)]
    for half in range(2):
        rows = pl.ds(8 * half, 8)
        total = coefs[0] * own_ref[0, 0, rows, :]
        for m in range(1, 2 * members):
            ref, at = (own_ref, m) if m < members else (other_ref, m - members)
            total = total + coefs[m] * ref[at, 0, rows, :]
        out_ref[0, rows, :] = total


VMEM = pl.BlockSpec(memory_space=pltpu.VMEM)
SMEM = pl.BlockSpec(memory_space=pltpu.SMEM)


def call(kernel, ins, outs, scratch=(), limit=40):
    return pl.pallas_call(
        kernel,
        out_shape=[jax.ShapeDtypeStruct(s, jnp.float32) for s in outs],
        in_specs=ins,
        out_specs=[VMEM] * len(outs),
        scratch_shapes=[pltpu.VMEM(s, jnp.float32) for s in scratch],
        compiler_params=pltpu.CompilerParams(vmem_limit_bytes=limit * 2**20),
        name=kernel.__name__,
    )


def on_device(
    increment,
    wind_lon,
    wind_lat,
    model_precision,
    perturbations,
    obs_rows,
    obs_jacobian,
    obs_values,
    obs_precision,
    obs_counts,
):
    core = lax.axis_index("ens")
    count_t = lax.axis_size(TM)
    count_l = lax.axis_size(LAT)
    has_next = (lax.axis_index(TM) < count_t - 1).astype(jnp.int32)
    flags = jnp.stack([core, has_next]).astype(jnp.int32)
    levels, band_rows, lons = increment.shape[1:]
    wide = lons + (-lons % LANES)

    def rows_of(value, start, size):
        return lax.dynamic_slice_in_dim(value[0], start, size, axis=1)

    trade = []
    for i in range(count_l - 1):
        trade += [(2 * i + 1, 2 * i + 2), (2 * i + 2, 2 * i + 1)]
    partner = [(0, 1), (1, 0)]
    outgoing = row_major(
        jnp.concatenate(
            [rows_of(increment, 12 * core, 4), rows_of(wind_lon, 13 * core, 3), rows_of(wind_lat, 13 * core, 3)], axis=1
        )
    )
    halo = lax.ppermute(outgoing, LAT + ("ens",), trade)
    own_rows = row_major(rows_of(increment, 8 * core, 8))
    next_rows = lax.ppermute(own_rows, TM, [(i + 1, i) for i in range(count_t - 1)])
    other_pert = lax.ppermute(perturbations, "ens", partner)

    inc12 = row_major(rows_of(increment, 4 * core, 12))
    lon12 = row_major(rows_of(wind_lon, 4 * core, 12))
    lat12 = row_major(rows_of(wind_lat, 4 * core, 12))
    prec = jnp.broadcast_to(model_precision[:, None], (levels, wide))
    blocks, slots = obs_values.shape[1:]

    def by_slot(value):
        return jnp.pad(value.T, ((0, 0), (0, LANES - blocks)))

    slot = jnp.arange(slots, dtype=jnp.int32)
    mine = (obs_rows[0] % band_rows) // 8 == core
    used = ((slot[None, :] < obs_counts[0][:, None]) & mine[:, None]).astype(jnp.float32)

    own_shape = (8, levels, wide)
    end, adj, outer, inner, coefs = call(
        forward_kernel,
        [SMEM, SMEM] + [VMEM] * 10,
        [own_shape, own_shape, (4, levels, wide), (4, levels, wide), (5, 16, levels, wide)],
        [(16, levels, wide), (16, levels, wide), (blocks, wide), (slots, LANES)],
    )(
        flags, obs_rows, prec, inc12, lon12, lat12, halo, next_rows, obs_jacobian[0],
        by_slot(obs_values[0]), by_slot(obs_precision[0]), by_slot(used),
    )
    outer = lax.ppermute(outer, LAT + ("ens",), trade)
    inner = lax.ppermute(inner, "ens", partner)
    prior = lax.ppermute(end, TM, [(i, i + 1) for i in range(count_t - 1)])

    forcing, start = call(
        adjoint_kernel,
        [SMEM] + [VMEM] * 4,
        [(levels, 8, lons), own_shape],
        [(16, levels, wide), (16, levels, wide)],
    )(flags, adj, outer, inner, coefs)
    pieces = lax.all_to_all(forcing, TM, 0, 0, tiled=True)

    own_grad = start[..., :lons] + model_precision[:, None] * (own_rows[..., :lons] - prior[..., :lons])
    other_grad = lax.ppermute(own_grad, "ens", partner)
    grad = jnp.where(
        core == 0,
        jnp.concatenate([own_grad, other_grad], axis=0),
        jnp.concatenate([other_grad, own_grad], axis=0),
    )
    grad_state = jnp.swapaxes(grad, 0, 1)[None]

    peers = lax.axis_size(ALL)
    (products,) = call(product_kernel, [SMEM] + [VMEM] * 3, [(peers, 1, LANES)])(
        flags, pieces, perturbations, other_pert
    )
    sums = lax.all_to_all(products, ALL, 0, 0, tiled=True)
    (forcing_step,) = call(step_kernel, [SMEM] + [VMEM] * 3, [(1, band_rows, lons)])(
        flags, sums, perturbations, other_pert
    )
    return (grad_state, forcing_step)


def solution(mesh):
    torus = Mesh(
        mesh.devices.reshape(2, 4, 8, 2, mesh.shape["ens"]),
        ("tm_0", "tm_1", "lat_0", "lat_1", "ens"),
    )
    in_specs = (
        P(TM, None, LAT, None),
        P(TM, None, LAT, None),
        P(TM, None, LAT, None),
        P(),
        P("ens", TM, LAT, None),
        P(TM, LAT),
        P(TM, LAT, None, None),
        P(TM, LAT, None),
        P(TM, LAT, None),
        P(TM, LAT),
    )
    out_specs = (P(TM, None, LAT, None), P(TM, LAT, None))
    return jax.shard_map(
        on_device, mesh=torus, in_specs=in_specs, out_specs=out_specs, check_vma=False
    )
```

time: 163 us -> 102 us (0.63)
  blocking collectives: 50.5 us -> 18.8 us
  other arithmetic: 25.9 us -> 1.74 us
  matrix products: 13.4 us -> 0 us
  waiting for transfers between devices: 28.6 us -> 16 us
  Pallas kernels: 0 us -> 12.5 us
  starting transfers between devices: 25.9 us -> 31.5 us
  local copies, waits for them, and re-layouts: 16.4 us -> 20 us
    psum x4 -> x0, blocking collectives: 38.1 us -> none  [by_axis(): value = lax.psum(value, axis)]
    ppermute x6 -> x7, waiting for transfers between devices: 25.3 us -> 4.61 us  [the longest x1 4.6 us: on_device(): outer = lax.ppermute(outer, LAT + ('ens',), trade)]
    dot_general x6 -> x0, matrix products: 13.4 us -> none  [the longest x1 3.9 us: on_device(): jnp.einsum('mlan,lan->m', perturbations, reduced, precision=highest)]
    pallas_call x0 -> x4, Pallas kernels: none -> 12.5 us  [the longest x1 4.81 us: on_device(): call(forward_kernel, [SMEM, SMEM] + [VMEM] * 10, [own_shape, own_shape, (...]
    all_to_all x1, starting transfers between devices: 5.89 us -> 15.4 us  [on_device(): sums = lax.all_to_all(products, ALL, 0, 0, tiled=True)]
    slice x3 -> x0, other arithmetic: 8.38 us -> none  [trim_coefs(): return tuple((item[:, first:last] for item in coefs))]
    all_to_all x1, waiting for transfers between devices: 3.28 us -> 11.4 us  [on_device(): sums = lax.all_to_all(products, ALL, 0, 0, tiled=True)]
    all_to_all x1, blocking collectives: 12.4 us -> 18.8 us  [on_device(): pieces = lax.all_to_all(forcing, TM, 0, 0, tiled=True)]
  transfers between devices with their start and end apart: 7 -> 8, of which waited for: 3 -> 2; matrix products, arithmetic and copies ran while one was open for 22% -> 14% of each run, Pallas kernels for 0% -> 10%
where the time goes in v1:
time: 102 us; the launch traced here: 101 us
  starting transfers between devices  31.5 us (31%)
  local copies, waits for them, and re-layouts  20 us (20%)
  blocking collectives  18.8 us (18%)
  waiting for transfers between devices  16 us (16%)
  Pallas kernels  12.5 us (12%)
  other arithmetic  1.74 us (2%)
    all_to_all x1, blocking collectives, on_device(): pieces = lax.all_to_all(forcing, TM, 0, 0, tiled=True)  18.8 us
    all_to_all x1, starting transfers between devices, on_device(): sums = lax.all_to_all(products, ALL, 0, 0, tiled=True)  15.4 us
    all_to_all x1, waiting for transfers between devices, on_device(): sums = lax.all_to_all(products, ALL, 0, 0, tiled=True)  11.4 us
    unnamed x31, local copies, waits for them, and re-layouts  6.54 us
    ppermute x1, starting transfers between devices, on_device(): halo = lax.ppermute(outgoing, LAT + ('ens',), trade)  6.27 us
    concatenate x5, local copies, waits for them, and re-layouts, wrapped(): jnp.concatenate([value, value[..., :half], value[..., lon - half:]], axis...  5.9 us
    pallas_call x1, Pallas kernels, on_device(): call(forward_kernel, [SMEM, SMEM] + [VMEM] * 10, [own_shape, own_shape, (...  4.81 us
    ppermute x1, waiting for transfers between devices, on_device(): outer = lax.ppermute(outer, LAT + ('ens',), trade)  4.6 us
  transfers between devices with their start and end apart: 8, of which 2 were waited for; matrix products, arithmetic and copies ran while one was open for 14% of the time, Pallas kernels for 10%

profile of v1, /device:TPU:1, one launch (start us, length us, event | category | flops | bytes accessed | tf_op | source)
XLA Modules:
  0.0 101.5 jit_solution(1098576474715450646)
XLA Ops:
  0.6 1.3 %constant_dynamic-slice_fusion.1 = (f32[1,8,3,1440]{3,2,1,0:T(4,128)S(1)}, f32[1,8,3,1440]{3,2,1,0:T(4,128)S(1)}) fusion(f32[1,8,16,1440]{3,2,1,0:T(8,128)} %param.12, s32[]{:T(128)S(6)} %select_n.46, f32[1,8,16,1440]{3,2,1,0:T(8,128)} %param.11), kind=kLoop, calls=%fused_computation.21 | loop fusion | bytes 552964 | tf_op jit(solution)/shard_map/dynamic_slice | solution.py:235
  2.3 0.9 concatenate.28
  3.2 6.3 %collective-permute-start = (f32[10,8,1536]{2,1,0:T(8,128)}, f32[10,8,1536]{2,1,0:T(8,128)}, u32[]{:S(2)}, u32[]{:S(2)}) collective-permute-start(f32[10,8,1536]{2,1,0:T(8,128)} %concatenate.28), channel_id=1, source_target_pairs={{1,2},{2,1},{3,4},{4,3},{5,6},{6,5},{7,8},{8,7},{9,10},{10,9},{11,... | collective-permute-start | bytes 1474568 | tf_op jit(solution)/shard_map/ppermute | solution.py:246
  9.5 0.7 copy-done.8
  10.6 0.9 concatenate.29
  11.4 1.3 %collective-permute-start.1 = (f32[8,8,1536]{2,1,0:T(8,128)}, f32[8,8,1536]{2,1,0:T(8,128)}, u32[]{:S(2)}, u32[]{:S(2)}) collective-permute-start(f32[8,8,1536]{2,1,0:T(8,128)} %concatenate.29), channel_id=1, source_target_pairs={{32,0},{64,32},{96,64},{128,96},{160,128},{192,160},{224,192},{33,... | collective-permute-start | bytes 1179656 | tf_op jit(solution)/shard_map/ppermute | solution.py:248
  12.8 1.6 %constant_dynamic-slice_fusion.4 = (f32[1,8,12,1440]{3,2,1,0:T(8,128)S(1)}, f32[1,8,12,1440]{3,2,1,0:T(8,128)S(1)}) fusion(f32[1,8,16,1440]{3,2,1,0:T(8,128)} %param.12, s32[]{:T(128)S(6)} %select_n.44, f32[1,8,16,1440]{3,2,1,0:T(8,128)} %param.11), kind=kLoop, calls=%fused_computation.24 | loop fusion | bytes 2211844 | tf_op jit(solution)/shard_map/dynamic_slice | solution.py:235
  14.5 0.3 copy.29
  14.9 0.7 fusion.6
  15.9 0.8 fusion.7
  17.1 0.8 copy-done.11
  17.9 0.7 fusion.8
  18.6 0.6 fusion.5
  19.3 1.0 concatenate.26.lat_ref
  20.2 1.2 %concatenate.25.lon_ref = f32[12,8,1536]{2,1,0:T(8,128)S(1)} concatenate(f32[12,8,1440]{2,1,0:T(8,128)} %bitcast.57, f32[12,8,48]{2,1,0:T(8,128)} %get-tuple-element.21, f32[12,8,48]{2,1,0:T(8,128)} %get-tuple-element.20), dimensions={2} | concatenate | bytes 1179648 | tf_op jit(solution)/shard_map/concatenate | solution.py:20
  21.4 2.0 %concatenate.24.inc_ref = f32[12,8,1536]{2,1,0:T(8,128)} concatenate(f32[12,8,1440]{2,1,0:T(8,128)} %bitcast.59, f32[12,8,48]{2,1,0:T(8,128)} %get-tuple-element.23, f32[12,8,48]{2,1,0:T(8,128)} %get-tuple-element.22), dimensions={2} | concatenate | bytes 1179648 | tf_op jit(solution)/shard_map/concatenate | solution.py:20
  23.4 0.7 fusion.3
  24.2 0.7 broadcast_in_dim.4.prec_ref
  24.9 1.9 %copy-done.2 = f32[1,32,16,1440]{3,2,1,0:T(8,128)S(1)} copy-done((f32[1,32,16,1440]{3,2,1,0:T(8,128)S(1)}, f32[1,32,16,1440]{3,2,1,0:T(8,128)}, u32[]{:S(2)}) %copy-start.2) | copy-done | bytes 2949144
  26.8 1.1 %copy-done.3 = f32[12,8,1536]{2,1,0:T(8,128)S(1)} copy-done((f32[12,8,1536]{2,1,0:T(8,128)S(1)}, f32[12,8,1536]{2,1,0:T(8,128)}, u32[]{:S(2)}) %copy-start.3) | copy-done | bytes 589848
  27.9 0.7 copy-done.7
  28.6 4.8 %forward_kernel.1 = (f32[8,8,1536]{2,1,0:T(8,128)S(1)}, f32[8,8,1536]{2,1,0:T(8,128)S(1)}, f32[4,8,1536]{2,1,0:T(8,128)S(1)}, f32[4,8,1536]{2,1,0:T(8,128)S(1)}, f32[5,16,8,1536]{3,2,1,0:T(8,128)S(1)}) custom-call(s32[2]{0:T(128)S(1)} %pad_add_fusion.core_ref, s32[1,32]{1,0:T(1,128)S(1)} %copy-done.7, f32[8,1536]{1,0:T(8,128)S(1)} %broadcast_in_dim.4.prec_ref, ...), custom_call_target="tpu_custom_call" | custom-call | tf_op jit(solution)/shard_map/forward_kernel/pallas_call | solution.py:265
  33.4 4.1 %collective-permute-start.4 = (f32[8,8,1536]{2,1,0:T(8,128)S(1)}, f32[8,8,1536]{2,1,0:T(8,128)S(1)}, u32[]{:S(2)}, u32[]{:S(2)}) collective-permute-start(f32[8,8,1536]{2,1,0:T(8,128)S(1)} %get-tuple-element.14), channel_id=1, source_target_pairs={{0,32},{32,64},{64,96},{96,128},{128,160},{160,192},{192,224},{1,3... | collective-permute-start | bytes 1179656 | tf_op jit(solution)/shard_map/ppermute | solution.py:276
  37.5 4.2 %collective-permute-start.2 = (f32[4,8,1536]{2,1,0:T(8,128)S(1)}, f32[4,8,1536]{2,1,0:T(8,128)S(1)}, u32[]{:S(2)}, u32[]{:S(2)}) collective-permute-start(f32[4,8,1536]{2,1,0:T(8,128)S(1)} %get-tuple-element.10), channel_id=1, source_target_pairs={{1,2},{2,1},{3,4},{4,3},{5,6},{6,5},{7,8},{8,7},{9,10},{10,9},{11,... | collective-permute-start | bytes 589832 | tf_op jit(solution)/shard_map/ppermute | solution.py:274
  41.8 4.6 %collective-permute-done.2.outer_ref = f32[4,8,1536]{2,1,0:T(8,128)S(1)} collective-permute-done((f32[4,8,1536]{2,1,0:T(8,128)S(1)}, f32[4,8,1536]{2,1,0:T(8,128)S(1)}, u32[]{:S(2)}, u32[]{:S(2)}) %collective-permute-start.2) | collective-permute-done | bytes 196640 | tf_op jit(solution)/shard_map/ppermute | solution.py:274
  46.4 2.5 %adjoint_kernel.1 = (f32[8,8,1440]{2,1,0:T(8,128)S(1)}, f32[8,8,1536]{2,1,0:T(8,128)S(1)}) custom-call(s32[2]{0:T(128)S(1)} %pad_add_fusion.core_ref, f32[8,8,1536]{2,1,0:T(8,128)S(1)} %get-tuple-element.9.adj_ref, f32[4,8,1536]{2,1,0:T(8,128)S(1)} %collective-permute-done.2.outer_ref, f32[4,8,1536]{2,1,0:T(8,128)S(1)} %collective-permute-done.3.inner_ref, ...), custom_call_target="tpu_custom_call" | custom-call | tf_op jit(solution)/shard_map/adjoint_kernel/pallas_call | solution.py:278
  49.4 18.8 %all_to_all.10.pieces_ref = f32[8,8,1440]{2,1,0:T(8,128)S(1)} all-to-all(f32[8,8,1440]{2,1,0:T(8,128)S(1)} %get-tuple-element.15), channel_id=1, replica_groups=mesh['tm_0'=2,'tm_1'=4,'lat_0'=8,'lat_1'=2,'ens'=2] {'tm_0','tm_1'}, dimensions={0} | all-to-all | bytes 737280 | tf_op jit(solution)/shard_map/all_to_all | solution.py:284
  68.2 2.4 %product_kernel.1 = f32[256,1,128]{2,1,0:T(1,128)} custom-call(s32[2]{0:T(128)S(1)} %pad_add_fusion.core_ref, f32[8,8,1440]{2,1,0:T(8,128)S(1)} %all_to_all.10.pieces_ref, f32[16,1,16,1440]{3,2,1,0:T(8,128)S(1)} %copy-done.1, f32[16,1,16,1440]{3,2,1,0:T(8,128)} %collective-permute-done.6.other_ref), custom_call_target="tpu_custom_call" | custom-call | tf_op jit(solution)/shard_map/product_kernel/pallas_call | solution.py:296
  70.6 15.4 %all-to-all-start.1 = ((f32[256,1,128]{2,1,0:T(1,128)}), f32[256,1,128]{2,1,0:T(1,128)S(1)}, u32[]{:S(2)}, u32[]{:S(2)}) async-start(f32[256,1,128]{2,1,0:T(1,128)} %product_kernel.1), calls=%async_computation.1 | async-start | bytes 262144 | tf_op jit(solution)/shard_map/all_to_all | solution.py:299
  86.1 1.3 %copy.19 = f32[1,8,16,1440]{3,2,1,0:T(8,128)} copy(f32[1,8,16,1440]{3,1,2,0:T(8,128)S(1)} %fusion) | data formatting | bytes 1474560
  87.4 11.4 %all-to-all-done.1.sums_ref = f32[256,1,128]{2,1,0:T(1,128)S(1)} async-done(((f32[256,1,128]{2,1,0:T(1,128)}), f32[256,1,128]{2,1,0:T(1,128)S(1)}, u32[]{:S(2)}, u32[]{:S(2)}) %all-to-all-start.1) | async-done | bytes 131104 | tf_op jit(solution)/shard_map/all_to_all | solution.py:299
  98.8 2.7 %step_kernel.1 = f32[1,16,1440]{2,1,0:T(8,128)} custom-call(s32[2]{0:T(128)S(1)} %copy-done.5, f32[256,1,128]{2,1,0:T(1,128)S(1)} %all-to-all-done.1.sums_ref, f32[16,1,16,1440]{3,2,1,0:T(8,128)S(1)} %copy-done.1, f32[16,1,16,1440]{3,2,1,0:T(8,128)} %collective-permute-done.6.other_ref), custom_call_target="tpu_custom_call" | custom-call | tf_op jit(solution)/shard_map/step_kernel/pallas_call | solution.py:300
  (52 shorter events, 2.2 us)
Async XLA Ops:
  0.6 1.4 %copy-start = (f32[1,8,16,1440]{3,2,1,0:T(8,128)S(1)}, f32[1,8,16,1440]{3,2,1,0:T(8,128)}, u32[]{:S(2)}) copy-start(f32[1,8,16,1440]{3,2,1,0:T(8,128)} %param.10) | copy-start | bytes 2211844
  1.9 10.8 %copy-start.1 = (f32[16,1,16,1440]{3,2,1,0:T(8,128)S(1)}, f32[16,1,16,1440]{3,2,1,0:T(8,128)}, u32[]{:S(2)}) copy-start(f32[16,1,16,1440]{3,2,1,0:T(8,128)} %own_ref.3) | copy-start | bytes 4423684
  3.2 21.0 %collective-permute-start = (f32[10,8,1536]{2,1,0:T(8,128)}, f32[10,8,1536]{2,1,0:T(8,128)}, u32[]{:S(2)}, u32[]{:S(2)}) collective-permute-start(f32[10,8,1536]{2,1,0:T(8,128)} %concatenate.28), channel_id=1, source_target_pairs={{1,2},{2,1},{3,4},{4,3},{5,6},{6,5},{7,8},{8,7},{9,10},{10,9},{11,... | collective-permute-start | bytes 1474568 | tf_op jit(solution)/shard_map/ppermute | solution.py:246
  9.5 0.7 copy-start.8
  11.4 12.8 %collective-permute-start.1 = (f32[8,8,1536]{2,1,0:T(8,128)}, f32[8,8,1536]{2,1,0:T(8,128)}, u32[]{:S(2)}, u32[]{:S(2)}) collective-permute-start(f32[8,8,1536]{2,1,0:T(8,128)} %concatenate.29), channel_id=1, source_target_pairs={{32,0},{64,32},{96,64},{128,96},{160,128},{192,160},{224,192},{33,... | collective-permute-start | bytes 1179656 | tf_op jit(solution)/shard_map/ppermute | solution.py:248
  12.7 55.4 %collective-permute-start.6 = (f32[16,1,16,1440]{3,2,1,0:T(8,128)S(1)}, f32[16,1,16,1440]{3,2,1,0:T(8,128)}, u32[]{:S(2)}, u32[]{:S(2)}) collective-permute-start(f32[16,1,16,1440]{3,2,1,0:T(8,128)S(1)} %copy-done.1), channel_id=1, source_target_pairs={{0,1},{1,0},{2,3},{3,2},{4,5},{5,4},{6,7},{7,6},{8,9},{9,8},{10,11... | collective-permute-start | bytes 4423688 | tf_op jit(solution)/shard_map/ppermute | solution.py:249
  14.4 4.2 %copy-start.6 = (s32[1,32]{1,0:T(1,128)S(1)}, s32[1,32]{1,0:T(1,128)}, u32[]{:S(2)}) copy-start(s32[1,32]{1,0:T(1,128)} %rows_ref.1) | copy-start | bytes 388
  14.4 4.8 %copy-start.12 = (f32[1,32,16]{1,2,0:T(8,128)S(1)}, f32[1,32,16]{1,2,0:T(8,128)}, u32[]{:S(2)}) copy-start(f32[1,32,16]{1,2,0:T(8,128)} %param.17) | copy-start | bytes 6148
  14.4 4.8 %copy-start.13 = (f32[1,32,16]{1,2,0:T(8,128)S(1)}, f32[1,32,16]{1,2,0:T(8,128)}, u32[]{:S(2)}) copy-start(f32[1,32,16]{1,2,0:T(8,128)} %param.18) | copy-start | bytes 6148
  15.9 1.2 %copy-start.10 = (f32[1,8,12,1440]{3,1,2,0:T(8,128)}, f32[1,8,12,1440]{3,1,2,0:T(8,128)S(1)}, u32[]{:S(2)}) copy-start(f32[1,8,12,1440]{3,1,2,0:T(8,128)S(1)} %copy.30) | copy-start | bytes 1658884
  17.1 0.8 copy-start.11
  24.2 44.0 %copy-start.4 = (s32[2]{0:T(128)}, s32[2]{0:T(128)S(1)}, u32[]{:S(2)}) copy-start(s32[2]{0:T(128)S(1)} %pad_add_fusion.core_ref) | copy-start | bytes 28
  24.9 1.9 %copy-start.2 = (f32[1,32,16,1440]{3,2,1,0:T(8,128)S(1)}, f32[1,32,16,1440]{3,2,1,0:T(8,128)}, u32[]{:S(2)}) copy-start(f32[1,32,16,1440]{3,2,1,0:T(8,128)} %param.16) | copy-start | bytes 8847364
  26.8 1.1 %copy-start.3 = (f32[12,8,1536]{2,1,0:T(8,128)S(1)}, f32[12,8,1536]{2,1,0:T(8,128)}, u32[]{:S(2)}) copy-start(f32[12,8,1536]{2,1,0:T(8,128)} %concatenate.24.inc_ref) | copy-start | bytes 1769476
  27.9 0.7 copy-start.7
  33.4 15.6 %copy-start.9 = (f32[1,8,8,1440]{3,2,1,0:T(8,128)S(1)}, f32[1,8,8,1440]{3,2,1,0:T(8,128)}, u32[]{:S(2)}) copy-start(f32[1,8,8,1440]{3,2,1,0:T(8,128)} %copy-done.8) | copy-start | bytes 1105924
  33.4 15.6 %copy-start.14 = (f32[8]{0:T(128)S(1)}, f32[8]{0:T(128)}, u32[]{:S(2)}) copy-start(f32[8]{0:T(128)} %param.13) | copy-start | bytes 100
  33.4 15.6 %collective-permute-start.4 = (f32[8,8,1536]{2,1,0:T(8,128)S(1)}, f32[8,8,1536]{2,1,0:T(8,128)S(1)}, u32[]{:S(2)}, u32[]{:S(2)}) collective-permute-start(f32[8,8,1536]{2,1,0:T(8,128)S(1)} %get-tuple-element.14), channel_id=1, source_target_pairs={{0,32},{32,64},{64,96},{96,128},{128,160},{160,192},{192,224},{1,3... | collective-permute-start | bytes 1179656 | tf_op jit(solution)/shard_map/ppermute | solution.py:276
  37.5 8.9 %collective-permute-start.2 = (f32[4,8,1536]{2,1,0:T(8,128)S(1)}, f32[4,8,1536]{2,1,0:T(8,128)S(1)}, u32[]{:S(2)}, u32[]{:S(2)}) collective-permute-start(f32[4,8,1536]{2,1,0:T(8,128)S(1)} %get-tuple-element.10), channel_id=1, source_target_pairs={{1,2},{2,1},{3,4},{4,3},{5,6},{6,5},{7,8},{8,7},{9,10},{10,9},{11,... | collective-permute-start | bytes 589832 | tf_op jit(solution)/shard_map/ppermute | solution.py:274
  41.7 4.7 %collective-permute-start.3 = (f32[4,8,1536]{2,1,0:T(8,128)S(1)}, f32[4,8,1536]{2,1,0:T(8,128)S(1)}, u32[]{:S(2)}, u32[]{:S(2)}) collective-permute-start(f32[4,8,1536]{2,1,0:T(8,128)S(1)} %get-tuple-element.11), channel_id=1, source_target_pairs={{0,1},{1,0},{2,3},{3,2},{4,5},{5,4},{6,7},{7,6},{8,9},{9,8},{10,11... | collective-permute-start | bytes 589832 | tf_op jit(solution)/shard_map/ppermute | solution.py:275
  49.3 36.7 %collective-permute-start.5 = (f32[8,8,1440]{2,1,0:T(8,128)S(1)}, f32[8,8,1440]{2,1,0:T(8,128)S(1)}, u32[]{:S(2)}, u32[]{:S(2)}) collective-permute-start(f32[8,8,1440]{2,1,0:T(8,128)S(1)} %fusion.2), channel_id=1, source_target_pairs={{0,1},{1,0},{2,3},{3,2},{4,5},{5,4},{6,7},{7,6},{8,9},{9,8},{10,11... | collective-permute-start | bytes 1105928 | tf_op jit(solution)/shard_map/ppermute | solution.py:287
  70.6 28.2 %copy-start.5 = (s32[2]{0:T(128)S(1)}, s32[2]{0:T(128)}, u32[]{:S(2)}) copy-start(s32[2]{0:T(128)} %copy-done.4) | copy-start | bytes 28
  70.6 28.2 %all-to-all-start.1 = ((f32[256,1,128]{2,1,0:T(1,128)}), f32[256,1,128]{2,1,0:T(1,128)S(1)}, u32[]{:S(2)}, u32[]{:S(2)}) async-start(f32[256,1,128]{2,1,0:T(1,128)} %product_kernel.1), calls=%async_computation.1 | async-start | bytes 262144 | tf_op jit(solution)/shard_map/all_to_all | solution.py:299

commit v2 on v1

v2 whole, which is shorter than its diff:
```python
import jax
import jax.numpy as jnp
from jax import lax
from jax.experimental import pallas as pl
from jax.experimental.pallas import tpu as pltpu
from jax.sharding import Mesh
from jax.sharding import PartitionSpec as P

MEM = 32
STEPS = 4
LANES = 128
HALF = 8
TM = ("tm_0", "tm_1")
LAT = ("lat_0", "lat_1")
TM_LAT = ("tm_0", "tm_1", "lat_0", "lat_1")


def east(value):
    return pltpu.roll(value, value.shape[-1] - 1, 1)


def west(value):
    return pltpu.roll(value, 1, 1)


def wrap(ref, lons):
    tail = lons % LANES
    half = (LANES - tail) // 2
    first = ref[:, 0:LANES]
    lane = lax.broadcasted_iota(jnp.int32, first.shape, 1)
    last = jnp.where(lane < tail, ref[:, lons - tail :], 0.0)
    ref[:, lons - tail :] = jnp.where(
        lane < tail, last, jnp.where(lane < tail + half, pltpu.roll(first, tail, 1), pltpu.roll(last, LANES - tail, 1))
    )


def fetch(source, first, size, target, sem):
    return pltpu.make_async_copy(source.at[0, :, pl.ds(first, size), :], target, sem)


def edge_kernel(inc_hbm, lon_hbm, lat_hbm, out_ref, inc, lon, lat, sems):
    core = lax.axis_index("ens")
    lons = inc.shape[-1]
    levels = inc.shape[0]

    def rows(first, at):
        copies = [
            fetch(source, first, HALF, target, sems.at[i])
            for i, (source, target) in enumerate(((inc_hbm, inc), (lon_hbm, lon), (lat_hbm, lat)))
        ]
        for copy in copies:
            copy.start()
        sign = 1.0 if at(0) == 7 else -1.0
        for i, copy in enumerate(copies):
            copy.wait()
            buf = (inc, lon, lat)[i]
            base = (0, 4, 7)[i]
            for q in range(4 if i == 0 else 3):
                r = 3 - q if i == 0 else 2 - q
                value = buf[:, at(r), :]
                if i == 2:
                    value = sign * value
                out_ref[base + q, :, 0:lons] = value
                wrap(out_ref.at[base + q], lons)

    @pl.when(core == 0)
    def _():
        rows(0, lambda r: r)

    @pl.when(core == 1)
    def _():
        rows(HALF, lambda r: 7 - r)


def prepare_kernel(inc_hbm, lon_hbm, lat_hbm, prec_ref, own_ref, field_ref, coef_ref, prec_out, inc, lon, lat, sems):
    core = lax.axis_index("ens")
    lons = inc.shape[-1]
    levels = inc.shape[0]
    copies = [
        fetch(source, 0, 2 * HALF, target, sems.at[i])
        for i, (source, target) in enumerate(((inc_hbm, inc), (lon_hbm, lon), (lat_hbm, lat)))
    ]
    for copy in copies:
        copy.start()
    level = lax.broadcasted_iota(jnp.int32, prec_out.shape, 0)
    prec = jnp.zeros(prec_out.shape, jnp.float32)
    for k in range(levels):
        prec = jnp.where(level == k, prec_ref[k], prec)
    prec_out[...] = prec
    for copy in copies:
        copy.wait()

    def rows(at, sign):
        for r in range(12):
            field_ref[r, :, 0:lons] = inc[:, at(r), :]
            wrap(field_ref.at[r], lons)
            if r < HALF:
                own_ref[r] = field_ref[r]
            coef_ref[1, r, :, 0:lons] = lon[:, at(r), :]
            wrap(coef_ref.at[1, r], lons)
            coef_ref[4, r, :, 0:lons] = sign * lat[:, at(r), :]
            wrap(coef_ref.at[4, r], lons)
            store_coefficients(coef_ref, r, coef_ref[1, r], coef_ref[4, r])

    @pl.when(core == 0)
    def _():
        rows(lambda r: r, 1.0)

    @pl.when(core == 1)
    def _():
        rows(lambda r: 15 - r, -1.0)


def store_coefficients(coef_ref, at, c, e):
    cc = c * c
    ee = e * e
    coef_ref[0, at] = 1.0 - cc - ee
    coef_ref[1, at] = 0.5 * (cc - c)
    coef_ref[2, at] = 0.5 * (cc + c)
    coef_ref[3, at] = 0.5 * (ee - e)
    coef_ref[4, at] = 0.5 * (ee + e)


class Rows:
    def __init__(self, halo_ref, own_ref, at):
        self.halo, self.own, self.at = halo_ref, own_ref, at

    def __getitem__(self, j):
        return self.halo[self.at, j] if j < 4 else self.own[self.at, j - 4]


def forward_kernel(
    field_ref, coef_ref, prec_ref, halo_ref, next_ref, jac_hbm, rows_hbm, rows_ref, counts_ref, val_ref, oprec_ref,
    later_ref, adj_ref, outer_ref, inner_ref, edge_ref, x0, x1, pk, wgt, jac, rows, sems,
):
    core = lax.axis_index("ens")
    has_next = (lax.axis_index(TM) < lax.axis_size(TM) - 1).astype(jnp.float32)
    blocks, slots, lons = jac.shape
    jac_copy = pltpu.make_async_copy(jac_hbm.at[0], jac, sems.at[0])
    rows_copy = pltpu.make_async_copy(rows_hbm, rows, sems.at[1])
    jac_copy.start()
    rows_copy.start()
    x0[0:4] = halo_ref[0:4]
    x0[4:16] = field_ref[...]
    center, plon, mlon, plat, mlat = (Rows(edge_ref, coef_ref, i) for i in range(5))
    edge_ref[3, 0] = jnp.ones(x0.shape[1:], jnp.float32)
    for r in range(3):
        store_coefficients(edge_ref, 1 + r, halo_ref[4 + r], halo_ref[7 + r])

    bufs = (x0, x1)
    for step in range(STEPS):
        src, dst = bufs[step % 2], bufs[(step + 1) % 2]
        for j in range(step + 1, 15 - step):
            f = src[j]
            dst[j] = (
                center[j] * f + plon[j] * east(f) + mlon[j] * west(f) + plat[j] * src[j + 1] + mlat[j] * src[j - 1]
            )
    field = bufs[STEPS % 2]
    prec = prec_ref[...] * has_next
    for r in range(HALF):
        later = prec * (next_ref[r] - field[4 + r])
        later_ref[r] = later
        adj_ref[r] = -later

    rows_copy.wait()
    jac_copy.wait()

    def place(j):
        r = rows[0, j]
        lat = r % 16
        row = jnp.clip(jnp.where(core == 0, lat, 15 - lat), 0, HALF - 1)
        return row, pl.ds(r // 16, 1)

    for j in range(blocks):
        row, lev = place(j)
        pk[pl.ds(j, 1), :] = field[4 + row, lev, :]
    lane = lax.broadcasted_iota(jnp.int32, (slots, blocks), 1)
    slot = lax.broadcasted_iota(jnp.int32, (slots, blocks), 0)
    ev = jnp.zeros((slots, blocks), jnp.float32)
    for j in range(blocks):
        total = jnp.sum(jac[j] * pk[pl.ds(j, 1), 0:lons], axis=1, keepdims=True)
        ev = jnp.where(lane == j, total, ev)
    mine = (rows_ref[...] % 16) // HALF == core
    used = (slot < counts_ref[...]) & mine
    wgt[...] = jnp.where(used, oprec_ref[...] * (ev - val_ref[...]), 0.0)
    for j in range(blocks):
        w = jnp.sum(jnp.where(lane == j, wgt[...], 0.0), axis=1, keepdims=True)
        pk[pl.ds(j, 1), 0:lons] = jnp.sum(jac[j] * w, axis=0, keepdims=True)
    wrap(pk, lons)
    for j in range(blocks):
        row, lev = place(j)
        adj_ref[row, lev, :] = adj_ref[row, lev, :] + pk[pl.ds(j, 1), :]

    for q in range(4):
        outer_ref[q] = adj_ref[3 - q] * mlat[7] if q == 0 else adj_ref[3 - q]
        inner_ref[q] = adj_ref[7 - q]


def adjoint_kernel(adj_ref, outer_ref, inner_ref, edge_ref, coef_ref, forcing_ref, start_ref, g0, g1, total):
    core = lax.axis_index("ens")
    lons = forcing_ref.shape[-1]
    center, plon, mlon, plat, mlat = (Rows(edge_ref, coef_ref, i) for i in range(5))
    g0[0:4] = outer_ref[...]
    g0[4:12] = adj_ref[...]
    g0[12:16] = inner_ref[...]
    bufs = (g0, g1)
    for step in range(STEPS):
        src, dst = bufs[step % 2], bufs[(step + 1) % 2]
        for j in range(step + 1, 15 - step):
            g = src[j]
            out = (
                center[j] * g
                + west(plon[j] * g)
                + east(mlon[j] * g)
                + plat[j - 1] * src[j - 1]
                + mlat[j + 1] * src[j + 1]
            )
            if step + 1 < STEPS:
                dst[j] = out
                if 4 <= j < 12:
                    total[j - 4] = (g if step == 0 else total[j - 4]) + out
            else:
                start_ref[j - 4] = out

    @pl.when(core == 0)
    def _():
        for r in range(HALF):
            forcing_ref[:, r, :] = total[r, :, 0:lons]

    @pl.when(core == 1)
    def _():
        for r in range(HALF):
            forcing_ref[:, 7 - r, :] = total[r, :, 0:lons]


def product_kernel(pieces_ref, own_ref, other_ref, start_ref, mismatch_ref, inc_ref, prec_ref, out_ref, grad_ref):
    core = lax.axis_index("ens")
    first_window = lax.axis_index(TM) == 0
    prec = prec_ref[...]
    for r in range(HALF):
        grad_ref[r] = start_ref[r] + jnp.where(first_window, prec * inc_ref[r], mismatch_ref[r])
    forcing = jnp.sum(pieces_ref[...], axis=0)
    lane = lax.broadcasted_iota(jnp.int32, (HALF, LANES), 1)
    members = own_ref.shape[0]
    first = pl.multiple_of(HALF * core, HALF)
    vec = jnp.zeros((HALF, LANES), jnp.float32)
    for m in range(2 * members):
        ref, at = (own_ref, m) if m < members else (other_ref, m - members)
        col = jnp.sum(ref[at, 0, pl.ds(first, HALF), :] * forcing, axis=1, keepdims=True)
        vec = jnp.where(lane == m, col, vec)
    vec = jnp.sum(vec, axis=0, keepdims=True)
    out_ref[...] = jnp.broadcast_to(vec[None], out_ref.shape)


def sum_kernel(sums_ref, out_ref):
    vec = jnp.sum(sums_ref[...], axis=0)
    out_ref[...] = jnp.broadcast_to(vec, out_ref.shape)


def step_kernel(sum_ref, other_sum_ref, own_ref, other_ref, out_ref):
    members = own_ref.shape[0]
    lane = lax.broadcasted_iota(jnp.int32, (HALF, LANES), 1)
    theirs = other_sum_ref[...]
    swapped = jnp.where(
        lane < members, pltpu.roll(theirs, LANES - members, 1), pltpu.roll(theirs, members, 1)
    )
    vec = (sum_ref[...] + swapped) * (-1.0 / (MEM - 1.0))
    coefs = [jnp.sum(jnp.where(lane == m, vec, 0.0), axis=1, keepdims=True) for m in range(2 * members)]
    for half in range(2):
        rows = pl.ds(HALF * half, HALF)
        total = coefs[0] * own_ref[0, 0, rows, :]
        for m in range(1, 2 * members):
            ref, at = (own_ref, m) if m < members else (other_ref, m - members)
            total = total + coefs[m] * ref[at, 0, rows, :]
        out_ref[0, rows, :] = total


def gradient_kernel(own_ref, other_ref, out_ref):
    core = lax.axis_index("ens")
    lons = out_ref.shape[-1]

    def store(north, south):
        for r in range(HALF):
            out_ref[0, :, r, :] = north[r, :, 0:lons]
            out_ref[0, :, 15 - r, :] = south[r, :, 0:lons]

    @pl.when(core == 0)
    def _():
        store(own_ref, other_ref)

    @pl.when(core == 1)
    def _():
        store(other_ref, own_ref)


VMEM = pl.BlockSpec(memory_space=pltpu.VMEM)
SMEM = pl.BlockSpec(memory_space=pltpu.SMEM)
ANY = pl.BlockSpec(memory_space=pl.ANY)
HBM = pl.BlockSpec(memory_space=pltpu.HBM)


def buf(*shape):
    return pltpu.VMEM(shape, jnp.float32)


def call(kernel, ins, outs, scratch=(), limit=40):
    return pl.pallas_call(
        kernel,
        out_shape=[jax.ShapeDtypeStruct(s, jnp.float32) for s in outs],
        in_specs=ins,
        out_specs=[VMEM] * len(outs),
        scratch_shapes=list(scratch),
        compiler_params=pltpu.CompilerParams(vmem_limit_bytes=limit * 2**20),
    )


def on_device(
    increment,
    wind_lon,
    wind_lat,
    model_precision,
    perturbations,
    obs_rows,
    obs_jacobian,
    obs_values,
    obs_precision,
    obs_counts,
):
    count_t = lax.axis_size(TM)
    count_l = lax.axis_size(LAT)
    levels, band_rows, lons = increment.shape[1:]
    wide = lons + (-lons % LANES)
    blocks, slots = obs_values.shape[1:]

    trade = []
    for i in range(count_l - 1):
        trade += [(2 * i + 1, 2 * i + 2), (2 * i + 2, 2 * i + 1)]
    band = LAT + ("ens",)
    partner = [(0, 1), (1, 0)]
    own = (HALF, levels, wide)
    quarter = (4, levels, wide)
    fields = (increment, wind_lon, wind_lat)
    piece = buf(levels, HALF, lons)
    whole = buf(levels, band_rows, lons)

    (outgoing,) = call(
        edge_kernel, [HBM] * 3, [(10, levels, wide)], [piece, piece, piece, pltpu.SemaphoreType.DMA((3,))]
    )(*fields)
    halo = lax.ppermute(outgoing, band, trade)
    own_rows, field, coefs, prec = call(
        prepare_kernel,
        [ANY] * 3 + [SMEM],
        [own, (12, levels, wide), (5, 12, levels, wide), (levels, wide)],
        [whole, whole, whole, pltpu.SemaphoreType.DMA((3,))],
    )(*fields, model_precision)
    next_rows = lax.ppermute(own_rows, TM, [(i + 1, i) for i in range(count_t - 1)])
    other_pert = lax.ppermute(perturbations, "ens", partner)

    later, adj, outer, inner, edges = call(
        forward_kernel,
        [VMEM] * 5 + [ANY, ANY] + [VMEM] * 4,
        [own, own, quarter, quarter, (5, 4, levels, wide)],
        [
            buf(16, levels, wide), buf(16, levels, wide), buf(blocks, wide), buf(slots, blocks),
            buf(blocks, slots, lons), pltpu.SMEM((1, blocks), jnp.int32), pltpu.SemaphoreType.DMA((2,)),
        ],
    )(
        field, coefs, prec, halo, next_rows, obs_jacobian, obs_rows, obs_rows, obs_counts,
        obs_values[0].T, obs_precision[0].T,
    )
    outer = lax.ppermute(outer, band, trade)
    inner = lax.ppermute(inner, "ens", partner)
    mismatch = lax.ppermute(later, TM, [(i, i + 1) for i in range(count_t - 1)])

    forcing, start = call(
        adjoint_kernel,
        [VMEM] * 5,
        [(levels, HALF, lons), own],
        [buf(16, levels, wide), buf(16, levels, wide), buf(*own)],
    )(adj, outer, inner, edges, coefs)
    forcing, mismatch = lax.optimization_barrier((forcing, mismatch))
    pieces = lax.all_to_all(forcing, TM, 0, 0, tiled=True)

    products, own_grad = call(product_kernel, [VMEM] * 7, [(count_t * count_l, 1, LANES), own])(
        pieces, perturbations, other_pert, start, mismatch, own_rows, prec
    )
    other_grad = lax.ppermute(own_grad, "ens", partner)
    sums = lax.all_to_all(products, TM_LAT, 0, 0, tiled=True)
    (grad_state,) = call(gradient_kernel, [VMEM] * 2, [(1, levels, band_rows, lons)])(own_grad, other_grad)

    (total,) = call(sum_kernel, [VMEM], [(HALF, LANES)])(sums)
    other_total = lax.ppermute(total, "ens", partner)
    (forcing_step,) = call(step_kernel, [VMEM] * 4, [(1, band_rows, lons)])(
        total, other_total, perturbations, other_pert
    )
    return (grad_state, forcing_step)


def solution(mesh):
    torus = Mesh(
        mesh.devices.reshape(2, 4, 8, 2, mesh.shape["ens"]),
        ("tm_0", "tm_1", "lat_0", "lat_1", "ens"),
    )
    in_specs = (
        P(TM, None, LAT, None),
        P(TM, None, LAT, None),
        P(TM, None, LAT, None),
        P(),
        P("ens", TM, LAT, None),
        P(TM, LAT),
        P(TM, LAT, None, None),
        P(TM, LAT, None),
        P(TM, LAT, None),
        P(TM, LAT),
    )
    out_specs = (P(TM, None, LAT, None), P(TM, LAT, None))

    return jax.shard_map(on_device, mesh=torus, in_specs=in_specs, out_specs=out_specs, check_vma=False)
```

time: 102 us -> 93.5 us (0.917)
  blocking collectives: 18.8 us -> 44.4 us
  local copies, waits for them, and re-layouts: 20 us -> 4.72 us
  starting transfers between devices: 31.5 us -> 17.9 us
  Pallas kernels: 12.5 us -> 10.1 us
  other arithmetic: 1.74 us -> 0 us
    all_to_all x0 -> x1, blocking collectives: none -> 27.9 us  [on_device(): sums = lax.all_to_all(products, TM_LAT, 0, 0, tiled=True)]
    all_to_all x1 -> x0, starting transfers between devices: 15.4 us -> none  [on_device(): sums = lax.all_to_all(products, ALL, 0, 0, tiled=True)]
    all_to_all x1 -> x0, waiting for transfers between devices: 11.4 us -> none  [on_device(): sums = lax.all_to_all(products, ALL, 0, 0, tiled=True)]
    ppermute x1, waiting for transfers between devices: 0.01 us -> 9.72 us  [on_device(): lax.ppermute(own_rows, TM, [(i + 1, i) for i in range(count_t - 1)])]
    concatenate x5 -> x0, local copies, waits for them, and re-layouts: 5.9 us -> none  [wrapped(): jnp.concatenate([value, value[..., :half], value[..., lon - half:]], axis...]
    dynamic_slice x12 -> x0, local copies, waits for them, and re-layouts: 4.45 us -> none  [rows_of(): return lax.dynamic_slice_in_dim(value[0], start, size, axis=1)]
    ppermute x1, starting transfers between devices: 0.09 us -> 3.29 us  [on_device(): other_pert = lax.ppermute(perturbations, 'ens', partner)]
    slice x5 -> x0, local copies, waits for them, and re-layouts: 2.38 us -> none  [wrapped(): value[..., lon - half:]]
  transfers between devices with their start and end apart: 8 -> 8, of which waited for: 2 -> 3; matrix products, arithmetic and copies ran while one was open for 14% -> 0% of each run, Pallas kernels for 10% -> 9%
where the time goes in v2:
time: 93.5 us; the launch traced here: 93.1 us
  blocking collectives  44.4 us (47%)
  starting transfers between devices  17.9 us (19%)
  waiting for transfers between devices  15.2 us (16%)
  Pallas kernels  10.1 us (11%)
  local copies, waits for them, and re-layouts  4.72 us (5%)
    all_to_all x1, blocking collectives, on_device(): sums = lax.all_to_all(products, TM_LAT, 0, 0, tiled=True)  27.9 us
    all_to_all x1, blocking collectives, on_device(): pieces = lax.all_to_all(forcing, TM, 0, 0, tiled=True)  16.5 us
    ppermute x1, waiting for transfers between devices, on_device(): lax.ppermute(own_rows, TM, [(i + 1, i) for i in range(count_t - 1)])  9.72 us
    ppermute x1, starting transfers between devices, on_device(): outer = lax.ppermute(outer, band, trade)  6.92 us
    unnamed x20, local copies, waits for them, and re-layouts  4.72 us
    ppermute x1, waiting for transfers between devices, on_device(): outer = lax.ppermute(outer, band, trade)  4.6 us
    pallas_call x1, Pallas kernels, on_device(): call(forward_kernel, [VMEM] * 5 + [ANY, ANY] + [VMEM] * 4, [own, own, qua...  3.86 us
    ppermute x1, starting transfers between devices, on_device(): other_pert = lax.ppermute(perturbations, 'ens', partner)  3.29 us
  transfers between devices with their start and end apart: 8, of which 3 were waited for; matrix products, arithmetic and copies ran while one was open for 0% of the time, Pallas kernels for 9%

profile of v2, /device:TPU:1, one launch (start us, length us, event | category | flops | bytes accessed | tf_op | source)
XLA Modules:
  0.0 93.1 jit_solution(1922683964079673006)
XLA Ops:
  0.6 3.3 %collective-permute-start.5 = (f32[16,1,16,1440]{3,2,1,0:T(8,128)}, f32[16,1,16,1440]{3,2,1,0:T(8,128)S(1)}, u32[]{:S(2)}, u32[]{:S(2)}) collective-permute-start(f32[16,1,16,1440]{3,2,1,0:T(8,128)} %own_ref.3), channel_id=1, source_target_pairs={{0,1},{1,0},{2,3},{3,2},{4,5},{5,4},{6,7},{7,6},{8,9},{9,8},{10,11... | collective-permute-start | bytes 4423688 | tf_op jit(solution)/shard_map/ppermute | solution.py:357
  3.9 1.1 %copy-done.2 = f32[1,8,16,1440]{3,2,1,0:T(8,128)S(1)} copy-done((f32[1,8,16,1440]{3,2,1,0:T(8,128)S(1)}, f32[1,8,16,1440]{3,2,1,0:T(8,128)}, u32[]{:S(2)}) %copy-start.2) | copy-done | bytes 737304
  5.1 1.1 %copy-done.3 = f32[1,8,16,1440]{3,2,1,0:T(8,128)S(1)} copy-done((f32[1,8,16,1440]{3,2,1,0:T(8,128)S(1)}, f32[1,8,16,1440]{3,2,1,0:T(8,128)}, u32[]{:S(2)}) %copy-start.3) | copy-done | bytes 737304
  6.2 1.1 %copy-done.4 = f32[1,8,16,1440]{3,2,1,0:T(8,128)S(1)} copy-done((f32[1,8,16,1440]{3,2,1,0:T(8,128)S(1)}, f32[1,8,16,1440]{3,2,1,0:T(8,128)}, u32[]{:S(2)}) %copy-start.4) | copy-done | bytes 737304
  7.3 0.5 shard_map.114
  7.8 3.0 %collective-permute-start = (f32[10,8,1536]{2,1,0:T(8,128)S(1)}, f32[10,8,1536]{2,1,0:T(8,128)S(1)}, u32[]{:S(2)}, u32[]{:S(2)}) collective-permute-start(f32[10,8,1536]{2,1,0:T(8,128)S(1)} %shard_map.114), channel_id=1, source_target_pairs={{1,2},{2,1},{3,4},{4,3},{5,6},{6,5},{7,8},{8,7},{9,10},{10,9},{11,... | collective-permute-start | bytes 1474568 | tf_op jit(solution)/shard_map/ppermute | solution.py:349
  10.8 0.0 copy-start.8
  10.8 0.6 copy-done.8
  11.5 1.5 %shard_map.113 = (f32[8,8,1536]{2,1,0:T(8,128)S(1)}, f32[12,8,1536]{2,1,0:T(8,128)S(1)}, f32[5,12,8,1536]{3,2,1,0:T(8,128)S(1)}, f32[8,1536]{1,0:T(8,128)S(1)}) custom-call(f32[1,8,16,1440]{3,2,1,0:T(8,128)S(1)} %copy-done.2, f32[1,8,16,1440]{3,2,1,0:T(8,128)S(1)} %copy-done.3, f32[1,8,16,1440]{3,2,1,0:T(8,128)S(1)} %copy-done.4, f32[8]{0:T(128)S(1)} %copy-done.8), custom_call_target="tpu_custom_call" | custom-call | tf_op jit(solution)/shard_map/pallas_call | solution.py:350
  13.0 1.3 %collective-permute-start.1 = (f32[8,8,1536]{2,1,0:T(8,128)S(1)}, f32[8,8,1536]{2,1,0:T(8,128)S(1)}, u32[]{:S(2)}, u32[]{:S(2)}) collective-permute-start(f32[8,8,1536]{2,1,0:T(8,128)S(1)} %get-tuple-element.20.inc_ref), channel_id=1, source_target_pairs={{32,0},{64,32},{96,64},{128,96},{160,128},{192,160},{224,192},{33,... | collective-permute-start | bytes 1179656 | tf_op jit(solution)/shard_map/ppermute | solution.py:356
  14.3 9.7 %collective-permute-done.1.next_ref = f32[8,8,1536]{2,1,0:T(8,128)S(1)} collective-permute-done((f32[8,8,1536]{2,1,0:T(8,128)S(1)}, f32[8,8,1536]{2,1,0:T(8,128)S(1)}, u32[]{:S(2)}, u32[]{:S(2)}) %collective-permute-start.1) | collective-permute-done | bytes 393248 | tf_op jit(solution)/shard_map/ppermute | solution.py:356
  24.0 0.0 collective-permute-done.halo_ref
  24.0 0.0 copy-start.9
  24.1 0.6 copy-done.9
  24.7 3.9 %shard_map.115 = (f32[8,8,1536]{2,1,0:T(8,128)S(1)}, f32[8,8,1536]{2,1,0:T(8,128)S(1)}, f32[4,8,1536]{2,1,0:T(8,128)S(1)}, f32[4,8,1536]{2,1,0:T(8,128)S(1)}, f32[5,4,8,1536]{3,2,1,0:T(8,128)S(1)}) custom-call(f32[12,8,1536]{2,1,0:T(8,128)S(1)} %get-tuple-element.17.field_ref, f32[5,12,8,1536]{3,2,1,0:T(8,128)S(1)} %get-tuple-element.18.coef_ref, ...), custom_call_target="tpu_custom_call" | custom-call | tf_op jit(solution)/shard_map/pallas_call | solution.py:359
  28.6 0.0 copy-start
  28.6 1.7 %collective-permute-start.4 = (f32[8,8,1536]{2,1,0:T(8,128)S(1)}, f32[8,8,1536]{2,1,0:T(8,128)S(1)}, u32[]{:S(2)}, u32[]{:S(2)}) collective-permute-start(f32[8,8,1536]{2,1,0:T(8,128)S(1)} %get-tuple-element.26), channel_id=1, source_target_pairs={{0,32},{32,64},{64,96},{96,128},{128,160},{160,192},{192,224},{1,3... | collective-permute-start | bytes 1179656 | tf_op jit(solution)/shard_map/ppermute | solution.py:373
  30.2 6.9 %collective-permute-start.2 = (f32[4,8,1536]{2,1,0:T(8,128)S(1)}, f32[4,8,1536]{2,1,0:T(8,128)S(1)}, u32[]{:S(2)}, u32[]{:S(2)}) collective-permute-start(f32[4,8,1536]{2,1,0:T(8,128)S(1)} %get-tuple-element.22), channel_id=1, source_target_pairs={{1,2},{2,1},{3,4},{4,3},{5,6},{6,5},{7,8},{8,7},{9,10},{10,9},{11,... | collective-permute-start | bytes 589832 | tf_op jit(solution)/shard_map/ppermute | solution.py:371
  37.2 0.1 collective-permute-start.3
  37.3 4.6 %collective-permute-done.2.outer_ref = f32[4,8,1536]{2,1,0:T(8,128)S(1)} collective-permute-done((f32[4,8,1536]{2,1,0:T(8,128)S(1)}, f32[4,8,1536]{2,1,0:T(8,128)S(1)}, u32[]{:S(2)}, u32[]{:S(2)}) %collective-permute-start.2) | collective-permute-done | bytes 196640 | tf_op jit(solution)/shard_map/ppermute | solution.py:371
  41.9 0.0 collective-permute-done.3.inner_ref
  41.9 1.7 %shard_map.116 = (f32[8,8,1440]{2,1,0:T(8,128)S(1)}, f32[8,8,1536]{2,1,0:T(8,128)S(1)}) custom-call(f32[8,8,1536]{2,1,0:T(8,128)S(1)} %get-tuple-element.21.adj_ref, f32[4,8,1536]{2,1,0:T(8,128)S(1)} %collective-permute-done.2.outer_ref, f32[4,8,1536]{2,1,0:T(8,128)S(1)} %collective-permute-done.3.inner_ref, ...), custom_call_target="tpu_custom_call" | custom-call | tf_op jit(solution)/shard_map/pallas_call | solution.py:375
  43.6 16.5 %all_to_all.10.pieces_ref = f32[8,8,1440]{2,1,0:T(8,128)S(1)} all-to-all(f32[8,8,1440]{2,1,0:T(8,128)S(1)} %get-tuple-element.27), channel_id=1, replica_groups=mesh['tm_0'=2,'tm_1'=4,'lat_0'=8,'lat_1'=2,'ens'=2] {'tm_0','tm_1'}, dimensions={0} | all-to-all | bytes 737280 | tf_op jit(solution)/shard_map/all_to_all | solution.py:382
  60.1 0.0 collective-permute-done.5.other_ref
  60.1 0.3 shard_map.117
  60.4 0.1 collective-permute-start.6
  60.5 27.9 %all_to_all.11.sums_ref = f32[128,1,128]{2,1,0:T(1,128)S(1)} all-to-all(f32[128,1,128]{2,1,0:T(1,128)S(1)} %get-tuple-element.31), channel_id=1, replica_groups=mesh['tm_0'=2,'tm_1'=4,'lat_0'=8,'lat_1'=2,'ens'=2] {'tm_0','tm_1','lat_..., dimensions={0} | all-to-all | bytes 131072 | tf_op jit(solution)/shard_map/all_to_all | solution.py:388
  88.4 0.1 shard_map.119.sum_ref
  88.6 1.6 %collective-permute-start.7 = (f32[8,128]{1,0:T(8,128)S(1)}, f32[8,128]{1,0:T(8,128)S(1)}, u32[]{:S(2)}, u32[]{:S(2)}) collective-permute-start(f32[8,128]{1,0:T(8,128)S(1)} %shard_map.119.sum_ref), channel_id=1, source_target_pairs={{0,1},{1,0},{2,3},{3,2},{4,5},{5,4},{6,7},{7,6},{8,9},{9,8},{10,11... | collective-permute-start | bytes 12296 | tf_op jit(solution)/shard_map/ppermute | solution.py:392
  90.1 0.8 collective-permute-done.7.other_sum_ref
  91.0 1.0 %shard_map.120 = f32[1,16,1440]{2,1,0:T(8,128)} custom-call(f32[8,128]{1,0:T(8,128)S(1)} %shard_map.119.sum_ref, f32[8,128]{1,0:T(8,128)S(1)} %collective-permute-done.7.other_sum_ref, f32[16,1,16,1440]{3,2,1,0:T(8,128)S(1)} %copy-done, f32[16,1,16,1440]{3,2,1,0:T(8,128)S(1)} %collective-permute-done.5.other_ref), custom_call_target="tpu_custom_call" | custom-call | tf_op jit(solution)/shard_map/pallas_call | solution.py:393
  92.0 1.1 %shard_map.118 = f32[1,8,16,1440]{3,2,1,0:T(8,128)} custom-call(f32[8,8,1536]{2,1,0:T(8,128)S(1)} %get-tuple-element.30.own_ref, f32[8,8,1536]{2,1,0:T(8,128)S(1)} %collective-permute-done.6.other_ref), custom_call_target="tpu_custom_call" | custom-call | tf_op jit(solution)/shard_map/pallas_call | solution.py:389
  (14 shorter events, 0.0 us)
Async XLA Ops:
  0.6 23.4 %copy-start.1 = (f32[1,32,16,1440]{3,2,1,0:T(8,128)S(1)}, f32[1,32,16,1440]{3,2,1,0:T(8,128)}, u32[]{:S(2)}) copy-start(f32[1,32,16,1440]{3,2,1,0:T(8,128)} %jac_hbm.1) | copy-start | bytes 8847364
  0.6 59.5 %collective-permute-start.5 = (f32[16,1,16,1440]{3,2,1,0:T(8,128)}, f32[16,1,16,1440]{3,2,1,0:T(8,128)S(1)}, u32[]{:S(2)}, u32[]{:S(2)}) collective-permute-start(f32[16,1,16,1440]{3,2,1,0:T(8,128)} %own_ref.3), channel_id=1, source_target_pairs={{0,1},{1,0},{2,3},{3,2},{4,5},{5,4},{6,7},{7,6},{8,9},{9,8},{10,11... | collective-permute-start | bytes 4423688 | tf_op jit(solution)/shard_map/ppermute | solution.py:357
  3.9 1.1 %copy-start.2 = (f32[1,8,16,1440]{3,2,1,0:T(8,128)S(1)}, f32[1,8,16,1440]{3,2,1,0:T(8,128)}, u32[]{:S(2)}) copy-start(f32[1,8,16,1440]{3,2,1,0:T(8,128)} %inc_hbm.3) | copy-start | bytes 2211844
  5.1 1.1 %copy-start.3 = (f32[1,8,16,1440]{3,2,1,0:T(8,128)S(1)}, f32[1,8,16,1440]{3,2,1,0:T(8,128)}, u32[]{:S(2)}) copy-start(f32[1,8,16,1440]{3,2,1,0:T(8,128)} %lon_hbm.3) | copy-start | bytes 2211844
  6.2 1.1 %copy-start.4 = (f32[1,8,16,1440]{3,2,1,0:T(8,128)S(1)}, f32[1,8,16,1440]{3,2,1,0:T(8,128)}, u32[]{:S(2)}) copy-start(f32[1,8,16,1440]{3,2,1,0:T(8,128)} %lat_hbm.3) | copy-start | bytes 2211844
  7.3 16.7 %copy-start.5 = (f32[1,32,16]{1,2,0:T(8,128)S(1)}, f32[1,32,16]{1,2,0:T(8,128)}, u32[]{:S(2)}) copy-start(f32[1,32,16]{1,2,0:T(8,128)} %param.17) | copy-start | bytes 6148
  7.3 16.7 %copy-start.6 = (f32[1,32,16]{1,2,0:T(8,128)S(1)}, f32[1,32,16]{1,2,0:T(8,128)}, u32[]{:S(2)}) copy-start(f32[1,32,16]{1,2,0:T(8,128)} %param.18) | copy-start | bytes 6148
  7.3 16.7 %copy-start.7 = (s32[1,32]{1,0:T(1,128)S(1)}, s32[1,32]{1,0:T(1,128)}, u32[]{:S(2)}) copy-start(s32[1,32]{1,0:T(1,128)} %rows_ref.1) | copy-start | bytes 388
  7.8 16.2 %collective-permute-start = (f32[10,8,1536]{2,1,0:T(8,128)S(1)}, f32[10,8,1536]{2,1,0:T(8,128)S(1)}, u32[]{:S(2)}, u32[]{:S(2)}) collective-permute-start(f32[10,8,1536]{2,1,0:T(8,128)S(1)} %shard_map.114), channel_id=1, source_target_pairs={{1,2},{2,1},{3,4},{4,3},{5,6},{6,5},{7,8},{8,7},{9,10},{10,9},{11,... | collective-permute-start | bytes 1474568 | tf_op jit(solution)/shard_map/ppermute | solution.py:349
  10.8 0.7 copy-start.8
  13.0 11.0 %collective-permute-start.1 = (f32[8,8,1536]{2,1,0:T(8,128)S(1)}, f32[8,8,1536]{2,1,0:T(8,128)S(1)}, u32[]{:S(2)}, u32[]{:S(2)}) collective-permute-start(f32[8,8,1536]{2,1,0:T(8,128)S(1)} %get-tuple-element.20.inc_ref), channel_id=1, source_target_pairs={{32,0},{64,32},{96,64},{128,96},{160,128},{192,160},{224,192},{33,... | collective-permute-start | bytes 1179656 | tf_op jit(solution)/shard_map/ppermute | solution.py:356
  24.0 0.7 copy-start.9
  28.6 31.5 %copy-start = (f32[16,1,16,1440]{3,2,1,0:T(8,128)S(1)}, f32[16,1,16,1440]{3,2,1,0:T(8,128)}, u32[]{:S(2)}) copy-start(f32[16,1,16,1440]{3,2,1,0:T(8,128)} %own_ref.3) | copy-start | bytes 4423684
  28.6 15.0 %collective-permute-start.4 = (f32[8,8,1536]{2,1,0:T(8,128)S(1)}, f32[8,8,1536]{2,1,0:T(8,128)S(1)}, u32[]{:S(2)}, u32[]{:S(2)}) collective-permute-start(f32[8,8,1536]{2,1,0:T(8,128)S(1)} %get-tuple-element.26), channel_id=1, source_target_pairs={{0,32},{32,64},{64,96},{96,128},{128,160},{160,192},{192,224},{1,3... | collective-permute-start | bytes 1179656 | tf_op jit(solution)/shard_map/ppermute | solution.py:373
  30.2 11.6 %collective-permute-start.2 = (f32[4,8,1536]{2,1,0:T(8,128)S(1)}, f32[4,8,1536]{2,1,0:T(8,128)S(1)}, u32[]{:S(2)}, u32[]{:S(2)}) collective-permute-start(f32[4,8,1536]{2,1,0:T(8,128)S(1)} %get-tuple-element.22), channel_id=1, source_target_pairs={{1,2},{2,1},{3,4},{4,3},{5,6},{6,5},{7,8},{8,7},{9,10},{10,9},{11,... | collective-permute-start | bytes 589832 | tf_op jit(solution)/shard_map/ppermute | solution.py:371
  37.2 4.7 %collective-permute-start.3 = (f32[4,8,1536]{2,1,0:T(8,128)S(1)}, f32[4,8,1536]{2,1,0:T(8,128)S(1)}, u32[]{:S(2)}, u32[]{:S(2)}) collective-permute-start(f32[4,8,1536]{2,1,0:T(8,128)S(1)} %get-tuple-element.23), channel_id=1, source_target_pairs={{0,1},{1,0},{2,3},{3,2},{4,5},{5,4},{6,7},{7,6},{8,9},{9,8},{10,11... | collective-permute-start | bytes 589832 | tf_op jit(solution)/shard_map/ppermute | solution.py:372
  60.4 31.6 %collective-permute-start.6 = (f32[8,8,1536]{2,1,0:T(8,128)S(1)}, f32[8,8,1536]{2,1,0:T(8,128)S(1)}, u32[]{:S(2)}, u32[]{:S(2)}) collective-permute-start(f32[8,8,1536]{2,1,0:T(8,128)S(1)} %get-tuple-element.30.own_ref), channel_id=1, source_target_pairs={{0,1},{1,0},{2,3},{3,2},{4,5},{5,4},{6,7},{7,6},{8,9},{9,8},{10,11... | collective-permute-start | bytes 1179656 | tf_op jit(solution)/shard_map/ppermute | solution.py:387
  88.6 2.4 %collective-permute-start.7 = (f32[8,128]{1,0:T(8,128)S(1)}, f32[8,128]{1,0:T(8,128)S(1)}, u32[]{:S(2)}, u32[]{:S(2)}) collective-permute-start(f32[8,128]{1,0:T(8,128)S(1)} %shard_map.119.sum_ref), channel_id=1, source_target_pairs={{0,1},{1,0},{2,3},{3,2},{4,5},{5,4},{6,7},{7,6},{8,9},{9,8},{10,11... | collective-permute-start | bytes 12296 | tf_op jit(solution)/shard_map/ppermute | solution.py:392

commit v3 on v2

--- a/solution.py
+++ b/solution.py
@@ -72,13 +72,35 @@
         rows(HALF, lambda r: 7 - r)
 
 
-def prepare_kernel(inc_hbm, lon_hbm, lat_hbm, prec_ref, own_ref, field_ref, coef_ref, prec_out, inc, lon, lat, sems):
-    core = lax.axis_index("ens")
-    lons = inc.shape[-1]
-    levels = inc.shape[0]
+def own_kernel(inc_ref, own_ref, field_ref):
+    core = lax.axis_index("ens")
+    lons = inc_ref.shape[-1]
+
+    def rows(at):
+        for r in range(12):
+            field_ref[r, :, 0:lons] = inc_ref[0, :, at(r), :]
+            wrap(field_ref.at[r], lons)
+            if r < HALF:
+                own_ref[r] = field_ref[r]
+
+    @pl.when(core == 0)
+    def _():
+        rows(lambda r: r)
+
+    @pl.when(core == 1)
+    def _():
+        rows(lambda r: 15 - r)
+
+
+def prepare_kernel(
+    lon_hbm, lat_hbm, prec_ref, rows_ref, counts_ref, oprec_ref, coef_ref, prec_out, weight_ref, lon, lat, sems
+):
+    core = lax.axis_index("ens")
+    lons = lon.shape[-1]
+    levels = lon.shape[0]
     copies = [
         fetch(source, 0, 2 * HALF, target, sems.at[i])
-        for i, (source, target) in enumerate(((inc_hbm, inc), (lon_hbm, lon), (lat_hbm, lat)))
+        for i, (source, target) in enumerate(((lon_hbm, lon), (lat_hbm, lat)))
     ]
     for copy in copies:
         copy.start()
@@ -87,15 +109,14 @@
     for k in range(levels):
         prec = jnp.where(level == k, prec_ref[k], prec)
     prec_out[...] = prec
+    slot = lax.broadcasted_iota(jnp.int32, weight_ref.shape, 0)
+    mine = (rows_ref[...] % 16) // HALF == core
+    weight_ref[...] = jnp.where((slot < counts_ref[...]) & mine, oprec_ref[...], 0.0)
     for copy in copies:
         copy.wait()
 
     def rows(at, sign):
         for r in range(12):
-            field_ref[r, :, 0:lons] = inc[:, at(r), :]
-            wrap(field_ref.at[r], lons)
-            if r < HALF:
-                own_ref[r] = field_ref[r]
             coef_ref[1, r, :, 0:lons] = lon[:, at(r), :]
             wrap(coef_ref.at[1, r], lons)
             coef_ref[4, r, :, 0:lons] = sign * lat[:, at(r), :]
@@ -130,7 +151,7 @@
 
 
 def forward_kernel(
-    field_ref, coef_ref, prec_ref, halo_ref, next_ref, jac_hbm, rows_hbm, rows_ref, counts_ref, val_ref, oprec_ref,
+    field_ref, coef_ref, prec_ref, halo_ref, next_ref, jac_hbm, rows_hbm, val_ref, weight_ref,
     later_ref, adj_ref, outer_ref, inner_ref, edge_ref, x0, x1, pk, wgt, jac, rows, sems,
 ):
     core = lax.axis_index("ens")
@@ -175,14 +196,11 @@
         row, lev = place(j)
         pk[pl.ds(j, 1), :] = field[4 + row, lev, :]
     lane = lax.broadcasted_iota(jnp.int32, (slots, blocks), 1)
-    slot = lax.broadcasted_iota(jnp.int32, (slots, blocks), 0)
     ev = jnp.zeros((slots, blocks), jnp.float32)
     for j in range(blocks):
         total = jnp.sum(jac[j] * pk[pl.ds(j, 1), 0:lons], axis=1, keepdims=True)
         ev = jnp.where(lane == j, total, ev)
-    mine = (rows_ref[...] % 16) // HALF == core
-    used = (slot < counts_ref[...]) & mine
-    wgt[...] = jnp.where(used, oprec_ref[...] * (ev - val_ref[...]), 0.0)
+    wgt[...] = weight_ref[...] * (ev - val_ref[...])
     for j in range(blocks):
         w = jnp.sum(jnp.where(lane == j, wgt[...], 0.0), axis=1, keepdims=True)
         pk[pl.ds(j, 1), 0:lons] = jnp.sum(jac[j] * w, axis=0, keepdims=True)
@@ -233,12 +251,15 @@
             forcing_ref[:, 7 - r, :] = total[r, :, 0:lons]
 
 
-def product_kernel(pieces_ref, own_ref, other_ref, start_ref, mismatch_ref, inc_ref, prec_ref, out_ref, grad_ref):
-    core = lax.axis_index("ens")
+def mismatch_kernel(start_ref, mismatch_ref, inc_ref, prec_ref, grad_ref):
     first_window = lax.axis_index(TM) == 0
     prec = prec_ref[...]
     for r in range(HALF):
         grad_ref[r] = start_ref[r] + jnp.where(first_window, prec * inc_ref[r], mismatch_ref[r])
+
+
+def product_kernel(pieces_ref, own_ref, other_ref, out_ref):
+    core = lax.axis_index("ens")
     forcing = jnp.sum(pieces_ref[...], axis=0)
     lane = lax.broadcasted_iota(jnp.int32, (HALF, LANES), 1)
     members = own_ref.shape[0]
@@ -295,12 +316,15 @@
 
 VMEM = pl.BlockSpec(memory_space=pltpu.VMEM)
 SMEM = pl.BlockSpec(memory_space=pltpu.SMEM)
-ANY = pl.BlockSpec(memory_space=pl.ANY)
 HBM = pl.BlockSpec(memory_space=pltpu.HBM)
 
 
 def buf(*shape):
     return pltpu.VMEM(shape, jnp.float32)
+
+
+def in_hbm(value):
+    return pltpu.with_memory_space_constraint(value, pltpu.HBM)
 
 
 def call(kernel, ins, outs, scratch=(), limit=40):
@@ -310,7 +334,7 @@
         in_specs=ins,
         out_specs=[VMEM] * len(outs),
         scratch_shapes=list(scratch),
-        compiler_params=pltpu.CompilerParams(vmem_limit_bytes=limit * 2**20),
+        compiler_params=pltpu.CompilerParams(vmem_limit_bytes=int(limit * 2**20)),
     )
 
 
@@ -345,29 +369,27 @@
 
     (outgoing,) = call(
         edge_kernel, [HBM] * 3, [(10, levels, wide)], [piece, piece, piece, pltpu.SemaphoreType.DMA((3,))]
-    )(*fields)
+    )(*(in_hbm(field) for field in fields))
     halo = lax.ppermute(outgoing, band, trade)
-    own_rows, field, coefs, prec = call(
+    own_rows, field = call(own_kernel, [VMEM], [own, (12, levels, wide)])(increment)
+    next_rows = lax.ppermute(own_rows, TM, [(i + 1, i) for i in range(count_t - 1)])
+    coefs, prec, weight = call(
         prepare_kernel,
-        [ANY] * 3 + [SMEM],
-        [own, (12, levels, wide), (5, 12, levels, wide), (levels, wide)],
-        [whole, whole, whole, pltpu.SemaphoreType.DMA((3,))],
-    )(*fields, model_precision)
-    next_rows = lax.ppermute(own_rows, TM, [(i + 1, i) for i in range(count_t - 1)])
+        [HBM] * 2 + [SMEM] + [VMEM] * 3,
+        [(5, 12, levels, wide), (levels, wide), (slots, blocks)],
+        [whole, whole, pltpu.SemaphoreType.DMA((2,))],
+    )(in_hbm(wind_lon), in_hbm(wind_lat), model_precision, obs_rows, obs_counts, obs_precision[0].T)
     other_pert = lax.ppermute(perturbations, "ens", partner)
 
     later, adj, outer, inner, edges = call(
         forward_kernel,
-        [VMEM] * 5 + [ANY, ANY] + [VMEM] * 4,
+        [VMEM] * 5 + [HBM, HBM] + [VMEM] * 2,
         [own, own, quarter, quarter, (5, 4, levels, wide)],
         [
             buf(16, levels, wide), buf(16, levels, wide), buf(blocks, wide), buf(slots, blocks),
             buf(blocks, slots, lons), pltpu.SMEM((1, blocks), jnp.int32), pltpu.SemaphoreType.DMA((2,)),
         ],
-    )(
-        field, coefs, prec, halo, next_rows, obs_jacobian, obs_rows, obs_rows, obs_counts,
-        obs_values[0].T, obs_precision[0].T,
-    )
+    )(field, coefs, prec, halo, next_rows, in_hbm(obs_jacobian), in_hbm(obs_rows), obs_values[0].T, weight)
     outer = lax.ppermute(outer, band, trade)
     inner = lax.ppermute(inner, "ens", partner)
     mismatch = lax.ppermute(later, TM, [(i, i + 1) for i in range(count_t - 1)])
@@ -378,12 +400,13 @@
         [(levels, HALF, lons), own],
         [buf(16, levels, wide), buf(16, levels, wide), buf(*own)],
     )(adj, outer, inner, edges, coefs)
-    forcing, mismatch = lax.optimization_barrier((forcing, mismatch))
     pieces = lax.all_to_all(forcing, TM, 0, 0, tiled=True)
 
-    products, own_grad = call(product_kernel, [VMEM] * 7, [(count_t * count_l, 1, LANES), own])(
-        pieces, perturbations, other_pert, start, mismatch, own_rows, prec
-    )
+    (products,) = call(product_kernel, [VMEM] * 3, [(count_t * count_l, 1, LANES)])(
+        pieces, perturbations, other_pert
+    )
+    start, mismatch, products = lax.optimization_barrier((start, mismatch, products))
+    (own_grad,) = call(mismatch_kernel, [VMEM] * 4, [own])(start, mismatch, own_rows, prec)
     other_grad = lax.ppermute(own_grad, "ens", partner)
     sums = lax.all_to_all(products, TM_LAT, 0, 0, tiled=True)
     (grad_state,) = call(gradient_kernel, [VMEM] * 2, [(1, levels, band_rows, lons)])(own_grad, other_grad)

time: 93.5 us -> 83.4 us (0.89)
  waiting for transfers between devices: 15.2 us -> 9.5 us
  local copies, waits for them, and re-layouts: 4.72 us -> 0.03 us
  blocking collectives: 44.4 us -> 42.8 us
  Pallas kernels: 10.1 us -> 11.5 us
    unnamed x20 -> x14, local copies, waits for them, and re-layouts: 4.72 us -> 0.03 us
    ppermute x1, waiting for transfers between devices: 4.6 us -> 1.47 us  [on_device(): outer = lax.ppermute(outer, band, trade)]
    all_to_all x1, blocking collectives: 27.9 us -> 25 us  [on_device(): sums = lax.all_to_all(products, TM_LAT, 0, 0, tiled=True)]
    ppermute x1, waiting for transfers between devices: 9.72 us -> 7.19 us  [on_device(): lax.ppermute(own_rows, TM, [(i + 1, i) for i in range(count_t - 1)])]
    ppermute x1, starting transfers between devices: 1.66 us -> 3.12 us  [on_device(): mismatch = lax.ppermute(later, TM, [(i, i + 1) for i in range(count_t - 1)])]
    all_to_all x1, blocking collectives: 16.5 us -> 17.9 us  [on_device(): pieces = lax.all_to_all(forcing, TM, 0, 0, tiled=True)]
    ppermute x1, starting transfers between devices: 6.92 us -> 5.88 us  [on_device(): outer = lax.ppermute(outer, band, trade)]
    pallas_call x3 -> x5, Pallas kernels: 5.66 us -> 6.44 us  [the longest x1 3.41 us: on_device(): call(forward_kernel, [VMEM] * 5 + [HBM, HBM] + [VMEM] * 2, [own, own, qua...]
  transfers between devices with their start and end apart: 8 -> 8, of which waited for: 3 -> 3; matrix products, arithmetic and copies ran while one was open for 0% -> 0% of each run, Pallas kernels for 9% -> 12%
where the time goes in v3:
time: 83.4 us; the launch traced here: 83.1 us
  blocking collectives  42.8 us (51%)
  starting transfers between devices  18.4 us (22%)
  Pallas kernels  11.5 us (14%)
  waiting for transfers between devices  9.5 us (11%)
    all_to_all x1, blocking collectives, on_device(): sums = lax.all_to_all(products, TM_LAT, 0, 0, tiled=True)  25 us
    all_to_all x1, blocking collectives, on_device(): pieces = lax.all_to_all(forcing, TM, 0, 0, tiled=True)  17.9 us
    ppermute x1, waiting for transfers between devices, on_device(): lax.ppermute(own_rows, TM, [(i + 1, i) for i in range(count_t - 1)])  7.19 us
    ppermute x1, starting transfers between devices, on_device(): outer = lax.ppermute(outer, band, trade)  5.88 us
    pallas_call x1, Pallas kernels, on_device(): call(forward_kernel, [VMEM] * 5 + [HBM, HBM] + [VMEM] * 2, [own, own, qua...  3.41 us
    ppermute x1, starting transfers between devices, on_device(): other_pert = lax.ppermute(perturbations, 'ens', partner)  3.29 us
    ppermute x1, starting transfers between devices, on_device(): mismatch = lax.ppermute(later, TM, [(i, i + 1) for i in range(count_t - 1)])  3.12 us
    ppermute x1, starting transfers between devices, on_device(): halo = lax.ppermute(outgoing, band, trade)  3 us
  transfers between devices with their start and end apart: 8, of which 3 were waited for; matrix products, arithmetic and copies ran while one was open for 0% of the time, Pallas kernels for 12%

profile of v3, /device:TPU:1, one launch (start us, length us, event | category | flops | bytes accessed | tf_op | source)
XLA Modules:
  0.0 83.1 jit_solution(1956148130664775039)
XLA Ops:
  0.6 0.0 copy-start.1
  0.6 0.0 copy-start.2
  0.7 0.0 copy-start.4
  0.7 3.3 %collective-permute-start.5 = (f32[16,1,16,1440]{3,2,1,0:T(8,128)}, f32[16,1,16,1440]{3,2,1,0:T(8,128)S(1)}, u32[]{:S(2)}, u32[]{:S(2)}) collective-permute-start(f32[16,1,16,1440]{3,2,1,0:T(8,128)} %own_ref.3), channel_id=1, source_target_pairs={{0,1},{1,0},{2,3},{3,2},{4,5},{5,4},{6,7},{7,6},{8,9},{9,8},{10,11... | collective-permute-start | bytes 4423688 | tf_op jit(solution)/shard_map/ppermute | solution.py:382
  4.0 1.4 %shard_map.115 = f32[10,8,1536]{2,1,0:T(8,128)S(1)} custom-call(f32[1,8,16,1440]{3,2,1,0:T(8,128)} %inc_hbm.1, f32[1,8,16,1440]{3,2,1,0:T(8,128)} %lon_hbm.3, f32[1,8,16,1440]{3,2,1,0:T(8,128)} %lat_hbm.3), custom_call_target="tpu_custom_call" | custom-call | tf_op jit(solution)/shard_map/pallas_call | solution.py:370
  5.4 3.0 %collective-permute-start = (f32[10,8,1536]{2,1,0:T(8,128)S(1)}, f32[10,8,1536]{2,1,0:T(8,128)S(1)}, u32[]{:S(2)}, u32[]{:S(2)}) collective-permute-start(f32[10,8,1536]{2,1,0:T(8,128)S(1)} %shard_map.115), channel_id=1, source_target_pairs={{1,2},{2,1},{3,4},{4,3},{5,6},{6,5},{7,8},{8,7},{9,10},{10,9},{11,... | collective-permute-start | bytes 1474568 | tf_op jit(solution)/shard_map/ppermute | solution.py:373
  8.4 0.2 shard_map.113
  8.6 1.3 %collective-permute-start.1 = (f32[8,8,1536]{2,1,0:T(8,128)S(1)}, f32[8,8,1536]{2,1,0:T(8,128)S(1)}, u32[]{:S(2)}, u32[]{:S(2)}) collective-permute-start(f32[8,8,1536]{2,1,0:T(8,128)S(1)} %get-tuple-element.20.inc_ref), channel_id=1, source_target_pairs={{32,0},{64,32},{96,64},{128,96},{160,128},{192,160},{224,192},{33,... | collective-permute-start | bytes 1179656 | tf_op jit(solution)/shard_map/ppermute | solution.py:375
  9.9 2.5 %shard_map.114 = (f32[5,12,8,1536]{3,2,1,0:T(8,128)S(1)}, f32[8,1536]{1,0:T(8,128)S(1)}, f32[16,32]{1,0:T(8,128)S(1)}) custom-call(f32[1,8,16,1440]{3,2,1,0:T(8,128)} %lon_hbm.3, f32[1,8,16,1440]{3,2,1,0:T(8,128)} %lat_hbm.3, f32[8]{0:T(128)S(1)} %copy-done.5, s32[1,32]{1,0:T(1,128)S(1)} %copy-done.4, s32[1,32]{1,0:T(1,128)S(1)} %copy-done.6, ...), custom_call_target="tpu_custom_call" | custom-call | tf_op jit(solution)/shard_map/pallas_call | solution.py:376
  12.4 7.2 %collective-permute-done.1.next_ref = f32[8,8,1536]{2,1,0:T(8,128)S(1)} collective-permute-done((f32[8,8,1536]{2,1,0:T(8,128)S(1)}, f32[8,8,1536]{2,1,0:T(8,128)S(1)}, u32[]{:S(2)}, u32[]{:S(2)}) %collective-permute-start.1) | collective-permute-done | bytes 393248 | tf_op jit(solution)/shard_map/ppermute | solution.py:375
  19.6 0.0 collective-permute-done.halo_ref
  19.6 3.4 %shard_map.116 = (f32[8,8,1536]{2,1,0:T(8,128)S(1)}, f32[8,8,1536]{2,1,0:T(8,128)S(1)}, f32[4,8,1536]{2,1,0:T(8,128)S(1)}, f32[4,8,1536]{2,1,0:T(8,128)S(1)}, f32[5,4,8,1536]{3,2,1,0:T(8,128)S(1)}) custom-call(f32[12,8,1536]{2,1,0:T(8,128)S(1)} %get-tuple-element.17.field_ref, f32[5,12,8,1536]{3,2,1,0:T(8,128)S(1)} %get-tuple-element.18.coef_ref, ...), custom_call_target="tpu_custom_call" | custom-call | tf_op jit(solution)/shard_map/pallas_call | solution.py:384
  23.1 0.0 copy-start
  23.1 5.9 %collective-permute-start.2 = (f32[4,8,1536]{2,1,0:T(8,128)S(1)}, f32[4,8,1536]{2,1,0:T(8,128)S(1)}, u32[]{:S(2)}, u32[]{:S(2)}) collective-permute-start(f32[4,8,1536]{2,1,0:T(8,128)S(1)} %get-tuple-element.23), channel_id=1, source_target_pairs={{1,2},{2,1},{3,4},{4,3},{5,6},{6,5},{7,8},{8,7},{9,10},{10,9},{11,... | collective-permute-start | bytes 589832 | tf_op jit(solution)/shard_map/ppermute | solution.py:393
  29.0 0.1 collective-permute-start.3
  29.1 3.1 %collective-permute-start.4 = (f32[8,8,1536]{2,1,0:T(8,128)S(1)}, f32[8,8,1536]{2,1,0:T(8,128)S(1)}, u32[]{:S(2)}, u32[]{:S(2)}) collective-permute-start(f32[8,8,1536]{2,1,0:T(8,128)S(1)} %get-tuple-element.27), channel_id=1, source_target_pairs={{0,32},{32,64},{64,96},{96,128},{128,160},{160,192},{192,224},{1,3... | collective-permute-start | bytes 1179656 | tf_op jit(solution)/shard_map/ppermute | solution.py:395
  32.2 1.5 %collective-permute-done.2.outer_ref = f32[4,8,1536]{2,1,0:T(8,128)S(1)} collective-permute-done((f32[4,8,1536]{2,1,0:T(8,128)S(1)}, f32[4,8,1536]{2,1,0:T(8,128)S(1)}, u32[]{:S(2)}, u32[]{:S(2)}) %collective-permute-start.2) | collective-permute-done | bytes 196640 | tf_op jit(solution)/shard_map/ppermute | solution.py:393
  33.7 0.0 collective-permute-done.3.inner_ref
  33.7 1.5 %shard_map.117 = (f32[8,8,1440]{2,1,0:T(8,128)S(1)}, f32[8,8,1536]{2,1,0:T(8,128)S(1)}) custom-call(f32[8,8,1536]{2,1,0:T(8,128)S(1)} %get-tuple-element.22.adj_ref, f32[4,8,1536]{2,1,0:T(8,128)S(1)} %collective-permute-done.2.outer_ref, f32[4,8,1536]{2,1,0:T(8,128)S(1)} %collective-permute-done.3.inner_ref, ...), custom_call_target="tpu_custom_call" | custom-call | tf_op jit(solution)/shard_map/pallas_call | solution.py:397
  35.2 17.9 %all_to_all.10.pieces_ref = f32[8,8,1440]{2,1,0:T(8,128)S(1)} all-to-all(f32[8,8,1440]{2,1,0:T(8,128)S(1)} %get-tuple-element.28), channel_id=1, replica_groups=mesh['tm_0'=2,'tm_1'=4,'lat_0'=8,'lat_1'=2,'ens'=2] {'tm_0','tm_1'}, dimensions={0} | all-to-all | bytes 737280 | tf_op jit(solution)/shard_map/all_to_all | solution.py:403
  53.0 0.0 collective-permute-done.5.other_ref
  53.0 0.2 shard_map.118
  53.3 0.0 collective-permute-done.4.mismatch_ref
  53.3 0.1 shard_map.119.own_ref
  53.4 0.1 collective-permute-start.6
  53.5 25.0 %all_to_all.11.sums_ref = f32[128,1,128]{2,1,0:T(1,128)S(1)} all-to-all(f32[128,1,128]{2,1,0:T(1,128)S(1)} %shard_map.118), channel_id=1, replica_groups=mesh['tm_0'=2,'tm_1'=4,'lat_0'=8,'lat_1'=2,'ens'=2] {'tm_0','tm_1','lat_..., dimensions={0} | all-to-all | bytes 131072 | tf_op jit(solution)/shard_map/all_to_all | solution.py:411
  78.4 0.1 shard_map.121.sum_ref
  78.6 1.6 %collective-permute-start.7 = (f32[8,128]{1,0:T(8,128)S(1)}, f32[8,128]{1,0:T(8,128)S(1)}, u32[]{:S(2)}, u32[]{:S(2)}) collective-permute-start(f32[8,128]{1,0:T(8,128)S(1)} %shard_map.121.sum_ref), channel_id=1, source_target_pairs={{0,1},{1,0},{2,3},{3,2},{4,5},{5,4},{6,7},{7,6},{8,9},{9,8},{10,11... | collective-permute-start | bytes 12296 | tf_op jit(solution)/shard_map/ppermute | solution.py:415
  80.2 0.8 collective-permute-done.7.other_sum_ref
  81.0 1.0 %shard_map.122 = f32[1,16,1440]{2,1,0:T(8,128)} custom-call(f32[8,128]{1,0:T(8,128)S(1)} %shard_map.121.sum_ref, f32[8,128]{1,0:T(8,128)S(1)} %collective-permute-done.7.other_sum_ref, f32[16,1,16,1440]{3,2,1,0:T(8,128)S(1)} %copy-done, f32[16,1,16,1440]{3,2,1,0:T(8,128)S(1)} %collective-permute-done.5.other_ref), custom_call_target="tpu_custom_call" | custom-call | tf_op jit(solution)/shard_map/pallas_call | solution.py:416
  82.0 0.0 collective-permute-done.6.other_ref
  82.0 1.1 %shard_map.120 = f32[1,8,16,1440]{3,2,1,0:T(8,128)} custom-call(f32[8,8,1536]{2,1,0:T(8,128)S(1)} %shard_map.119.own_ref, f32[8,8,1536]{2,1,0:T(8,128)S(1)} %collective-permute-done.6.other_ref), custom_call_target="tpu_custom_call" | custom-call | tf_op jit(solution)/shard_map/pallas_call | solution.py:412
  (10 shorter events, 0.0 us)
Async XLA Ops:
  0.6 7.7 %copy-start.1 = (f32[1,8,16,1440]{3,2,1,0:T(8,128)S(1)}, f32[1,8,16,1440]{3,2,1,0:T(8,128)}, u32[]{:S(2)}) copy-start(f32[1,8,16,1440]{3,2,1,0:T(8,128)} %inc_hbm.1) | copy-start | bytes 2211844
  0.6 9.2 %copy-start.2 = (f32[1,32,16]{1,2,0:T(8,128)S(1)}, f32[1,32,16]{1,2,0:T(8,128)}, u32[]{:S(2)}) copy-start(f32[1,32,16]{1,2,0:T(8,128)} %param.18) | copy-start | bytes 6148
  0.7 9.2 %copy-start.5 = (f32[8]{0:T(128)S(1)}, f32[8]{0:T(128)}, u32[]{:S(2)}) copy-start(f32[8]{0:T(128)} %prec_ref.1) | copy-start | bytes 100
  0.7 9.2 %copy-start.4 = (s32[1,32]{1,0:T(1,128)S(1)}, s32[1,32]{1,0:T(1,128)}, u32[]{:S(2)}) copy-start(s32[1,32]{1,0:T(1,128)} %rows_hbm.1) | copy-start | bytes 388
  0.7 9.2 %copy-start.6 = (s32[1,32]{1,0:T(1,128)S(1)}, s32[1,32]{1,0:T(1,128)}, u32[]{:S(2)}) copy-start(s32[1,32]{1,0:T(1,128)} %counts_ref.1) | copy-start | bytes 388
  0.7 19.0 %copy-start.3 = (f32[1,32,16]{1,2,0:T(8,128)S(1)}, f32[1,32,16]{1,2,0:T(8,128)}, u32[]{:S(2)}) copy-start(f32[1,32,16]{1,2,0:T(8,128)} %param.17) | copy-start | bytes 6148
  0.7 52.4 %collective-permute-start.5 = (f32[16,1,16,1440]{3,2,1,0:T(8,128)}, f32[16,1,16,1440]{3,2,1,0:T(8,128)S(1)}, u32[]{:S(2)}, u32[]{:S(2)}) collective-permute-start(f32[16,1,16,1440]{3,2,1,0:T(8,128)} %own_ref.3), channel_id=1, source_target_pairs={{0,1},{1,0},{2,3},{3,2},{4,5},{5,4},{6,7},{7,6},{8,9},{9,8},{10,11... | collective-permute-start | bytes 4423688 | tf_op jit(solution)/shard_map/ppermute | solution.py:382
  5.4 14.3 %collective-permute-start = (f32[10,8,1536]{2,1,0:T(8,128)S(1)}, f32[10,8,1536]{2,1,0:T(8,128)S(1)}, u32[]{:S(2)}, u32[]{:S(2)}) collective-permute-start(f32[10,8,1536]{2,1,0:T(8,128)S(1)} %shard_map.115), channel_id=1, source_target_pairs={{1,2},{2,1},{3,4},{4,3},{5,6},{6,5},{7,8},{8,7},{9,10},{10,9},{11,... | collective-permute-start | bytes 1474568 | tf_op jit(solution)/shard_map/ppermute | solution.py:373
  8.6 11.1 %collective-permute-start.1 = (f32[8,8,1536]{2,1,0:T(8,128)S(1)}, f32[8,8,1536]{2,1,0:T(8,128)S(1)}, u32[]{:S(2)}, u32[]{:S(2)}) collective-permute-start(f32[8,8,1536]{2,1,0:T(8,128)S(1)} %get-tuple-element.20.inc_ref), channel_id=1, source_target_pairs={{32,0},{64,32},{96,64},{128,96},{160,128},{192,160},{224,192},{33,... | collective-permute-start | bytes 1179656 | tf_op jit(solution)/shard_map/ppermute | solution.py:375
  23.1 30.0 %copy-start = (f32[16,1,16,1440]{3,2,1,0:T(8,128)S(1)}, f32[16,1,16,1440]{3,2,1,0:T(8,128)}, u32[]{:S(2)}) copy-start(f32[16,1,16,1440]{3,2,1,0:T(8,128)} %own_ref.3) | copy-start | bytes 4423684
  23.1 10.6 %collective-permute-start.2 = (f32[4,8,1536]{2,1,0:T(8,128)S(1)}, f32[4,8,1536]{2,1,0:T(8,128)S(1)}, u32[]{:S(2)}, u32[]{:S(2)}) collective-permute-start(f32[4,8,1536]{2,1,0:T(8,128)S(1)} %get-tuple-element.23), channel_id=1, source_target_pairs={{1,2},{2,1},{3,4},{4,3},{5,6},{6,5},{7,8},{8,7},{9,10},{10,9},{11,... | collective-permute-start | bytes 589832 | tf_op jit(solution)/shard_map/ppermute | solution.py:393
  29.0 4.7 %collective-permute-start.3 = (f32[4,8,1536]{2,1,0:T(8,128)S(1)}, f32[4,8,1536]{2,1,0:T(8,128)S(1)}, u32[]{:S(2)}, u32[]{:S(2)}) collective-permute-start(f32[4,8,1536]{2,1,0:T(8,128)S(1)} %get-tuple-element.24), channel_id=1, source_target_pairs={{0,1},{1,0},{2,3},{3,2},{4,5},{5,4},{6,7},{7,6},{8,9},{9,8},{10,11... | collective-permute-start | bytes 589832 | tf_op jit(solution)/shard_map/ppermute | solution.py:394
  29.1 24.2 %collective-permute-start.4 = (f32[8,8,1536]{2,1,0:T(8,128)S(1)}, f32[8,8,1536]{2,1,0:T(8,128)S(1)}, u32[]{:S(2)}, u32[]{:S(2)}) collective-permute-start(f32[8,8,1536]{2,1,0:T(8,128)S(1)} %get-tuple-element.27), channel_id=1, source_target_pairs={{0,32},{32,64},{64,96},{96,128},{128,160},{160,192},{192,224},{1,3... | collective-permute-start | bytes 1179656 | tf_op jit(solution)/shard_map/ppermute | solution.py:395
  53.4 28.6 %collective-permute-start.6 = (f32[8,8,1536]{2,1,0:T(8,128)S(1)}, f32[8,8,1536]{2,1,0:T(8,128)S(1)}, u32[]{:S(2)}, u32[]{:S(2)}) collective-permute-start(f32[8,8,1536]{2,1,0:T(8,128)S(1)} %shard_map.119.own_ref), channel_id=1, source_target_pairs={{0,1},{1,0},{2,3},{3,2},{4,5},{5,4},{6,7},{7,6},{8,9},{9,8},{10,11... | collective-permute-start | bytes 1179656 | tf_op jit(solution)/shard_map/ppermute | solution.py:410
  78.6 2.4 %collective-permute-start.7 = (f32[8,128]{1,0:T(8,128)S(1)}, f32[8,128]{1,0:T(8,128)S(1)}, u32[]{:S(2)}, u32[]{:S(2)}) collective-permute-start(f32[8,128]{1,0:T(8,128)S(1)} %shard_map.121.sum_ref), channel_id=1, source_target_pairs={{0,1},{1,0},{2,3},{3,2},{4,5},{5,4},{6,7},{7,6},{8,9},{9,8},{10,11... | collective-permute-start | bytes 12296 | tf_op jit(solution)/shard_map/ppermute | solution.py:415

commit v4 on v3

--- a/solution.py
+++ b/solution.py
@@ -92,8 +92,57 @@
         rows(lambda r: 15 - r)
 
 
+class Rows:
+    def __init__(self, halo_ref, own_ref, at):
+        self.halo, self.own, self.at = halo_ref, own_ref, at
+
+    def __getitem__(self, j):
+        return self.halo[self.at, j] if j < 4 else self.own[self.at, j - 4]
+
+
+def forward_step(src, dst, coefs, first, last):
+    center, plon, mlon, plat, mlat = coefs
+    for j in range(first, last):
+        f = src[j]
+        dst[j] = center[j] * f + plon[j] * east(f) + mlon[j] * west(f) + plat[j] * src[j + 1] + mlat[j] * src[j - 1]
+
+
+def adjoint_step(src, dst, coefs, first, last):
+    center, plon, mlon, plat, mlat = coefs
+    for j in range(first, last):
+        g = src[j]
+        dst[j] = (
+            center[j] * g
+            + west(plon[j] * g)
+            + east(mlon[j] * g)
+            + plat[j - 1] * src[j - 1]
+            + mlat[j + 1] * src[j + 1]
+        )
+
+
+def inner_steps(step_of, bufs, coefs, joint_ref, done):
+    for s in range(1, STEPS + 1):
+        src, dst = bufs[(s - 1) % 2], bufs[s % 2]
+        step_of(src, dst, coefs, 4 + s, 16 - s)
+        if s < STEPS:
+            joint_ref[s - 1, 0] = dst[4 + s]
+            joint_ref[s - 1, 1] = dst[5 + s]
+        done(s, dst)
+
+
+def outer_steps(step_of, bufs, coefs, joint_ref, done):
+    for s in range(1, STEPS + 1):
+        src, dst = bufs[(s - 1) % 2], bufs[s % 2]
+        step_of(src, dst, coefs, s, 4 + s)
+        if s < STEPS:
+            dst[4 + s] = joint_ref[s - 1, 0]
+            dst[5 + s] = joint_ref[s - 1, 1]
+        done(s, dst)
+
+
 def prepare_kernel(
-    lon_hbm, lat_hbm, prec_ref, rows_ref, counts_ref, oprec_ref, coef_ref, prec_out, weight_ref, lon, lat, sems
+    lon_hbm, lat_hbm, field_ref, prec_ref, rows_ref, counts_ref, oprec_ref,
+    coef_ref, prec_out, weight_ref, joint_ref, end_ref, lon, lat, x0, x1, sems,
 ):
     core = lax.axis_index("ens")
     lons = lon.shape[-1]
@@ -131,6 +180,15 @@
     def _():
         rows(lambda r: 15 - r, -1.0)
 
+    x0[4:16] = field_ref[...]
+    coefs = [Rows(None, coef_ref, i) for i in range(5)]
+
+    def done(step, dst):
+        if step == STEPS:
+            end_ref[...] = dst[8:12]
+
+    inner_steps(forward_step, (x0, x1), coefs, joint_ref, done)
+
 
 def store_coefficients(coef_ref, at, c, e):
     cc = c * c
@@ -142,46 +200,30 @@
     coef_ref[4, at] = 0.5 * (ee + e)
 
 
-class Rows:
-    def __init__(self, halo_ref, own_ref, at):
-        self.halo, self.own, self.at = halo_ref, own_ref, at
-
-    def __getitem__(self, j):
-        return self.halo[self.at, j] if j < 4 else self.own[self.at, j - 4]
-
-
 def forward_kernel(
-    field_ref, coef_ref, prec_ref, halo_ref, next_ref, jac_hbm, rows_hbm, val_ref, weight_ref,
-    later_ref, adj_ref, outer_ref, inner_ref, edge_ref, x0, x1, pk, wgt, jac, rows, sems,
+    field_ref, coef_ref, joint_ref, far_ref, halo_ref, jac_hbm, rows_hbm, val_ref, weight_ref,
+    end_ref, force_ref, edge_ref, x0, x1, pk, wgt, jac, rows, sems,
 ):
     core = lax.axis_index("ens")
-    has_next = (lax.axis_index(TM) < lax.axis_size(TM) - 1).astype(jnp.float32)
     blocks, slots, lons = jac.shape
     jac_copy = pltpu.make_async_copy(jac_hbm.at[0], jac, sems.at[0])
     rows_copy = pltpu.make_async_copy(rows_hbm, rows, sems.at[1])
     jac_copy.start()
     rows_copy.start()
     x0[0:4] = halo_ref[0:4]
-    x0[4:16] = field_ref[...]
-    center, plon, mlon, plat, mlat = (Rows(edge_ref, coef_ref, i) for i in range(5))
+    x0[4:6] = field_ref[0:2]
     edge_ref[3, 0] = jnp.ones(x0.shape[1:], jnp.float32)
     for r in range(3):
         store_coefficients(edge_ref, 1 + r, halo_ref[4 + r], halo_ref[7 + r])
-
-    bufs = (x0, x1)
-    for step in range(STEPS):
-        src, dst = bufs[step % 2], bufs[(step + 1) % 2]
-        for j in range(step + 1, 15 - step):
-            f = src[j]
-            dst[j] = (
-                center[j] * f + plon[j] * east(f) + mlon[j] * west(f) + plat[j] * src[j + 1] + mlat[j] * src[j - 1]
-            )
-    field = bufs[STEPS % 2]
-    prec = prec_ref[...] * has_next
-    for r in range(HALF):
-        later = prec * (next_ref[r] - field[4 + r])
-        later_ref[r] = later
-        adj_ref[r] = -later
+    coefs = [Rows(edge_ref, coef_ref, i) for i in range(5)]
+
+    def done(step, dst):
+        if step == STEPS:
+            end_ref[0:4] = dst[4:8]
+
+    outer_steps(forward_step, (x0, x1), coefs, joint_ref, done)
+    end_ref[4:8] = far_ref[...]
+    force_ref[...] = jnp.zeros(force_ref.shape, jnp.float32)
 
     rows_copy.wait()
     jac_copy.wait()
@@ -194,7 +236,7 @@
 
     for j in range(blocks):
         row, lev = place(j)
-        pk[pl.ds(j, 1), :] = field[4 + row, lev, :]
+        pk[pl.ds(j, 1), :] = end_ref[row, lev, :]
     lane = lax.broadcasted_iota(jnp.int32, (slots, blocks), 1)
     ev = jnp.zeros((slots, blocks), jnp.float32)
     for j in range(blocks):
@@ -207,48 +249,68 @@
     wrap(pk, lons)
     for j in range(blocks):
         row, lev = place(j)
-        adj_ref[row, lev, :] = adj_ref[row, lev, :] + pk[pl.ds(j, 1), :]
-
+        force_ref[row, lev, :] = force_ref[row, lev, :] + pk[pl.ds(j, 1), :]
+
+
+def seed_kernel(force_ref, end_ref, next_ref, prec_ref, coef_ref, later_ref, adj_ref, outer_ref, inner_ref):
+    has_next = (lax.axis_index(TM) < lax.axis_size(TM) - 1).astype(jnp.float32)
+    prec = prec_ref[...] * has_next
+    for r in range(HALF):
+        later = prec * (next_ref[r] - end_ref[r])
+        later_ref[r] = later
+        adj_ref[r] = force_ref[r] - later
     for q in range(4):
-        outer_ref[q] = adj_ref[3 - q] * mlat[7] if q == 0 else adj_ref[3 - q]
+        outer_ref[q] = adj_ref[3 - q] * coef_ref[4, 3] if q == 0 else adj_ref[3 - q]
         inner_ref[q] = adj_ref[7 - q]
 
 
-def adjoint_kernel(adj_ref, outer_ref, inner_ref, edge_ref, coef_ref, forcing_ref, start_ref, g0, g1, total):
-    core = lax.axis_index("ens")
-    lons = forcing_ref.shape[-1]
-    center, plon, mlon, plat, mlat = (Rows(edge_ref, coef_ref, i) for i in range(5))
-    g0[0:4] = outer_ref[...]
+def adjoint_inner_kernel(adj_ref, inner_ref, coef_ref, joint_ref, far_ref, total_ref, g0, g1):
     g0[4:12] = adj_ref[...]
     g0[12:16] = inner_ref[...]
-    bufs = (g0, g1)
-    for step in range(STEPS):
-        src, dst = bufs[step % 2], bufs[(step + 1) % 2]
-        for j in range(step + 1, 15 - step):
-            g = src[j]
-            out = (
-                center[j] * g
-                + west(plon[j] * g)
-                + east(mlon[j] * g)
-                + plat[j - 1] * src[j - 1]
-                + mlat[j + 1] * src[j + 1]
-            )
-            if step + 1 < STEPS:
-                dst[j] = out
-                if 4 <= j < 12:
-                    total[j - 4] = (g if step == 0 else total[j - 4]) + out
-            else:
-                start_ref[j - 4] = out
+    coefs = [Rows(None, coef_ref, i) for i in range(5)]
+    total_ref[...] = adj_ref[...]
+
+    def done(step, dst):
+        if step == STEPS:
+            far_ref[...] = dst[8:12]
+        else:
+            for j in range(4 + step, 12):
+                total_ref[j - 4] = total_ref[j - 4] + dst[j]
+
+    inner_steps(adjoint_step, (g0, g1), coefs, joint_ref, done)
+
+
+def adjoint_kernel(
+    adj_ref, outer_ref, edge_ref, coef_ref, joint_ref, far_ref, total_ref, forcing_ref, start_ref, g0, g1, sums
+):
+    core = lax.axis_index("ens")
+    lons = forcing_ref.shape[-1]
+    g0[0:4] = outer_ref[...]
+    g0[4:6] = adj_ref[0:2]
+    coefs = [Rows(edge_ref, coef_ref, i) for i in range(5)]
+    sums[...] = total_ref[0:3]
+    start_ref[4:8] = far_ref[...]
+
+    def done(step, dst):
+        if step == STEPS:
+            start_ref[0:4] = dst[4:8]
+        else:
+            for j in range(4, 4 + step):
+                sums[j - 4] = sums[j - 4] + dst[j]
+
+    outer_steps(adjoint_step, (g0, g1), coefs, joint_ref, done)
+
+    def store(at):
+        for r in range(HALF):
+            forcing_ref[:, at(r), :] = (sums if r < 3 else total_ref)[r, :, 0:lons]
 
     @pl.when(core == 0)
     def _():
-        for r in range(HALF):
-            forcing_ref[:, r, :] = total[r, :, 0:lons]
+        store(lambda r: r)
 
     @pl.when(core == 1)
     def _():
-        for r in range(HALF):
-            forcing_ref[:, 7 - r, :] = total[r, :, 0:lons]
+        store(lambda r: 7 - r)
 
 
 def mismatch_kernel(start_ref, mismatch_ref, inc_ref, prec_ref, grad_ref):
@@ -373,33 +435,42 @@
     halo = lax.ppermute(outgoing, band, trade)
     own_rows, field = call(own_kernel, [VMEM], [own, (12, levels, wide)])(increment)
     next_rows = lax.ppermute(own_rows, TM, [(i + 1, i) for i in range(count_t - 1)])
-    coefs, prec, weight = call(
+    working = buf(16, levels, wide)
+    joint = (STEPS - 1, 2, levels, wide)
+    coefs, prec, weight, joint_rows, far = call(
         prepare_kernel,
-        [HBM] * 2 + [SMEM] + [VMEM] * 3,
-        [(5, 12, levels, wide), (levels, wide), (slots, blocks)],
-        [whole, whole, pltpu.SemaphoreType.DMA((2,))],
-    )(in_hbm(wind_lon), in_hbm(wind_lat), model_precision, obs_rows, obs_counts, obs_precision[0].T)
+        [HBM] * 2 + [VMEM, SMEM] + [VMEM] * 3,
+        [(5, 12, levels, wide), (levels, wide), (slots, blocks), joint, quarter],
+        [whole, whole, working, working, pltpu.SemaphoreType.DMA((2,))],
+    )(in_hbm(wind_lon), in_hbm(wind_lat), field, model_precision, obs_rows, obs_counts, obs_precision[0].T)
     other_pert = lax.ppermute(perturbations, "ens", partner)
 
-    later, adj, outer, inner, edges = call(
+    end, force, edges = call(
         forward_kernel,
         [VMEM] * 5 + [HBM, HBM] + [VMEM] * 2,
-        [own, own, quarter, quarter, (5, 4, levels, wide)],
+        [own, own, (5, 4, levels, wide)],
         [
-            buf(16, levels, wide), buf(16, levels, wide), buf(blocks, wide), buf(slots, blocks),
+            working, working, buf(blocks, wide), buf(slots, blocks),
             buf(blocks, slots, lons), pltpu.SMEM((1, blocks), jnp.int32), pltpu.SemaphoreType.DMA((2,)),
         ],
-    )(field, coefs, prec, halo, next_rows, in_hbm(obs_jacobian), in_hbm(obs_rows), obs_values[0].T, weight)
+    )(field, coefs, joint_rows, far, halo, in_hbm(obs_jacobian), in_hbm(obs_rows), obs_values[0].T, weight)
+    next_rows, end = lax.optimization_barrier((next_rows, end))
+    later, adj, outer, inner = call(seed_kernel, [VMEM] * 5, [own, own, quarter, quarter])(
+        force, end, next_rows, prec, coefs
+    )
     outer = lax.ppermute(outer, band, trade)
     inner = lax.ppermute(inner, "ens", partner)
     mismatch = lax.ppermute(later, TM, [(i, i + 1) for i in range(count_t - 1)])
 
+    joint_rows, far, total = call(
+        adjoint_inner_kernel, [VMEM] * 3, [joint, quarter, own], [working, working]
+    )(adj, inner, coefs)
     forcing, start = call(
         adjoint_kernel,
-        [VMEM] * 5,
+        [VMEM] * 7,
         [(levels, HALF, lons), own],
-        [buf(16, levels, wide), buf(16, levels, wide), buf(*own)],
-    )(adj, outer, inner, edges, coefs)
+        [working, working, buf(3, levels, wide)],
+    )(adj, outer, edges, coefs, joint_rows, far, total)
     pieces = lax.all_to_all(forcing, TM, 0, 0, tiled=True)
 
     (products,) = call(product_kernel, [VMEM] * 3, [(count_t * count_l, 1, LANES)])(

time: 83.4 us -> 81.6 us (0.978)
  waiting for transfers between devices: 9.5 us -> 7.42 us
  blocking collectives: 42.8 us -> 41.5 us
  Pallas kernels: 11.5 us -> 12.4 us
    ppermute x1, waiting for transfers between devices: 7.19 us -> 0.01 us  [on_device(): lax.ppermute(own_rows, TM, [(i + 1, i) for i in range(count_t - 1)])]
    ppermute x1, waiting for transfers between devices: 0.01 us -> 6.01 us  [on_device(): halo = lax.ppermute(outgoing, band, trade)]
    all_to_all x1, blocking collectives: 17.9 us -> 15.2 us  [on_device(): pieces = lax.all_to_all(forcing, TM, 0, 0, tiled=True)]
    all_to_all x1, blocking collectives: 25 us -> 26.4 us  [on_device(): sums = lax.all_to_all(products, TM_LAT, 0, 0, tiled=True)]
    ppermute x1, waiting for transfers between devices: 1.47 us -> 0.58 us  [on_device(): outer = lax.ppermute(outer, band, trade)]
    pallas_call x3 -> x5, Pallas kernels: 7.41 us -> 8.28 us  [the longest x1 3.44 us: on_device(): call(prepare_kernel, [HBM] * 2 + [VMEM, SMEM] + [VMEM] * 3, [(5, 12, leve...]
  transfers between devices with their start and end apart: 8 -> 8, of which waited for: 3 -> 3; matrix products, arithmetic and copies ran while one was open for 0% -> 0% of each run, Pallas kernels for 12% -> 14%
where the time goes in v4:
time: 81.6 us; the launch traced here: 81.2 us
  blocking collectives  41.5 us (51%)
  starting transfers between devices  19 us (23%)
  Pallas kernels  12.4 us (15%)
  waiting for transfers between devices  7.42 us (9%)
  between operations  0.85 us (1%)
    all_to_all x1, blocking collectives, on_device(): sums = lax.all_to_all(products, TM_LAT, 0, 0, tiled=True)  26.4 us
    all_to_all x1, blocking collectives, on_device(): pieces = lax.all_to_all(forcing, TM, 0, 0, tiled=True)  15.2 us
    ppermute x1, waiting for transfers between devices, on_device(): halo = lax.ppermute(outgoing, band, trade)  6.01 us
    ppermute x1, starting transfers between devices, on_device(): outer = lax.ppermute(outer, band, trade)  5.89 us
    pallas_call x1, Pallas kernels, on_device(): call(prepare_kernel, [HBM] * 2 + [VMEM, SMEM] + [VMEM] * 3, [(5, 12, leve...  3.44 us
    ppermute x1, starting transfers between devices, on_device(): other_pert = lax.ppermute(perturbations, 'ens', partner)  3.29 us
    pallas_call x1, Pallas kernels, on_device(): call(forward_kernel, [VMEM] * 5 + [HBM, HBM] + [VMEM] * 2, [own, own, (5,...  3.23 us
    ppermute x1, starting transfers between devices, on_device(): mismatch = lax.ppermute(later, TM, [(i, i + 1) for i in range(count_t - 1)])  3.23 us
  transfers between devices with their start and end apart: 8, of which 3 were waited for; matrix products, arithmetic and copies ran while one was open for 0% of the time, Pallas kernels for 14%

profile of v4, /device:TPU:1, one launch (start us, length us, event | category | flops | bytes accessed | tf_op | source)
XLA Modules:
  0.0 81.2 jit_solution(8609404524413682628)
XLA Ops:
  0.6 0.0 copy-start.1
  0.7 0.0 copy-start.4
  0.7 3.3 %collective-permute-start.5 = (f32[16,1,16,1440]{3,2,1,0:T(8,128)}, f32[16,1,16,1440]{3,2,1,0:T(8,128)S(1)}, u32[]{:S(2)}, u32[]{:S(2)}) collective-permute-start(f32[16,1,16,1440]{3,2,1,0:T(8,128)} %own_ref.3), channel_id=1, source_target_pairs={{0,1},{1,0},{2,3},{3,2},{4,5},{5,4},{6,7},{7,6},{8,9},{9,8},{10,11... | collective-permute-start | bytes 4423688 | tf_op jit(solution)/shard_map/ppermute | solution.py:446
  4.0 1.4 %shard_map.115 = f32[10,8,1536]{2,1,0:T(8,128)S(1)} custom-call(f32[1,8,16,1440]{3,2,1,0:T(8,128)} %inc_hbm.1, f32[1,8,16,1440]{3,2,1,0:T(8,128)} %lon_hbm.3, f32[1,8,16,1440]{3,2,1,0:T(8,128)} %lat_hbm.3), custom_call_target="tpu_custom_call" | custom-call | tf_op jit(solution)/shard_map/pallas_call | solution.py:432
  5.4 3.0 %collective-permute-start = (f32[10,8,1536]{2,1,0:T(8,128)S(1)}, f32[10,8,1536]{2,1,0:T(8,128)S(1)}, u32[]{:S(2)}, u32[]{:S(2)}) collective-permute-start(f32[10,8,1536]{2,1,0:T(8,128)S(1)} %shard_map.115), channel_id=1, source_target_pairs={{1,2},{2,1},{3,4},{4,3},{5,6},{6,5},{7,8},{8,7},{9,10},{10,9},{11,... | collective-permute-start | bytes 1474568 | tf_op jit(solution)/shard_map/ppermute | solution.py:435
  8.4 0.2 shard_map.113
  8.6 1.3 %collective-permute-start.1 = (f32[8,8,1536]{2,1,0:T(8,128)S(1)}, f32[8,8,1536]{2,1,0:T(8,128)S(1)}, u32[]{:S(2)}, u32[]{:S(2)}) collective-permute-start(f32[8,8,1536]{2,1,0:T(8,128)S(1)} %get-tuple-element.32.inc_ref), channel_id=1, source_target_pairs={{32,0},{64,32},{96,64},{128,96},{160,128},{192,160},{224,192},{33,... | collective-permute-start | bytes 1179656 | tf_op jit(solution)/shard_map/ppermute | solution.py:437
  9.9 3.4 %shard_map.114 = (f32[5,12,8,1536]{3,2,1,0:T(8,128)S(1)}, f32[8,1536]{1,0:T(8,128)S(1)}, f32[16,32]{1,0:T(8,128)S(1)}, f32[3,2,8,1536]{3,2,1,0:T(8,128)S(1)}, f32[4,8,1536]{2,1,0:T(8,128)S(1)}) custom-call(f32[1,8,16,1440]{3,2,1,0:T(8,128)} %lon_hbm.3, f32[1,8,16,1440]{3,2,1,0:T(8,128)} %lat_hbm.3, f32[12,8,1536]{2,1,0:T(8,128)S(1)} %get-tuple-element.26.field_ref, ...), custom_call_target="tpu_custom_call" | custom-call | tf_op jit(solution)/shard_map/pallas_call | solution.py:440
  13.4 6.0 %collective-permute-done.halo_ref = f32[10,8,1536]{2,1,0:T(8,128)S(1)} collective-permute-done((f32[10,8,1536]{2,1,0:T(8,128)S(1)}, f32[10,8,1536]{2,1,0:T(8,128)S(1)}, u32[]{:S(2)}, u32[]{:S(2)}) %collective-permute-start) | collective-permute-done | bytes 491552 | tf_op jit(solution)/shard_map/ppermute | solution.py:435
  19.4 3.2 %shard_map.116 = (f32[8,8,1536]{2,1,0:T(8,128)S(1)}, f32[8,8,1536]{2,1,0:T(8,128)S(1)}, f32[5,4,8,1536]{3,2,1,0:T(8,128)S(1)}) custom-call(f32[12,8,1536]{2,1,0:T(8,128)S(1)} %get-tuple-element.26.field_ref, f32[5,12,8,1536]{3,2,1,0:T(8,128)S(1)} %get-tuple-element.27.coef_ref, f32[3,2,8,1536]{3,2,1,0:T(8,128)S(1)} %get-tuple-element.28.joint_ref, ...), custom_call_target="tpu_custom_call" | custom-call | tf_op jit(solution)/shard_map/pallas_call | solution.py:448
  22.6 0.0 collective-permute-done.1.next_ref
  22.6 0.1 shard_map.117
  22.7 0.1 collective-permute-start.3
  22.8 5.9 %collective-permute-start.2 = (f32[4,8,1536]{2,1,0:T(8,128)S(1)}, f32[4,8,1536]{2,1,0:T(8,128)S(1)}, u32[]{:S(2)}, u32[]{:S(2)}) collective-permute-start(f32[4,8,1536]{2,1,0:T(8,128)S(1)} %get-tuple-element.38), channel_id=1, source_target_pairs={{1,2},{2,1},{3,4},{4,3},{5,6},{6,5},{7,8},{8,7},{9,10},{10,9},{11,... | collective-permute-start | bytes 589832 | tf_op jit(solution)/shard_map/ppermute | solution.py:461
  28.7 3.2 %collective-permute-start.4 = (f32[8,8,1536]{2,1,0:T(8,128)S(1)}, f32[8,8,1536]{2,1,0:T(8,128)S(1)}, u32[]{:S(2)}, u32[]{:S(2)}) collective-permute-start(f32[8,8,1536]{2,1,0:T(8,128)S(1)} %get-tuple-element.45), channel_id=1, source_target_pairs={{0,32},{32,64},{64,96},{96,128},{128,160},{160,192},{192,224},{1,3... | collective-permute-start | bytes 1179656 | tf_op jit(solution)/shard_map/ppermute | solution.py:463
  32.0 0.0 collective-permute-done.3.inner_ref
  32.0 0.9 %shard_map.118 = (f32[3,2,8,1536]{3,2,1,0:T(8,128)S(1)}, f32[4,8,1536]{2,1,0:T(8,128)S(1)}, f32[8,8,1536]{2,1,0:T(8,128)S(1)}) custom-call(f32[8,8,1536]{2,1,0:T(8,128)S(1)} %get-tuple-element.37.adj_ref, f32[4,8,1536]{2,1,0:T(8,128)S(1)} %collective-permute-done.3.inner_ref, f32[5,12,8,1536]{3,2,1,0:T(8,128)S(1)} %get-tuple-element.27.coef_ref), custom_call_target="tpu_custom_call" | custom-call | tf_op jit(solution)/shard_map/pallas_call | solution.py:465
  32.9 0.6 collective-permute-done.2.outer_ref
  33.5 0.6 shard_map.119
  34.1 15.2 %all_to_all.10.pieces_ref = f32[8,8,1440]{2,1,0:T(8,128)S(1)} all-to-all(f32[8,8,1440]{2,1,0:T(8,128)S(1)} %get-tuple-element.46), channel_id=1, replica_groups=mesh['tm_0'=2,'tm_1'=4,'lat_0'=8,'lat_1'=2,'ens'=2] {'tm_0','tm_1'}, dimensions={0} | all-to-all | bytes 737280 | tf_op jit(solution)/shard_map/all_to_all | solution.py:474
  49.3 0.0 collective-permute-done.5.other_ref
  49.3 0.2 shard_map.120
  49.5 0.0 collective-permute-done.4.mismatch_ref
  49.5 0.1 shard_map.121.own_ref
  49.6 0.3 collective-permute-start.6
  49.9 26.4 %all_to_all.11.sums_ref = f32[128,1,128]{2,1,0:T(1,128)S(1)} all-to-all(f32[128,1,128]{2,1,0:T(1,128)S(1)} %shard_map.120), channel_id=1, replica_groups=mesh['tm_0'=2,'tm_1'=4,'lat_0'=8,'lat_1'=2,'ens'=2] {'tm_0','tm_1','lat_..., dimensions={0} | all-to-all | bytes 131072 | tf_op jit(solution)/shard_map/all_to_all | solution.py:482
  76.3 0.1 shard_map.123.sum_ref
  76.4 1.9 %collective-permute-start.7 = (f32[8,128]{1,0:T(8,128)S(1)}, f32[8,128]{1,0:T(8,128)S(1)}, u32[]{:S(2)}, u32[]{:S(2)}) collective-permute-start(f32[8,128]{1,0:T(8,128)S(1)} %shard_map.123.sum_ref), channel_id=1, source_target_pairs={{0,1},{1,0},{2,3},{3,2},{4,5},{5,4},{6,7},{7,6},{8,9},{9,8},{10,11... | collective-permute-start | bytes 12296 | tf_op jit(solution)/shard_map/ppermute | solution.py:486
  78.3 0.8 %collective-permute-done.7.other_sum_ref = f32[8,128]{1,0:T(8,128)S(1)} collective-permute-done((f32[8,128]{1,0:T(8,128)S(1)}, f32[8,128]{1,0:T(8,128)S(1)}, u32[]{:S(2)}, u32[]{:S(2)}) %collective-permute-start.7) | collective-permute-done | bytes 4128 | tf_op jit(solution)/shard_map/ppermute | solution.py:486
  79.1 1.0 %shard_map.124 = f32[1,16,1440]{2,1,0:T(8,128)} custom-call(f32[8,128]{1,0:T(8,128)S(1)} %shard_map.123.sum_ref, f32[8,128]{1,0:T(8,128)S(1)} %collective-permute-done.7.other_sum_ref, f32[16,1,16,1440]{3,2,1,0:T(8,128)S(1)} %copy-done, f32[16,1,16,1440]{3,2,1,0:T(8,128)S(1)} %collective-permute-done.5.other_ref), custom_call_target="tpu_custom_call" | custom-call | tf_op jit(solution)/shard_map/pallas_call | solution.py:487
  80.1 0.0 collective-permute-done.6.other_ref
  80.1 1.1 %shard_map.122 = f32[1,8,16,1440]{3,2,1,0:T(8,128)} custom-call(f32[8,8,1536]{2,1,0:T(8,128)S(1)} %shard_map.121.own_ref, f32[8,8,1536]{2,1,0:T(8,128)S(1)} %collective-permute-done.6.other_ref), custom_call_target="tpu_custom_call" | custom-call | tf_op jit(solution)/shard_map/pallas_call | solution.py:483
  (12 shorter events, 0.0 us)
Async XLA Ops:
  0.6 7.7 %copy-start.1 = (f32[1,8,16,1440]{3,2,1,0:T(8,128)S(1)}, f32[1,8,16,1440]{3,2,1,0:T(8,128)}, u32[]{:S(2)}) copy-start(f32[1,8,16,1440]{3,2,1,0:T(8,128)} %inc_hbm.1) | copy-start | bytes 2211844
  0.6 9.2 %copy-start.2 = (f32[1,32,16]{1,2,0:T(8,128)S(1)}, f32[1,32,16]{1,2,0:T(8,128)}, u32[]{:S(2)}) copy-start(f32[1,32,16]{1,2,0:T(8,128)} %param.18) | copy-start | bytes 6148
  0.7 9.2 %copy-start.5 = (f32[8]{0:T(128)S(1)}, f32[8]{0:T(128)}, u32[]{:S(2)}) copy-start(f32[8]{0:T(128)} %prec_ref.1) | copy-start | bytes 100
  0.7 9.2 %copy-start.4 = (s32[1,32]{1,0:T(1,128)S(1)}, s32[1,32]{1,0:T(1,128)}, u32[]{:S(2)}) copy-start(s32[1,32]{1,0:T(1,128)} %rows_hbm.1) | copy-start | bytes 388
  0.7 9.2 %copy-start.6 = (s32[1,32]{1,0:T(1,128)S(1)}, s32[1,32]{1,0:T(1,128)}, u32[]{:S(2)}) copy-start(s32[1,32]{1,0:T(1,128)} %counts_ref.1) | copy-start | bytes 388
  0.7 18.7 %copy-start.3 = (f32[1,32,16]{1,2,0:T(8,128)S(1)}, f32[1,32,16]{1,2,0:T(8,128)}, u32[]{:S(2)}) copy-start(f32[1,32,16]{1,2,0:T(8,128)} %param.17) | copy-start | bytes 6148
  0.7 48.6 %collective-permute-start.5 = (f32[16,1,16,1440]{3,2,1,0:T(8,128)}, f32[16,1,16,1440]{3,2,1,0:T(8,128)S(1)}, u32[]{:S(2)}, u32[]{:S(2)}) collective-permute-start(f32[16,1,16,1440]{3,2,1,0:T(8,128)} %own_ref.3), channel_id=1, source_target_pairs={{0,1},{1,0},{2,3},{3,2},{4,5},{5,4},{6,7},{7,6},{8,9},{9,8},{10,11... | collective-permute-start | bytes 4423688 | tf_op jit(solution)/shard_map/ppermute | solution.py:446
  5.4 14.0 %collective-permute-start = (f32[10,8,1536]{2,1,0:T(8,128)S(1)}, f32[10,8,1536]{2,1,0:T(8,128)S(1)}, u32[]{:S(2)}, u32[]{:S(2)}) collective-permute-start(f32[10,8,1536]{2,1,0:T(8,128)S(1)} %shard_map.115), channel_id=1, source_target_pairs={{1,2},{2,1},{3,4},{4,3},{5,6},{6,5},{7,8},{8,7},{9,10},{10,9},{11,... | collective-permute-start | bytes 1474568 | tf_op jit(solution)/shard_map/ppermute | solution.py:435
  8.6 14.0 %collective-permute-start.1 = (f32[8,8,1536]{2,1,0:T(8,128)S(1)}, f32[8,8,1536]{2,1,0:T(8,128)S(1)}, u32[]{:S(2)}, u32[]{:S(2)}) collective-permute-start(f32[8,8,1536]{2,1,0:T(8,128)S(1)} %get-tuple-element.32.inc_ref), channel_id=1, source_target_pairs={{32,0},{64,32},{96,64},{128,96},{160,128},{192,160},{224,192},{33,... | collective-permute-start | bytes 1179656 | tf_op jit(solution)/shard_map/ppermute | solution.py:437
  22.7 9.2 %collective-permute-start.3 = (f32[4,8,1536]{2,1,0:T(8,128)S(1)}, f32[4,8,1536]{2,1,0:T(8,128)S(1)}, u32[]{:S(2)}, u32[]{:S(2)}) collective-permute-start(f32[4,8,1536]{2,1,0:T(8,128)S(1)} %get-tuple-element.40), channel_id=1, source_target_pairs={{0,1},{1,0},{2,3},{3,2},{4,5},{5,4},{6,7},{7,6},{8,9},{9,8},{10,11... | collective-permute-start | bytes 589832 | tf_op jit(solution)/shard_map/ppermute | solution.py:462
  22.8 10.6 %collective-permute-start.2 = (f32[4,8,1536]{2,1,0:T(8,128)S(1)}, f32[4,8,1536]{2,1,0:T(8,128)S(1)}, u32[]{:S(2)}, u32[]{:S(2)}) collective-permute-start(f32[4,8,1536]{2,1,0:T(8,128)S(1)} %get-tuple-element.38), channel_id=1, source_target_pairs={{1,2},{2,1},{3,4},{4,3},{5,6},{6,5},{7,8},{8,7},{9,10},{10,9},{11,... | collective-permute-start | bytes 589832 | tf_op jit(solution)/shard_map/ppermute | solution.py:461
  28.7 20.8 %collective-permute-start.4 = (f32[8,8,1536]{2,1,0:T(8,128)S(1)}, f32[8,8,1536]{2,1,0:T(8,128)S(1)}, u32[]{:S(2)}, u32[]{:S(2)}) collective-permute-start(f32[8,8,1536]{2,1,0:T(8,128)S(1)} %get-tuple-element.45), channel_id=1, source_target_pairs={{0,32},{32,64},{64,96},{96,128},{128,160},{160,192},{192,224},{1,3... | collective-permute-start | bytes 1179656 | tf_op jit(solution)/shard_map/ppermute | solution.py:463
  33.4 15.8 %copy-start = (f32[16,1,16,1440]{3,2,1,0:T(8,128)S(1)}, f32[16,1,16,1440]{3,2,1,0:T(8,128)}, u32[]{:S(2)}) copy-start(f32[16,1,16,1440]{3,2,1,0:T(8,128)} %own_ref.3) | copy-start | bytes 4423684
  49.6 30.5 %collective-permute-start.6 = (f32[8,8,1536]{2,1,0:T(8,128)S(1)}, f32[8,8,1536]{2,1,0:T(8,128)S(1)}, u32[]{:S(2)}, u32[]{:S(2)}) collective-permute-start(f32[8,8,1536]{2,1,0:T(8,128)S(1)} %shard_map.121.own_ref), channel_id=1, source_target_pairs={{0,1},{1,0},{2,3},{3,2},{4,5},{5,4},{6,7},{7,6},{8,9},{9,8},{10,11... | collective-permute-start | bytes 1179656 | tf_op jit(solution)/shard_map/ppermute | solution.py:481
  76.4 2.7 %collective-permute-start.7 = (f32[8,128]{1,0:T(8,128)S(1)}, f32[8,128]{1,0:T(8,128)S(1)}, u32[]{:S(2)}, u32[]{:S(2)}) collective-permute-start(f32[8,128]{1,0:T(8,128)S(1)} %shard_map.123.sum_ref), channel_id=1, source_target_pairs={{0,1},{1,0},{2,3},{3,2},{4,5},{5,4},{6,7},{7,6},{8,9},{9,8},{10,11... | collective-permute-start | bytes 12296 | tf_op jit(solution)/shard_map/ppermute | solution.py:486

commit v5 on v4

--- a/solution.py
+++ b/solution.py
@@ -72,7 +72,7 @@
         rows(HALF, lambda r: 7 - r)
 
 
-def own_kernel(inc_ref, own_ref, field_ref):
+def own_kernel(inc_ref, near_ref, far_ref, field_ref):
     core = lax.axis_index("ens")
     lons = inc_ref.shape[-1]
 
@@ -81,7 +81,7 @@
             field_ref[r, :, 0:lons] = inc_ref[0, :, at(r), :]
             wrap(field_ref.at[r], lons)
             if r < HALF:
-                own_ref[r] = field_ref[r]
+                (near_ref if r < 4 else far_ref)[r % 4] = field_ref[r]
 
     @pl.when(core == 0)
     def _():
@@ -141,8 +141,8 @@
 
 
 def prepare_kernel(
-    lon_hbm, lat_hbm, field_ref, prec_ref, rows_ref, counts_ref, oprec_ref,
-    coef_ref, prec_out, weight_ref, joint_ref, end_ref, lon, lat, x0, x1, sems,
+    lon_hbm, lat_hbm, jac_hbm, field_ref, prec_ref, rows_ref, counts_ref, oprec_ref,
+    coef_ref, prec_out, weight_ref, joint_ref, end_ref, jac_ref, lon, lat, x0, x1, sems,
 ):
     core = lax.axis_index("ens")
     lons = lon.shape[-1]
@@ -153,6 +153,8 @@
     ]
     for copy in copies:
         copy.start()
+    jac_copy = pltpu.make_async_copy(jac_hbm.at[0], jac_ref, sems.at[2])
+    jac_copy.start()
     level = lax.broadcasted_iota(jnp.int32, prec_out.shape, 0)
     prec = jnp.zeros(prec_out.shape, jnp.float32)
     for k in range(levels):
@@ -188,6 +190,7 @@
             end_ref[...] = dst[8:12]
 
     inner_steps(forward_step, (x0, x1), coefs, joint_ref, done)
+    jac_copy.wait()
 
 
 def store_coefficients(coef_ref, at, c, e):
@@ -201,14 +204,12 @@
 
 
 def forward_kernel(
-    field_ref, coef_ref, joint_ref, far_ref, halo_ref, jac_hbm, rows_hbm, val_ref, weight_ref,
-    end_ref, force_ref, edge_ref, x0, x1, pk, wgt, jac, rows, sems,
+    field_ref, coef_ref, joint_ref, far_ref, halo_ref, jac, rows_hbm, val_ref, weight_ref,
+    end_ref, force_ref, edge_ref, x0, x1, pk, wgt, rows, sem,
 ):
     core = lax.axis_index("ens")
     blocks, slots, lons = jac.shape
-    jac_copy = pltpu.make_async_copy(jac_hbm.at[0], jac, sems.at[0])
-    rows_copy = pltpu.make_async_copy(rows_hbm, rows, sems.at[1])
-    jac_copy.start()
+    rows_copy = pltpu.make_async_copy(rows_hbm, rows, sem)
     rows_copy.start()
     x0[0:4] = halo_ref[0:4]
     x0[4:6] = field_ref[0:2]
@@ -219,14 +220,14 @@
 
     def done(step, dst):
         if step == STEPS:
-            end_ref[0:4] = dst[4:8]
+            end_ref[...] = dst[4:8]
+            dst[8:12] = far_ref[...]
 
     outer_steps(forward_step, (x0, x1), coefs, joint_ref, done)
-    end_ref[4:8] = far_ref[...]
+    field = (x0, x1)[STEPS % 2]
     force_ref[...] = jnp.zeros(force_ref.shape, jnp.float32)
 
     rows_copy.wait()
-    jac_copy.wait()
 
     def place(j):
         r = rows[0, j]
@@ -236,7 +237,7 @@
 
     for j in range(blocks):
         row, lev = place(j)
-        pk[pl.ds(j, 1), :] = end_ref[row, lev, :]
+        pk[pl.ds(j, 1), :] = field[4 + row, lev, :]
     lane = lax.broadcasted_iota(jnp.int32, (slots, blocks), 1)
     ev = jnp.zeros((slots, blocks), jnp.float32)
     for j in range(blocks):
@@ -252,23 +253,33 @@
         force_ref[row, lev, :] = force_ref[row, lev, :] + pk[pl.ds(j, 1), :]
 
 
-def seed_kernel(force_ref, end_ref, next_ref, prec_ref, coef_ref, later_ref, adj_ref, outer_ref, inner_ref):
-    has_next = (lax.axis_index(TM) < lax.axis_size(TM) - 1).astype(jnp.float32)
-    prec = prec_ref[...] * has_next
-    for r in range(HALF):
-        later = prec * (next_ref[r] - end_ref[r])
-        later_ref[r] = later
-        adj_ref[r] = force_ref[r] - later
-    for q in range(4):
-        outer_ref[q] = adj_ref[3 - q] * coef_ref[4, 3] if q == 0 else adj_ref[3 - q]
-        inner_ref[q] = adj_ref[7 - q]
-
-
-def adjoint_inner_kernel(adj_ref, inner_ref, coef_ref, joint_ref, far_ref, total_ref, g0, g1):
-    g0[4:12] = adj_ref[...]
+def with_next():
+    return (lax.axis_index(TM) < lax.axis_size(TM) - 1).astype(jnp.float32)
+
+
+def near_kernel(force_ref, end_ref, next_ref, prec_ref, coef_ref, adj_ref, outer_ref):
+    prec = prec_ref[...] * with_next()
+    for r in range(4):
+        adj = force_ref[r] - prec * (next_ref[r] - end_ref[r])
+        adj_ref[r] = adj
+        outer_ref[3 - r] = adj * coef_ref[4, 3] if r == 3 else adj
+
+
+def far_kernel(force_ref, end_ref, next_ref, prec_ref, adj_ref, inner_ref):
+    prec = prec_ref[...] * with_next()
+    for r in range(4):
+        adj = force_ref[4 + r] - prec * (next_ref[r] - end_ref[r])
+        adj_ref[r] = adj
+        inner_ref[3 - r] = adj
+
+
+def adjoint_inner_kernel(near_ref, adj_ref, inner_ref, coef_ref, joint_ref, far_ref, total_ref, g0, g1):
+    g0[4:8] = near_ref[...]
+    g0[8:12] = adj_ref[...]
     g0[12:16] = inner_ref[...]
     coefs = [Rows(None, coef_ref, i) for i in range(5)]
-    total_ref[...] = adj_ref[...]
+    total_ref[0:4] = near_ref[...]
+    total_ref[4:8] = adj_ref[...]
 
     def done(step, dst):
         if step == STEPS:
@@ -313,11 +324,11 @@
         store(lambda r: 7 - r)
 
 
-def mismatch_kernel(start_ref, mismatch_ref, inc_ref, prec_ref, grad_ref):
-    first_window = lax.axis_index(TM) == 0
+def mismatch_kernel(start_ref, near_prior_ref, far_prior_ref, near_ref, far_ref, prec_ref, grad_ref):
     prec = prec_ref[...]
-    for r in range(HALF):
-        grad_ref[r] = start_ref[r] + jnp.where(first_window, prec * inc_ref[r], mismatch_ref[r])
+    for r in range(4):
+        grad_ref[r] = start_ref[r] + prec * (near_ref[r] - near_prior_ref[r])
+        grad_ref[4 + r] = start_ref[4 + r] + prec * (far_ref[r] - far_prior_ref[r])
 
 
 def product_kernel(pieces_ref, own_ref, other_ref, out_ref):
@@ -340,7 +351,8 @@
     out_ref[...] = jnp.broadcast_to(vec, out_ref.shape)
 
 
-def step_kernel(sum_ref, other_sum_ref, own_ref, other_ref, out_ref):
+def final_kernel(sum_ref, other_sum_ref, own_ref, other_ref, own_grad_ref, other_grad_ref, out_ref, grad_ref):
+    store_gradient(own_grad_ref, other_grad_ref, grad_ref)
     members = own_ref.shape[0]
     lane = lax.broadcasted_iota(jnp.int32, (HALF, LANES), 1)
     theirs = other_sum_ref[...]
@@ -358,7 +370,7 @@
         out_ref[0, rows, :] = total
 
 
-def gradient_kernel(own_ref, other_ref, out_ref):
+def store_gradient(own_ref, other_ref, out_ref):
     core = lax.axis_index("ens")
     lons = out_ref.shape[-1]
 
@@ -433,60 +445,59 @@
         edge_kernel, [HBM] * 3, [(10, levels, wide)], [piece, piece, piece, pltpu.SemaphoreType.DMA((3,))]
     )(*(in_hbm(field) for field in fields))
     halo = lax.ppermute(outgoing, band, trade)
-    own_rows, field = call(own_kernel, [VMEM], [own, (12, levels, wide)])(increment)
-    next_rows = lax.ppermute(own_rows, TM, [(i + 1, i) for i in range(count_t - 1)])
+    near_rows, far_rows, field = call(own_kernel, [VMEM], [quarter, quarter, (12, levels, wide)])(increment)
+    earlier = [(i + 1, i) for i in range(count_t - 1)]
+    next_near = lax.ppermute(near_rows, TM, earlier)
+    next_far = lax.ppermute(far_rows, TM, earlier)
     working = buf(16, levels, wide)
     joint = (STEPS - 1, 2, levels, wide)
-    coefs, prec, weight, joint_rows, far = call(
+    coefs, prec, weight, joint_rows, far, jacobian = call(
         prepare_kernel,
-        [HBM] * 2 + [VMEM, SMEM] + [VMEM] * 3,
-        [(5, 12, levels, wide), (levels, wide), (slots, blocks), joint, quarter],
-        [whole, whole, working, working, pltpu.SemaphoreType.DMA((2,))],
-    )(in_hbm(wind_lon), in_hbm(wind_lat), field, model_precision, obs_rows, obs_counts, obs_precision[0].T)
+        [HBM] * 3 + [VMEM, SMEM] + [VMEM] * 3,
+        [(5, 12, levels, wide), (levels, wide), (slots, blocks), joint, quarter, (blocks, slots, lons)],
+        [whole, whole, working, working, pltpu.SemaphoreType.DMA((3,))],
+    )(in_hbm(wind_lon), in_hbm(wind_lat), in_hbm(obs_jacobian), field, model_precision, obs_rows, obs_counts, obs_precision[0].T)
     other_pert = lax.ppermute(perturbations, "ens", partner)
 
+    later = [(i, i + 1) for i in range(count_t - 1)]
+    far_prior = lax.ppermute(far, TM, later)
     end, force, edges = call(
         forward_kernel,
-        [VMEM] * 5 + [HBM, HBM] + [VMEM] * 2,
-        [own, own, (5, 4, levels, wide)],
+        [VMEM] * 6 + [HBM] + [VMEM] * 2,
+        [quarter, own, (5, 4, levels, wide)],
         [
             working, working, buf(blocks, wide), buf(slots, blocks),
-            buf(blocks, slots, lons), pltpu.SMEM((1, blocks), jnp.int32), pltpu.SemaphoreType.DMA((2,)),
+            pltpu.SMEM((1, blocks), jnp.int32), pltpu.SemaphoreType.DMA,
         ],
-    )(field, coefs, joint_rows, far, halo, in_hbm(obs_jacobian), in_hbm(obs_rows), obs_values[0].T, weight)
-    next_rows, end = lax.optimization_barrier((next_rows, end))
-    later, adj, outer, inner = call(seed_kernel, [VMEM] * 5, [own, own, quarter, quarter])(
-        force, end, next_rows, prec, coefs
-    )
+    )(field, coefs, joint_rows, far, halo, jacobian, in_hbm(obs_rows), obs_values[0].T, weight)
+    near, outer = call(near_kernel, [VMEM] * 5, [quarter, quarter])(force, end, next_near, prec, coefs)
     outer = lax.ppermute(outer, band, trade)
+    adj, inner = call(far_kernel, [VMEM] * 4, [quarter, quarter])(force, far, next_far, prec)
     inner = lax.ppermute(inner, "ens", partner)
-    mismatch = lax.ppermute(later, TM, [(i, i + 1) for i in range(count_t - 1)])
-
-    joint_rows, far, total = call(
-        adjoint_inner_kernel, [VMEM] * 3, [joint, quarter, own], [working, working]
-    )(adj, inner, coefs)
+    near_prior = lax.ppermute(end, TM, later)
+    joint_rows, far_start, total = call(
+        adjoint_inner_kernel, [VMEM] * 4, [joint, quarter, own], [working, working]
+    )(near, adj, inner, coefs)
     forcing, start = call(
         adjoint_kernel,
         [VMEM] * 7,
         [(levels, HALF, lons), own],
         [working, working, buf(3, levels, wide)],
-    )(adj, outer, edges, coefs, joint_rows, far, total)
+    )(near, outer, edges, coefs, joint_rows, far_start, total)
     pieces = lax.all_to_all(forcing, TM, 0, 0, tiled=True)
 
     (products,) = call(product_kernel, [VMEM] * 3, [(count_t * count_l, 1, LANES)])(
         pieces, perturbations, other_pert
     )
-    start, mismatch, products = lax.optimization_barrier((start, mismatch, products))
-    (own_grad,) = call(mismatch_kernel, [VMEM] * 4, [own])(start, mismatch, own_rows, prec)
+    start, near_prior, products = lax.optimization_barrier((start, near_prior, products))
+    (own_grad,) = call(mismatch_kernel, [VMEM] * 6, [own])(start, near_prior, far_prior, near_rows, far_rows, prec)
     other_grad = lax.ppermute(own_grad, "ens", partner)
     sums = lax.all_to_all(products, TM_LAT, 0, 0, tiled=True)
-    (grad_state,) = call(gradient_kernel, [VMEM] * 2, [(1, levels, band_rows, lons)])(own_grad, other_grad)
-
     (total,) = call(sum_kernel, [VMEM], [(HALF, LANES)])(sums)
     other_total = lax.ppermute(total, "ens", partner)
-    (forcing_step,) = call(step_kernel, [VMEM] * 4, [(1, band_rows, lons)])(
-        total, other_total, perturbations, other_pert
-    )
+    forcing_step, grad_state = call(
+        final_kernel, [VMEM] * 6, [(1, band_rows, lons), (1, levels, band_rows, lons)]
+    )(total, other_total, perturbations, other_pert, own_grad, other_grad)
     return (grad_state, forcing_step)
 
 

time: 81.6 us -> 89.2 us (1.093)
  starting transfers between devices: 19 us -> 32.2 us
  blocking collectives: 41.5 us -> 31.3 us
  waiting for transfers between devices: 7.42 us -> 11.2 us
  local copies, waits for them, and re-layouts: 0.03 us -> 1.56 us
  Pallas kernels: 12.4 us -> 11.5 us
    all_to_all x1 -> x0, blocking collectives: 15.2 us -> none  [on_device(): pieces = lax.all_to_all(forcing, TM, 0, 0, tiled=True)]
    all_to_all x0 -> x1, starting transfers between devices: none -> 8.49 us  [on_device(): pieces = lax.all_to_all(forcing, TM, 0, 0, tiled=True)]
    ppermute x2 -> x4, starting transfers between devices: 4.52 us -> 9.72 us  [the longest x1 4.04 us: on_device(): near_prior = lax.ppermute(end, TM, later)]
    all_to_all x1, blocking collectives: 26.4 us -> 31.3 us  [on_device(): sums = lax.all_to_all(products, TM_LAT, 0, 0, tiled=True)]
    ppermute x1, waiting for transfers between devices: 0.58 us -> 3.81 us  [on_device(): outer = lax.ppermute(outer, band, trade)]
    ppermute x2 -> x4, waiting for transfers between devices: 0.01 us -> 1.95 us  [the longest x1 1.94 us: on_device(): far_prior = lax.ppermute(far, TM, later)]
    unnamed x14 -> x36, local copies, waits for them, and re-layouts: 0.03 us -> 1.56 us
    ppermute x1, waiting for transfers between devices: 6.01 us -> 4.64 us  [on_device(): halo = lax.ppermute(outgoing, band, trade)]
  transfers between devices with their start and end apart: 8 -> 11, of which waited for: 3 -> 4; matrix products, arithmetic and copies ran while one was open for 0% -> 0% of each run, Pallas kernels for 14% -> 10%
where the time goes in v5:
time: 89.2 us; the launch traced here: 88.7 us
  starting transfers between devices  32.2 us (36%)
  blocking collectives  31.3 us (35%)
  Pallas kernels  11.5 us (13%)
  waiting for transfers between devices  11.2 us (13%)
  local copies, waits for them, and re-layouts  1.56 us (2%)
  between operations  0.98 us (1%)
    all_to_all x1, blocking collectives, on_device(): sums = lax.all_to_all(products, TM_LAT, 0, 0, tiled=True)  31.3 us
    all_to_all x1, starting transfers between devices, on_device(): pieces = lax.all_to_all(forcing, TM, 0, 0, tiled=True)  8.49 us
    ppermute x1, starting transfers between devices, on_device(): outer = lax.ppermute(outer, band, trade)  5.9 us
    ppermute x1, waiting for transfers between devices, on_device(): halo = lax.ppermute(outgoing, band, trade)  4.64 us
    ppermute x1, starting transfers between devices, on_device(): near_prior = lax.ppermute(end, TM, later)  4.04 us
    ppermute x1, waiting for transfers between devices, on_device(): outer = lax.ppermute(outer, band, trade)  3.81 us
    pallas_call x1, Pallas kernels, on_device(): call(prepare_kernel, [HBM] * 3 + [VMEM, SMEM] + [VMEM] * 3, [(5, 12, leve...  3.47 us
    ppermute x1, starting transfers between devices, on_device(): other_pert = lax.ppermute(perturbations, 'ens', partner)  3.29 us
  transfers between devices with their start and end apart: 11, of which 4 were waited for; matrix products, arithmetic and copies ran while one was open for 0% of the time, Pallas kernels for 10%

profile of v5, /device:TPU:1, one launch (start us, length us, event | category | flops | bytes accessed | tf_op | source)
XLA Modules:
  0.0 88.7 jit_solution(6473203401868134785)
XLA Ops:
  0.7 0.0 copy-start.15
  0.7 3.3 %collective-permute-start.6 = (f32[16,1,16,1440]{3,2,1,0:T(8,128)}, f32[16,1,16,1440]{3,2,1,0:T(8,128)S(1)}, u32[]{:S(2)}, u32[]{:S(2)}) collective-permute-start(f32[16,1,16,1440]{3,2,1,0:T(8,128)} %own_ref.3), channel_id=1, source_target_pairs={{0,1},{1,0},{2,3},{3,2},{4,5},{5,4},{6,7},{7,6},{8,9},{9,8},{10,11... | collective-permute-start | bytes 4423688 | tf_op jit(solution)/shard_map/ppermute | solution.py:460
  4.0 1.4 %shard_map.115 = f32[10,8,1536]{2,1,0:T(8,128)S(1)} custom-call(f32[1,8,16,1440]{3,2,1,0:T(8,128)} %inc_hbm.1, f32[1,8,16,1440]{3,2,1,0:T(8,128)} %lon_hbm.3, f32[1,8,16,1440]{3,2,1,0:T(8,128)} %lat_hbm.3), custom_call_target="tpu_custom_call" | custom-call | tf_op jit(solution)/shard_map/pallas_call | solution.py:444
  5.3 0.0 copy-start.14
  5.4 3.0 %collective-permute-start = (f32[10,8,1536]{2,1,0:T(8,128)S(1)}, f32[10,8,1536]{2,1,0:T(8,128)S(1)}, u32[]{:S(2)}, u32[]{:S(2)}) collective-permute-start(f32[10,8,1536]{2,1,0:T(8,128)S(1)} %shard_map.115), channel_id=1, source_target_pairs={{1,2},{2,1},{3,4},{4,3},{5,6},{6,5},{7,8},{8,7},{9,10},{10,9},{11,... | collective-permute-start | bytes 1474568 | tf_op jit(solution)/shard_map/ppermute | solution.py:447
  8.4 0.2 shard_map.113
  8.6 1.3 %collective-permute-start.3 = (f32[4,8,1536]{2,1,0:T(8,128)S(1)}, f32[4,8,1536]{2,1,0:T(8,128)S(1)}, u32[]{:S(2)}, u32[]{:S(2)}) collective-permute-start(f32[4,8,1536]{2,1,0:T(8,128)S(1)} %get-tuple-element.41.far_ref), channel_id=1, source_target_pairs={{32,0},{64,32},{96,64},{128,96},{160,128},{192,160},{224,192},{33,... | collective-permute-start | bytes 589832 | tf_op jit(solution)/shard_map/ppermute | solution.py:451
  9.9 1.3 %collective-permute-start.1 = (f32[4,8,1536]{2,1,0:T(8,128)S(1)}, f32[4,8,1536]{2,1,0:T(8,128)S(1)}, u32[]{:S(2)}, u32[]{:S(2)}) collective-permute-start(f32[4,8,1536]{2,1,0:T(8,128)S(1)} %get-tuple-element.36.near_ref), channel_id=1, source_target_pairs={{32,0},{64,32},{96,64},{128,96},{160,128},{192,160},{224,192},{33,... | collective-permute-start | bytes 589832 | tf_op jit(solution)/shard_map/ppermute | solution.py:450
  11.2 3.5 %shard_map.114 = (f32[5,12,8,1536]{3,2,1,0:T(8,128)S(1)}, f32[8,1536]{1,0:T(8,128)S(1)}, f32[16,32]{1,0:T(8,128)S(1)}, f32[3,2,8,1536]{3,2,1,0:T(8,128)S(1)}, f3...) custom-call(f32[1,8,16,1440]{3,2,1,0:T(8,128)} %lon_hbm.3, f32[1,8,16,1440]{3,2,1,0:T(8,128)} %lat_hbm.3, ...), custom_call_target="tpu_custom_call" | custom-call | tf_op jit(solution)/shard_map/pallas_call | solution.py:454
  14.7 0.0 copy-start.3
  14.7 4.6 %collective-permute-done.halo_ref = f32[10,8,1536]{2,1,0:T(8,128)S(1)} collective-permute-done((f32[10,8,1536]{2,1,0:T(8,128)S(1)}, f32[10,8,1536]{2,1,0:T(8,128)S(1)}, u32[]{:S(2)}, u32[]{:S(2)}) %collective-permute-start) | collective-permute-done | bytes 491552 | tf_op jit(solution)/shard_map/ppermute | solution.py:447
  19.4 2.0 %shard_map.116 = (f32[4,8,1536]{2,1,0:T(8,128)S(1)}, f32[8,8,1536]{2,1,0:T(8,128)S(1)}, f32[5,4,8,1536]{3,2,1,0:T(8,128)S(1)}) custom-call(f32[12,8,1536]{2,1,0:T(8,128)S(1)} %get-tuple-element.28.field_ref, f32[5,12,8,1536]{3,2,1,0:T(8,128)S(1)} %get-tuple-element.29.coef_ref, f32[3,2,8,1536]{3,2,1,0:T(8,128)S(1)} %get-tuple-element.30.joint_ref, ...), custom_call_target="tpu_custom_call" | custom-call | tf_op jit(solution)/shard_map/pallas_call | solution.py:464
  21.5 0.1 collective-permute-start.4
  21.7 5.9 %collective-permute-start.2 = (f32[4,8,1536]{2,1,0:T(8,128)S(1)}, f32[4,8,1536]{2,1,0:T(8,128)S(1)}, u32[]{:S(2)}, u32[]{:S(2)}) collective-permute-start(f32[4,8,1536]{2,1,0:T(8,128)S(1)} %get-tuple-element.39), channel_id=1, source_target_pairs={{1,2},{2,1},{3,4},{4,3},{5,6},{6,5},{7,8},{8,7},{9,10},{10,9},{11,... | collective-permute-start | bytes 589832 | tf_op jit(solution)/shard_map/ppermute | solution.py:474
  27.6 0.9 shard_map.119
  28.5 3.8 %collective-permute-done.2.outer_ref = f32[4,8,1536]{2,1,0:T(8,128)S(1)} collective-permute-done((f32[4,8,1536]{2,1,0:T(8,128)S(1)}, f32[4,8,1536]{2,1,0:T(8,128)S(1)}, u32[]{:S(2)}, u32[]{:S(2)}) %collective-permute-start.2) | collective-permute-done | bytes 196640 | tf_op jit(solution)/shard_map/ppermute | solution.py:474
  32.3 0.6 shard_map.120
  32.9 0.0 copy-start.5
  32.9 0.7 copy-done.5
  33.7 0.7 copy-done.6
  34.4 8.5 %all-to-all-start = ((f32[8,8,1440]{2,1,0:T(8,128)}), f32[8,8,1440]{2,1,0:T(8,128)S(1)}, u32[]{:S(2)}, u32[]{:S(2)}) async-start(f32[8,8,1440]{2,1,0:T(8,128)} %copy-done.5), calls=%async_computation | async-start | bytes 786432 | tf_op jit(solution)/shard_map/all_to_all | solution.py:487
  42.9 4.0 %collective-permute-start.5 = (f32[4,8,1536]{2,1,0:T(8,128)}, f32[4,8,1536]{2,1,0:T(8,128)}, u32[]{:S(2)}, u32[]{:S(2)}) collective-permute-start(f32[4,8,1536]{2,1,0:T(8,128)} %copy-done.12), channel_id=1, source_target_pairs={{0,32},{32,64},{64,96},{96,128},{128,160},{160,192},{192,224},{1,3... | collective-permute-start | bytes 589832 | tf_op jit(solution)/shard_map/ppermute | solution.py:477
  47.0 3.1 %collective-permute-start.8 = (f32[4,8,1536]{2,1,0:T(8,128)}, f32[4,8,1536]{2,1,0:T(8,128)}, u32[]{:S(2)}, u32[]{:S(2)}) collective-permute-start(f32[4,8,1536]{2,1,0:T(8,128)} %copy-done.2), channel_id=1, source_target_pairs={{0,32},{32,64},{64,96},{96,128},{128,160},{160,192},{192,224},{1,3... | collective-permute-start | bytes 589832 | tf_op jit(solution)/shard_map/ppermute | solution.py:463
  50.1 0.2 shard_map.121
  50.3 1.9 %collective-permute-done.8.far_prior_ref = f32[4,8,1536]{2,1,0:T(8,128)} collective-permute-done((f32[4,8,1536]{2,1,0:T(8,128)}, f32[4,8,1536]{2,1,0:T(8,128)}, u32[]{:S(2)}, u32[]{:S(2)}) %collective-permute-start.8) | collective-permute-done | bytes 196640 | tf_op jit(solution)/shard_map/ppermute | solution.py:463
  52.3 1.1 %shard_map.123.own_grad_ref = f32[8,8,1536]{2,1,0:T(8,128)S(1)} custom-call(f32[8,8,1536]{2,1,0:T(8,128)S(1)} %copy-done.7, f32[4,8,1536]{2,1,0:T(8,128)} %collective-permute-done.5.near_prior_ref, f32[4,8,1536]{2,1,0:T(8,128)} %collective-permute-done.8.far_prior_ref, f32[4,8,1536]{2,1,0:T(8,128)S(1)} %copy-done.9, f32[4,8,1536]{2,1,0:T(8,128)S(1)} %copy-done.11, ...), custom_call_target="tpu_custom_call" | custom-call | tf_op jit(solution)/shard_map/pallas_call | solution.py:493
  53.4 0.1 collective-permute-start.9
  53.5 31.3 %all_to_all.10.sums_ref = f32[128,1,128]{2,1,0:T(1,128)S(1)} all-to-all(f32[128,1,128]{2,1,0:T(1,128)S(1)} %shard_map.121), channel_id=1, replica_groups=mesh['tm_0'=2,'tm_1'=4,'lat_0'=8,'lat_1'=2,'ens'=2] {'tm_0','tm_1','lat_..., dimensions={0} | all-to-all | bytes 131072 | tf_op jit(solution)/shard_map/all_to_all | solution.py:495
  84.8 0.1 shard_map.122.sum_ref
  84.9 1.6 %collective-permute-start.7 = (f32[8,128]{1,0:T(8,128)S(1)}, f32[8,128]{1,0:T(8,128)S(1)}, u32[]{:S(2)}, u32[]{:S(2)}) collective-permute-start(f32[8,128]{1,0:T(8,128)S(1)} %shard_map.122.sum_ref), channel_id=1, source_target_pairs={{0,1},{1,0},{2,3},{3,2},{4,5},{5,4},{6,7},{7,6},{8,9},{9,8},{10,11... | collective-permute-start | bytes 12296 | tf_op jit(solution)/shard_map/ppermute | solution.py:497
  86.5 0.8 collective-permute-done.7.other_sum_ref
  87.3 1.4 %shard_map.124 = (f32[1,16,1440]{2,1,0:T(8,128)}, f32[1,8,16,1440]{3,2,1,0:T(8,128)}) custom-call(f32[8,128]{1,0:T(8,128)S(1)} %shard_map.122.sum_ref, f32[8,128]{1,0:T(8,128)S(1)} %collective-permute-done.7.other_sum_ref, f32[16,1,16,1440]{3,2,1,0:T(8,128)S(1)} %copy-done, f32[16,1,16,1440]{3,2,1,0:T(8,128)S(1)} %collective-permute-done.6.other_ref, ...), custom_call_target="tpu_custom_call" | custom-call | tf_op jit(solution)/shard_map/pallas_call | solution.py:498
  (39 shorter events, 0.2 us)
Async XLA Ops:
  0.6 7.7 %copy-start.1 = (f32[1,8,16,1440]{3,2,1,0:T(8,128)S(1)}, f32[1,8,16,1440]{3,2,1,0:T(8,128)}, u32[]{:S(2)}) copy-start(f32[1,8,16,1440]{3,2,1,0:T(8,128)} %inc_hbm.1) | copy-start | bytes 2211844
  0.6 10.6 %copy-start.13 = (f32[1,32,16]{1,2,0:T(8,128)S(1)}, f32[1,32,16]{1,2,0:T(8,128)}, u32[]{:S(2)}) copy-start(f32[1,32,16]{1,2,0:T(8,128)} %param.18) | copy-start | bytes 6148
  0.7 10.6 %copy-start.16 = (f32[8]{0:T(128)S(1)}, f32[8]{0:T(128)}, u32[]{:S(2)}) copy-start(f32[8]{0:T(128)} %prec_ref.1) | copy-start | bytes 100
  0.7 10.6 %copy-start.15 = (s32[1,32]{1,0:T(1,128)S(1)}, s32[1,32]{1,0:T(1,128)}, u32[]{:S(2)}) copy-start(s32[1,32]{1,0:T(1,128)} %rows_hbm.1) | copy-start | bytes 388
  0.7 10.6 %copy-start.17 = (s32[1,32]{1,0:T(1,128)S(1)}, s32[1,32]{1,0:T(1,128)}, u32[]{:S(2)}) copy-start(s32[1,32]{1,0:T(1,128)} %counts_ref.1) | copy-start | bytes 388
  0.7 49.4 %collective-permute-start.6 = (f32[16,1,16,1440]{3,2,1,0:T(8,128)}, f32[16,1,16,1440]{3,2,1,0:T(8,128)S(1)}, u32[]{:S(2)}, u32[]{:S(2)}) collective-permute-start(f32[16,1,16,1440]{3,2,1,0:T(8,128)} %own_ref.3), channel_id=1, source_target_pairs={{0,1},{1,0},{2,3},{3,2},{4,5},{5,4},{6,7},{7,6},{8,9},{9,8},{10,11... | collective-permute-start | bytes 4423688 | tf_op jit(solution)/shard_map/ppermute | solution.py:460
  5.3 14.0 %copy-start.14 = (f32[1,32,16]{1,2,0:T(8,128)S(1)}, f32[1,32,16]{1,2,0:T(8,128)}, u32[]{:S(2)}) copy-start(f32[1,32,16]{1,2,0:T(8,128)} %param.17) | copy-start | bytes 6148
  5.4 14.0 %collective-permute-start = (f32[10,8,1536]{2,1,0:T(8,128)S(1)}, f32[10,8,1536]{2,1,0:T(8,128)S(1)}, u32[]{:S(2)}, u32[]{:S(2)}) collective-permute-start(f32[10,8,1536]{2,1,0:T(8,128)S(1)} %shard_map.115), channel_id=1, source_target_pairs={{1,2},{2,1},{3,4},{4,3},{5,6},{6,5},{7,8},{8,7},{9,10},{10,9},{11,... | collective-permute-start | bytes 1474568 | tf_op jit(solution)/shard_map/ppermute | solution.py:447
  8.6 12.8 %copy-start.8 = (f32[4,8,1536]{2,1,0:T(8,128)}, f32[4,8,1536]{2,1,0:T(8,128)S(1)}, u32[]{:S(2)}) copy-start(f32[4,8,1536]{2,1,0:T(8,128)S(1)} %get-tuple-element.36.near_ref) | copy-start | bytes 589828
  8.6 12.8 %copy-start.10 = (f32[4,8,1536]{2,1,0:T(8,128)}, f32[4,8,1536]{2,1,0:T(8,128)S(1)}, u32[]{:S(2)}) copy-start(f32[4,8,1536]{2,1,0:T(8,128)S(1)} %get-tuple-element.41.far_ref) | copy-start | bytes 589828
  8.6 12.8 %collective-permute-start.3 = (f32[4,8,1536]{2,1,0:T(8,128)S(1)}, f32[4,8,1536]{2,1,0:T(8,128)S(1)}, u32[]{:S(2)}, u32[]{:S(2)}) collective-permute-start(f32[4,8,1536]{2,1,0:T(8,128)S(1)} %get-tuple-element.41.far_ref), channel_id=1, source_target_pairs={{32,0},{64,32},{96,64},{128,96},{160,128},{192,160},{224,192},{33,... | collective-permute-start | bytes 589832 | tf_op jit(solution)/shard_map/ppermute | solution.py:451
  9.9 11.7 %collective-permute-start.1 = (f32[4,8,1536]{2,1,0:T(8,128)S(1)}, f32[4,8,1536]{2,1,0:T(8,128)S(1)}, u32[]{:S(2)}, u32[]{:S(2)}) collective-permute-start(f32[4,8,1536]{2,1,0:T(8,128)S(1)} %get-tuple-element.36.near_ref), channel_id=1, source_target_pairs={{32,0},{64,32},{96,64},{128,96},{160,128},{192,160},{224,192},{33,... | collective-permute-start | bytes 589832 | tf_op jit(solution)/shard_map/ppermute | solution.py:450
  14.7 6.9 %copy-start.2 = (f32[4,8,1536]{2,1,0:T(8,128)}, f32[4,8,1536]{2,1,0:T(8,128)S(1)}, u32[]{:S(2)}) copy-start(f32[4,8,1536]{2,1,0:T(8,128)S(1)} %get-tuple-element.31.far_ref.end_ref) | copy-start | bytes 589828
  14.7 6.9 %copy-start.3 = (f32[8,1536]{1,0:T(8,128)}, f32[8,1536]{1,0:T(8,128)S(1)}, u32[]{:S(2)}) copy-start(f32[8,1536]{1,0:T(8,128)S(1)} %get-tuple-element.37.prec_ref) | copy-start | bytes 147460
  21.4 11.5 %copy-start.12 = (f32[4,8,1536]{2,1,0:T(8,128)}, f32[4,8,1536]{2,1,0:T(8,128)S(1)}, u32[]{:S(2)}) copy-start(f32[4,8,1536]{2,1,0:T(8,128)S(1)} %get-tuple-element.35.end_ref) | copy-start | bytes 589828
  21.5 6.1 %collective-permute-start.4 = (f32[4,8,1536]{2,1,0:T(8,128)S(1)}, f32[4,8,1536]{2,1,0:T(8,128)S(1)}, u32[]{:S(2)}, u32[]{:S(2)}) collective-permute-start(f32[4,8,1536]{2,1,0:T(8,128)S(1)} %get-tuple-element.43), channel_id=1, source_target_pairs={{0,1},{1,0},{2,3},{3,2},{4,5},{5,4},{6,7},{7,6},{8,9},{9,8},{10,11... | collective-permute-start | bytes 589832 | tf_op jit(solution)/shard_map/ppermute | solution.py:476
  21.7 10.6 %collective-permute-start.2 = (f32[4,8,1536]{2,1,0:T(8,128)S(1)}, f32[4,8,1536]{2,1,0:T(8,128)S(1)}, u32[]{:S(2)}, u32[]{:S(2)}) collective-permute-start(f32[4,8,1536]{2,1,0:T(8,128)S(1)} %get-tuple-element.39), channel_id=1, source_target_pairs={{1,2},{2,1},{3,4},{4,3},{5,6},{6,5},{7,8},{8,7},{9,10},{10,9},{11,... | collective-permute-start | bytes 589832 | tf_op jit(solution)/shard_map/ppermute | solution.py:474
  32.3 17.8 %copy-start = (f32[16,1,16,1440]{3,2,1,0:T(8,128)S(1)}, f32[16,1,16,1440]{3,2,1,0:T(8,128)}, u32[]{:S(2)}) copy-start(f32[16,1,16,1440]{3,2,1,0:T(8,128)} %own_ref.3) | copy-start | bytes 4423684
  32.9 0.7 copy-start.5
  33.7 0.7 copy-start.6
  34.4 15.6 %all-to-all-start = ((f32[8,8,1440]{2,1,0:T(8,128)}), f32[8,8,1440]{2,1,0:T(8,128)S(1)}, u32[]{:S(2)}, u32[]{:S(2)}) async-start(f32[8,8,1440]{2,1,0:T(8,128)} %copy-done.5), calls=%async_computation | async-start | bytes 786432 | tf_op jit(solution)/shard_map/all_to_all | solution.py:487
  42.9 7.4 %collective-permute-start.5 = (f32[4,8,1536]{2,1,0:T(8,128)}, f32[4,8,1536]{2,1,0:T(8,128)}, u32[]{:S(2)}, u32[]{:S(2)}) collective-permute-start(f32[4,8,1536]{2,1,0:T(8,128)} %copy-done.12), channel_id=1, source_target_pairs={{0,32},{32,64},{64,96},{96,128},{128,160},{160,192},{192,224},{1,3... | collective-permute-start | bytes 589832 | tf_op jit(solution)/shard_map/ppermute | solution.py:477
  47.0 5.3 %collective-permute-start.8 = (f32[4,8,1536]{2,1,0:T(8,128)}, f32[4,8,1536]{2,1,0:T(8,128)}, u32[]{:S(2)}, u32[]{:S(2)}) collective-permute-start(f32[4,8,1536]{2,1,0:T(8,128)} %copy-done.2), channel_id=1, source_target_pairs={{0,32},{32,64},{64,96},{96,128},{128,160},{160,192},{192,224},{1,3... | collective-permute-start | bytes 589832 | tf_op jit(solution)/shard_map/ppermute | solution.py:463
  50.0 2.2 %copy-start.4 = (f32[8,1536]{1,0:T(8,128)S(1)}, f32[8,1536]{1,0:T(8,128)}, u32[]{:S(2)}) copy-start(f32[8,1536]{1,0:T(8,128)} %copy-done.3) | copy-start | bytes 147460
  50.0 2.2 %copy-start.7 = (f32[8,8,1536]{2,1,0:T(8,128)S(1)}, f32[8,8,1536]{2,1,0:T(8,128)}, u32[]{:S(2)}) copy-start(f32[8,8,1536]{2,1,0:T(8,128)} %copy-done.6) | copy-start | bytes 1179652
  50.1 2.2 %copy-start.9 = (f32[4,8,1536]{2,1,0:T(8,128)S(1)}, f32[4,8,1536]{2,1,0:T(8,128)}, u32[]{:S(2)}) copy-start(f32[4,8,1536]{2,1,0:T(8,128)} %copy-done.8) | copy-start | bytes 589828
  50.1 2.2 %copy-start.11 = (f32[4,8,1536]{2,1,0:T(8,128)S(1)}, f32[4,8,1536]{2,1,0:T(8,128)}, u32[]{:S(2)}) copy-start(f32[4,8,1536]{2,1,0:T(8,128)} %copy-done.10) | copy-start | bytes 589828
  53.4 33.9 %collective-permute-start.9 = (f32[8,8,1536]{2,1,0:T(8,128)S(1)}, f32[8,8,1536]{2,1,0:T(8,128)S(1)}, u32[]{:S(2)}, u32[]{:S(2)}) collective-permute-start(f32[8,8,1536]{2,1,0:T(8,128)S(1)} %shard_map.123.own_grad_ref), channel_id=1, source_target_pairs={{0,1},{1,0},{2,3},{3,2},{4,5},{5,4},{6,7},{7,6},{8,9},{9,8},{10,11... | collective-permute-start | bytes 1179656 | tf_op jit(solution)/shard_map/ppermute | solution.py:494
  84.9 2.4 %collective-permute-start.7 = (f32[8,128]{1,0:T(8,128)S(1)}, f32[8,128]{1,0:T(8,128)S(1)}, u32[]{:S(2)}, u32[]{:S(2)}) collective-permute-start(f32[8,128]{1,0:T(8,128)S(1)} %shard_map.122.sum_ref), channel_id=1, source_target_pairs={{0,1},{1,0},{2,3},{3,2},{4,5},{5,4},{6,7},{7,6},{8,9},{9,8},{10,11... | collective-permute-start | bytes 12296 | tf_op jit(solution)/shard_map/ppermute | solution.py:497

commit v6 on v5

--- a/solution.py
+++ b/solution.py
@@ -38,38 +38,51 @@
     return pltpu.make_async_copy(source.at[0, :, pl.ds(first, size), :], target, sem)
 
 
-def edge_kernel(inc_hbm, lon_hbm, lat_hbm, out_ref, inc, lon, lat, sems):
+def edge_kernel(inc_hbm, lon_hbm, lat_hbm, out_ref, inc, lon, lat, x0, x1, coef, sems):
     core = lax.axis_index("ens")
     lons = inc.shape[-1]
-    levels = inc.shape[0]
-
-    def rows(first, at):
+
+    def rows(first, at, sign):
         copies = [
             fetch(source, first, HALF, target, sems.at[i])
             for i, (source, target) in enumerate(((inc_hbm, inc), (lon_hbm, lon), (lat_hbm, lat)))
         ]
         for copy in copies:
             copy.start()
-        sign = 1.0 if at(0) == 7 else -1.0
-        for i, copy in enumerate(copies):
-            copy.wait()
-            buf = (inc, lon, lat)[i]
-            base = (0, 4, 7)[i]
-            for q in range(4 if i == 0 else 3):
-                r = 3 - q if i == 0 else 2 - q
-                value = buf[:, at(r), :]
-                if i == 2:
-                    value = sign * value
-                out_ref[base + q, :, 0:lons] = value
-                wrap(out_ref.at[base + q], lons)
+        copies[0].wait()
+        for r in range(4):
+            x0[r, :, 0:lons] = inc[:, at(r), :]
+            wrap(x0.at[r], lons)
+        copies[1].wait()
+        copies[2].wait()
+        for r in range(3):
+            coef[1, r, :, 0:lons] = lon[:, at(r), :]
+            wrap(coef.at[1, r], lons)
+            coef[4, r, :, 0:lons] = sign * lat[:, at(r), :]
+            wrap(coef.at[4, r], lons)
+            c, e = coef[1, r], coef[4, r]
+            if r == 0:
+                out_ref[4] = c
+                out_ref[5] = -e
+            if r == 1:
+                out_ref[6] = -e
+            store_coefficients(coef, r, c, e)
+        out_ref[0] = x0[0]
+        for s in range(1, STEPS):
+            src, dst = (x0, x1) if s % 2 else (x1, x0)
+            for r in range(4 - s):
+                f = src[r]
+                value = coef[0, r] * f + coef[1, r] * east(f) + coef[2, r] * west(f) + coef[3, r] * src[r + 1]
+                dst[r] = value + coef[4, r] * src[r - 1] if r else value
+            out_ref[s] = dst[0]
 
     @pl.when(core == 0)
     def _():
-        rows(0, lambda r: r)
+        rows(0, lambda r: r, 1.0)
 
     @pl.when(core == 1)
     def _():
-        rows(HALF, lambda r: 7 - r)
+        rows(HALF, lambda r: 7 - r, -1.0)
 
 
 def own_kernel(inc_ref, near_ref, far_ref, field_ref):
@@ -97,7 +110,7 @@
         self.halo, self.own, self.at = halo_ref, own_ref, at
 
     def __getitem__(self, j):
-        return self.halo[self.at, j] if j < 4 else self.own[self.at, j - 4]
+        return self.halo[self.at, j - 2] if j < 4 else self.own[self.at, j - 4]
 
 
 def forward_step(src, dst, coefs, first, last):
@@ -130,13 +143,44 @@
         done(s, dst)
 
 
-def outer_steps(step_of, bufs, coefs, joint_ref, done):
+def outer_forward(bufs, coefs, joint_ref, halo_ref):
+    center, plon, mlon, plat, mlat = coefs
+    behind = rest = None
     for s in range(1, STEPS + 1):
         src, dst = bufs[(s - 1) % 2], bufs[s % 2]
-        step_of(src, dst, coefs, s, 4 + s)
+        forward_step(src, dst, coefs, 4, 4 + s)
         if s < STEPS:
             dst[4 + s] = joint_ref[s - 1, 0]
             dst[5 + s] = joint_ref[s - 1, 1]
+            value = plat[3] * src[4]
+            if s > 1:
+                value = value + center[3] * rest + plon[3] * east(rest) + mlon[3] * west(rest)
+            if s > 2:
+                value = value + mlat[3] * behind
+            behind = plat[2] * rest if s > 1 else None
+            rest = value
+            dst[3] = halo_ref[s] + rest
+
+
+def outer_adjoint(bufs, coefs, joint_ref, flux_ref, done):
+    center, plon, mlon, plat, mlat = coefs
+    behind = rest = None
+    for s in range(1, STEPS + 1):
+        src, dst = bufs[(s - 1) % 2], bufs[s % 2]
+        g = src[4]
+        flux = flux_ref[s - 1] if s == 1 else flux_ref[s - 1] + plat[3] * rest
+        dst[4] = center[4] * g + west(plon[4] * g) + east(mlon[4] * g) + flux + mlat[5] * src[5]
+        adjoint_step(src, dst, coefs, 5, 4 + s)
+        if s < STEPS:
+            dst[4 + s] = joint_ref[s - 1, 0]
+            dst[5 + s] = joint_ref[s - 1, 1]
+            value = mlat[4] * g
+            if s > 1:
+                value = value + center[3] * rest + west(plon[3] * rest) + east(mlon[3] * rest)
+            if s > 2:
+                value = value + plat[2] * behind
+            behind = mlat[3] * rest if s > 1 else None
+            rest = value
         done(s, dst)
 
 
@@ -211,20 +255,16 @@
     blocks, slots, lons = jac.shape
     rows_copy = pltpu.make_async_copy(rows_hbm, rows, sem)
     rows_copy.start()
-    x0[0:4] = halo_ref[0:4]
+    x0[3] = halo_ref[0]
     x0[4:6] = field_ref[0:2]
-    edge_ref[3, 0] = jnp.ones(x0.shape[1:], jnp.float32)
-    for r in range(3):
-        store_coefficients(edge_ref, 1 + r, halo_ref[4 + r], halo_ref[7 + r])
+    store_coefficients(edge_ref, 1, halo_ref[4], halo_ref[5])
+    lat = halo_ref[6]
+    edge_ref[3, 0] = 0.5 * (lat * lat - lat)
     coefs = [Rows(edge_ref, coef_ref, i) for i in range(5)]
-
-    def done(step, dst):
-        if step == STEPS:
-            end_ref[...] = dst[4:8]
-            dst[8:12] = far_ref[...]
-
-    outer_steps(forward_step, (x0, x1), coefs, joint_ref, done)
+    outer_forward((x0, x1), coefs, joint_ref, halo_ref)
     field = (x0, x1)[STEPS % 2]
+    end_ref[0:4] = field[4:8]
+    end_ref[4:8] = far_ref[...]
     force_ref[...] = jnp.zeros(force_ref.shape, jnp.float32)
 
     rows_copy.wait()
@@ -237,7 +277,7 @@
 
     for j in range(blocks):
         row, lev = place(j)
-        pk[pl.ds(j, 1), :] = field[4 + row, lev, :]
+        pk[pl.ds(j, 1), :] = end_ref[row, lev, :]
     lane = lax.broadcasted_iota(jnp.int32, (slots, blocks), 1)
     ev = jnp.zeros((slots, blocks), jnp.float32)
     for j in range(blocks):
@@ -257,18 +297,30 @@
     return (lax.axis_index(TM) < lax.axis_size(TM) - 1).astype(jnp.float32)
 
 
-def near_kernel(force_ref, end_ref, next_ref, prec_ref, coef_ref, adj_ref, outer_ref):
+def near_kernel(force_ref, end_ref, next_ref, prec_ref, coef_ref, adj_ref, flux_ref, x0, x1):
     prec = prec_ref[...] * with_next()
     for r in range(4):
         adj = force_ref[r] - prec * (next_ref[r] - end_ref[r])
         adj_ref[r] = adj
-        outer_ref[3 - r] = adj * coef_ref[4, 3] if r == 3 else adj
-
-
-def far_kernel(force_ref, end_ref, next_ref, prec_ref, adj_ref, inner_ref):
+        x0[r] = adj
+    center, plon, mlon, plat, mlat = (coef_ref.at[i] for i in range(5))
+    flux_ref[0] = mlat[0] * x0[0]
+    for s in range(1, STEPS):
+        src, dst = (x0, x1) if s % 2 else (x1, x0)
+        for r in range(4 - s):
+            g = src[r]
+            value = center[r] * g + west(plon[r] * g) + east(mlon[r] * g) + mlat[r + 1] * src[r + 1]
+            dst[r] = value + plat[r - 1] * src[r - 1] if r else value
+        flux_ref[s] = mlat[0] * dst[0]
+
+
+def far_kernel(force_ref, end_ref, near_ref, far_ref, prec_ref, later_ref, adj_ref, inner_ref):
     prec = prec_ref[...] * with_next()
     for r in range(4):
-        adj = force_ref[4 + r] - prec * (next_ref[r] - end_ref[r])
+        later_ref[r] = prec * (near_ref[r] - end_ref[r])
+        later = prec * (far_ref[r] - end_ref[4 + r])
+        later_ref[4 + r] = later
+        adj = force_ref[4 + r] - later
         adj_ref[r] = adj
         inner_ref[3 - r] = adj
 
@@ -296,7 +348,6 @@
 ):
     core = lax.axis_index("ens")
     lons = forcing_ref.shape[-1]
-    g0[0:4] = outer_ref[...]
     g0[4:6] = adj_ref[0:2]
     coefs = [Rows(edge_ref, coef_ref, i) for i in range(5)]
     sums[...] = total_ref[0:3]
@@ -309,7 +360,7 @@
             for j in range(4, 4 + step):
                 sums[j - 4] = sums[j - 4] + dst[j]
 
-    outer_steps(adjoint_step, (g0, g1), coefs, joint_ref, done)
+    outer_adjoint((g0, g1), coefs, joint_ref, outer_ref, done)
 
     def store(at):
         for r in range(HALF):
@@ -324,11 +375,12 @@
         store(lambda r: 7 - r)
 
 
-def mismatch_kernel(start_ref, near_prior_ref, far_prior_ref, near_ref, far_ref, prec_ref, grad_ref):
+def mismatch_kernel(start_ref, mismatch_ref, near_ref, far_ref, prec_ref, grad_ref):
+    first_window = lax.axis_index(TM) == 0
     prec = prec_ref[...]
-    for r in range(4):
-        grad_ref[r] = start_ref[r] + prec * (near_ref[r] - near_prior_ref[r])
-        grad_ref[4 + r] = start_ref[4 + r] + prec * (far_ref[r] - far_prior_ref[r])
+    for r in range(HALF):
+        inc = (near_ref if r < 4 else far_ref)[r % 4]
+        grad_ref[r] = start_ref[r] + jnp.where(first_window, prec * inc, mismatch_ref[r])
 
 
 def product_kernel(pieces_ref, own_ref, other_ref, out_ref):
@@ -441,8 +493,12 @@
     piece = buf(levels, HALF, lons)
     whole = buf(levels, band_rows, lons)
 
+    row = buf(4, levels, wide)
     (outgoing,) = call(
-        edge_kernel, [HBM] * 3, [(10, levels, wide)], [piece, piece, piece, pltpu.SemaphoreType.DMA((3,))]
+        edge_kernel,
+        [HBM] * 3,
+        [(7, levels, wide)],
+        [piece, piece, piece, row, row, buf(5, 3, levels, wide), pltpu.SemaphoreType.DMA((3,))],
     )(*(in_hbm(field) for field in fields))
     halo = lax.ppermute(outgoing, band, trade)
     near_rows, far_rows, field = call(own_kernel, [VMEM], [quarter, quarter, (12, levels, wide)])(increment)
@@ -459,23 +515,23 @@
     )(in_hbm(wind_lon), in_hbm(wind_lat), in_hbm(obs_jacobian), field, model_precision, obs_rows, obs_counts, obs_precision[0].T)
     other_pert = lax.ppermute(perturbations, "ens", partner)
 
-    later = [(i, i + 1) for i in range(count_t - 1)]
-    far_prior = lax.ppermute(far, TM, later)
     end, force, edges = call(
         forward_kernel,
         [VMEM] * 6 + [HBM] + [VMEM] * 2,
-        [quarter, own, (5, 4, levels, wide)],
+        [own, own, (5, 2, levels, wide)],
         [
             working, working, buf(blocks, wide), buf(slots, blocks),
             pltpu.SMEM((1, blocks), jnp.int32), pltpu.SemaphoreType.DMA,
         ],
     )(field, coefs, joint_rows, far, halo, jacobian, in_hbm(obs_rows), obs_values[0].T, weight)
-    near, outer = call(near_kernel, [VMEM] * 5, [quarter, quarter])(force, end, next_near, prec, coefs)
+    near, outer = call(near_kernel, [VMEM] * 5, [quarter, quarter], [buf(*quarter), buf(*quarter)])(force, end, next_near, prec, coefs)
     outer = lax.ppermute(outer, band, trade)
-    adj, inner = call(far_kernel, [VMEM] * 4, [quarter, quarter])(force, far, next_far, prec)
+    later, adj, inner = call(far_kernel, [VMEM] * 5, [own, quarter, quarter])(
+        force, end, next_near, next_far, prec
+    )
     inner = lax.ppermute(inner, "ens", partner)
-    near_prior = lax.ppermute(end, TM, later)
-    joint_rows, far_start, total = call(
+    mismatch = lax.ppermute(later, TM, [(i, i + 1) for i in range(count_t - 1)])
+    joint_rows, far, total = call(
         adjoint_inner_kernel, [VMEM] * 4, [joint, quarter, own], [working, working]
     )(near, adj, inner, coefs)
     forcing, start = call(
@@ -483,14 +539,14 @@
         [VMEM] * 7,
         [(levels, HALF, lons), own],
         [working, working, buf(3, levels, wide)],
-    )(near, outer, edges, coefs, joint_rows, far_start, total)
+    )(near, outer, edges, coefs, joint_rows, far, total)
     pieces = lax.all_to_all(forcing, TM, 0, 0, tiled=True)
 
     (products,) = call(product_kernel, [VMEM] * 3, [(count_t * count_l, 1, LANES)])(
         pieces, perturbations, other_pert
     )
-    start, near_prior, products = lax.optimization_barrier((start, near_prior, products))
-    (own_grad,) = call(mismatch_kernel, [VMEM] * 6, [own])(start, near_prior, far_prior, near_rows, far_rows, prec)
+    start, mismatch, products = lax.optimization_barrier((start, mismatch, products))
+    (own_grad,) = call(mismatch_kernel, [VMEM] * 5, [own])(start, mismatch, near_rows, far_rows, prec)
     other_grad = lax.ppermute(own_grad, "ens", partner)
     sums = lax.all_to_all(products, TM_LAT, 0, 0, tiled=True)
     (total,) = call(sum_kernel, [VMEM], [(HALF, LANES)])(sums)

time: 89.2 us -> 78.3 us (0.88)
  starting transfers between devices: 32.2 us -> 19.6 us
  blocking collectives: 31.3 us -> 41.6 us
  waiting for transfers between devices: 11.2 us -> 4.9 us
  local copies, waits for them, and re-layouts: 1.56 us -> 0.04 us
    all_to_all x0 -> x1, blocking collectives: none -> 15.3 us  [on_device(): pieces = lax.all_to_all(forcing, TM, 0, 0, tiled=True)]
    all_to_all x1 -> x0, starting transfers between devices: 8.49 us -> none  [on_device(): pieces = lax.all_to_all(forcing, TM, 0, 0, tiled=True)]
    all_to_all x1, blocking collectives: 31.3 us -> 26.3 us  [on_device(): sums = lax.all_to_all(products, TM_LAT, 0, 0, tiled=True)]
    ppermute x2 -> x1, starting transfers between devices: 7.14 us -> 2.63 us  [on_device(): mismatch = lax.ppermute(later, TM, [(i, i + 1) for i in range(count_t - 1)])]
    ppermute x1, waiting for transfers between devices: 4.64 us -> 1.53 us  [on_device(): halo = lax.ppermute(outgoing, band, trade)]
    ppermute x1, waiting for transfers between devices: 3.81 us -> 1.16 us  [on_device(): outer = lax.ppermute(outer, band, trade)]
    ppermute x2 -> x1, waiting for transfers between devices: 1.94 us -> 0.01 us  [on_device(): mismatch = lax.ppermute(later, TM, [(i, i + 1) for i in range(count_t - 1)])]
    unnamed x36 -> x14, local copies, waits for them, and re-layouts: 1.56 us -> 0.04 us
  transfers between devices with their start and end apart: 11 -> 9, of which waited for: 4 -> 4; matrix products, arithmetic and copies ran while one was open for 0% -> 0% of each run, Pallas kernels for 10% -> 12%
where the time goes in v6:
time: 78.3 us; the launch traced here: 78 us
  blocking collectives  41.6 us (53%)
  starting transfers between devices  19.6 us (25%)
  Pallas kernels  10.9 us (14%)
  waiting for transfers between devices  4.9 us (6%)
  between operations  0.87 us (1%)
    all_to_all x1, blocking collectives, on_device(): sums = lax.all_to_all(products, TM_LAT, 0, 0, tiled=True)  26.3 us
    all_to_all x1, blocking collectives, on_device(): pieces = lax.all_to_all(forcing, TM, 0, 0, tiled=True)  15.3 us
    ppermute x1, starting transfers between devices, on_device(): outer = lax.ppermute(outer, band, trade)  5.75 us
    pallas_call x1, Pallas kernels, on_device(): call(prepare_kernel, [HBM] * 3 + [VMEM, SMEM] + [VMEM] * 3, [(5, 12, leve...  3.46 us
    ppermute x1, starting transfers between devices, on_device(): other_pert = lax.ppermute(perturbations, 'ens', partner)  3.29 us
    ppermute x1, starting transfers between devices, on_device(): halo = lax.ppermute(outgoing, band, trade)  2.99 us
    ppermute x1, starting transfers between devices, on_device(): mismatch = lax.ppermute(later, TM, [(i, i + 1) for i in range(count_t - 1)])  2.63 us
    pallas_call x1, Pallas kernels, on_device(): call(forward_kernel, [VMEM] * 6 + [HBM] + [VMEM] * 2, [own, own, (5, 2, l...  2.01 us
  transfers between devices with their start and end apart: 9, of which 4 were waited for; matrix products, arithmetic and copies ran while one was open for 0% of the time, Pallas kernels for 12%

profile of v6, /device:TPU:1, one launch (start us, length us, event | category | flops | bytes accessed | tf_op | source)
XLA Modules:
  0.0 78.0 jit_solution(11805288622720487264)
XLA Ops:
  0.7 0.0 copy-start.4
  0.7 3.3 %collective-permute-start.6 = (f32[16,1,16,1440]{3,2,1,0:T(8,128)}, f32[16,1,16,1440]{3,2,1,0:T(8,128)S(1)}, u32[]{:S(2)}, u32[]{:S(2)}) collective-permute-start(f32[16,1,16,1440]{3,2,1,0:T(8,128)} %own_ref.3), channel_id=1, source_target_pairs={{0,1},{1,0},{2,3},{3,2},{4,5},{5,4},{6,7},{7,6},{8,9},{9,8},{10,11... | collective-permute-start | bytes 4423688 | tf_op jit(solution)/shard_map/ppermute | solution.py:516
  4.0 1.6 %shard_map.115 = f32[7,8,1536]{2,1,0:T(8,128)S(1)} custom-call(f32[1,8,16,1440]{3,2,1,0:T(8,128)} %inc_hbm.1, f32[1,8,16,1440]{3,2,1,0:T(8,128)} %lon_hbm.3, f32[1,8,16,1440]{3,2,1,0:T(8,128)} %lat_hbm.3), custom_call_target="tpu_custom_call" | custom-call | tf_op jit(solution)/shard_map/pallas_call | solution.py:497
  5.6 0.0 copy-start.3
  5.6 3.0 %collective-permute-start = (f32[7,8,1536]{2,1,0:T(8,128)S(1)}, f32[7,8,1536]{2,1,0:T(8,128)S(1)}, u32[]{:S(2)}, u32[]{:S(2)}) collective-permute-start(f32[7,8,1536]{2,1,0:T(8,128)S(1)} %shard_map.115), channel_id=1, source_target_pairs={{1,2},{2,1},{3,4},{4,3},{5,6},{6,5},{7,8},{8,7},{9,10},{10,9},{11,... | collective-permute-start | bytes 1032200 | tf_op jit(solution)/shard_map/ppermute | solution.py:503
  8.6 0.2 shard_map.113
  8.8 1.3 %collective-permute-start.1 = (f32[4,8,1536]{2,1,0:T(8,128)S(1)}, f32[4,8,1536]{2,1,0:T(8,128)S(1)}, u32[]{:S(2)}, u32[]{:S(2)}) collective-permute-start(f32[4,8,1536]{2,1,0:T(8,128)S(1)} %get-tuple-element.37.near_ref), channel_id=1, source_target_pairs={{32,0},{64,32},{96,64},{128,96},{160,128},{192,160},{224,192},{33,... | collective-permute-start | bytes 589832 | tf_op jit(solution)/shard_map/ppermute | solution.py:506
  10.1 1.3 %collective-permute-start.3 = (f32[4,8,1536]{2,1,0:T(8,128)S(1)}, f32[4,8,1536]{2,1,0:T(8,128)S(1)}, u32[]{:S(2)}, u32[]{:S(2)}) collective-permute-start(f32[4,8,1536]{2,1,0:T(8,128)S(1)} %get-tuple-element.42.far_ref), channel_id=1, source_target_pairs={{32,0},{64,32},{96,64},{128,96},{160,128},{192,160},{224,192},{33,... | collective-permute-start | bytes 589832 | tf_op jit(solution)/shard_map/ppermute | solution.py:507
  11.5 3.5 %shard_map.114 = (f32[5,12,8,1536]{3,2,1,0:T(8,128)S(1)}, f32[8,1536]{1,0:T(8,128)S(1)}, f32[16,32]{1,0:T(8,128)S(1)}, f32[3,2,8,1536]{3,2,1,0:T(8,128)S(1)}, f3...) custom-call(f32[1,8,16,1440]{3,2,1,0:T(8,128)} %lon_hbm.3, f32[1,8,16,1440]{3,2,1,0:T(8,128)} %lat_hbm.3, ...), custom_call_target="tpu_custom_call" | custom-call | tf_op jit(solution)/shard_map/pallas_call | solution.py:510
  14.9 1.5 %collective-permute-done.halo_ref = f32[7,8,1536]{2,1,0:T(8,128)S(1)} collective-permute-done((f32[7,8,1536]{2,1,0:T(8,128)S(1)}, f32[7,8,1536]{2,1,0:T(8,128)S(1)}, u32[]{:S(2)}, u32[]{:S(2)}) %collective-permute-start) | collective-permute-done | bytes 344096 | tf_op jit(solution)/shard_map/ppermute | solution.py:503
  16.5 2.0 %shard_map.116 = (f32[8,8,1536]{2,1,0:T(8,128)S(1)}, f32[8,8,1536]{2,1,0:T(8,128)S(1)}, f32[5,2,8,1536]{3,2,1,0:T(8,128)S(1)}) custom-call(f32[12,8,1536]{2,1,0:T(8,128)S(1)} %get-tuple-element.29.field_ref, f32[5,12,8,1536]{3,2,1,0:T(8,128)S(1)} %get-tuple-element.30.coef_ref, f32[3,2,8,1536]{3,2,1,0:T(8,128)S(1)} %get-tuple-element.31.joint_ref, ...), custom_call_target="tpu_custom_call" | custom-call | tf_op jit(solution)/shard_map/pallas_call | solution.py:518
  18.5 0.0 collective-permute-done.1.next_ref.near_ref
  18.5 1.4 %collective-permute-done.3.far_ref = f32[4,8,1536]{2,1,0:T(8,128)S(1)} collective-permute-done((f32[4,8,1536]{2,1,0:T(8,128)S(1)}, f32[4,8,1536]{2,1,0:T(8,128)S(1)}, u32[]{:S(2)}, u32[]{:S(2)}) %collective-permute-start.3) | collective-permute-done | bytes 196640 | tf_op jit(solution)/shard_map/ppermute | solution.py:507
  19.9 0.1 shard_map.118
  20.0 0.1 collective-permute-start.4
  20.1 0.3 shard_map.117
  20.4 5.8 %collective-permute-start.2 = (f32[4,8,1536]{2,1,0:T(8,128)S(1)}, f32[4,8,1536]{2,1,0:T(8,128)S(1)}, u32[]{:S(2)}, u32[]{:S(2)}) collective-permute-start(f32[4,8,1536]{2,1,0:T(8,128)S(1)} %get-tuple-element.40), channel_id=1, source_target_pairs={{1,2},{2,1},{3,4},{4,3},{5,6},{6,5},{7,8},{8,7},{9,10},{10,9},{11,... | collective-permute-start | bytes 589832 | tf_op jit(solution)/shard_map/ppermute | solution.py:528
  26.1 2.6 %collective-permute-start.5 = (f32[8,8,1536]{2,1,0:T(8,128)S(1)}, f32[8,8,1536]{2,1,0:T(8,128)S(1)}, u32[]{:S(2)}, u32[]{:S(2)}) collective-permute-start(f32[8,8,1536]{2,1,0:T(8,128)S(1)} %get-tuple-element.49), channel_id=1, source_target_pairs={{0,32},{32,64},{64,96},{96,128},{128,160},{160,192},{192,224},{1,3... | collective-permute-start | bytes 1179656 | tf_op jit(solution)/shard_map/ppermute | solution.py:533
  28.8 0.0 collective-permute-done.4.inner_ref
  28.8 0.9 %shard_map.119 = (f32[3,2,8,1536]{3,2,1,0:T(8,128)S(1)}, f32[4,8,1536]{2,1,0:T(8,128)S(1)}, f32[8,8,1536]{2,1,0:T(8,128)S(1)}) custom-call(f32[4,8,1536]{2,1,0:T(8,128)S(1)} %get-tuple-element.39.near_ref.adj_ref, f32[4,8,1536]{2,1,0:T(8,128)S(1)} %get-tuple-element.43.adj_ref, f32[4,8,1536]{2,1,0:T(8,128)S(1)} %collective-permute-done.4.inner_ref, ...), custom_call_target="tpu_custom_call" | custom-call | tf_op jit(solution)/shard_map/pallas_call | solution.py:534
  29.7 0.0 copy-start
  29.7 1.2 %collective-permute-done.2.outer_ref = f32[4,8,1536]{2,1,0:T(8,128)S(1)} collective-permute-done((f32[4,8,1536]{2,1,0:T(8,128)S(1)}, f32[4,8,1536]{2,1,0:T(8,128)S(1)}, u32[]{:S(2)}, u32[]{:S(2)}) %collective-permute-start.2) | collective-permute-done | bytes 196640 | tf_op jit(solution)/shard_map/ppermute | solution.py:528
  30.8 0.5 shard_map.120
  31.4 15.3 %all_to_all.10.pieces_ref = f32[8,8,1440]{2,1,0:T(8,128)S(1)} all-to-all(f32[8,8,1440]{2,1,0:T(8,128)S(1)} %get-tuple-element.50), channel_id=1, replica_groups=mesh['tm_0'=2,'tm_1'=4,'lat_0'=8,'lat_1'=2,'ens'=2] {'tm_0','tm_1'}, dimensions={0} | all-to-all | bytes 737280 | tf_op jit(solution)/shard_map/all_to_all | solution.py:543
  46.7 0.2 shard_map.121
  46.9 0.1 shard_map.123.own_grad_ref
  47.0 0.3 collective-permute-start.8
  47.3 26.3 %all_to_all.11.sums_ref = f32[128,1,128]{2,1,0:T(1,128)S(1)} all-to-all(f32[128,1,128]{2,1,0:T(1,128)S(1)} %shard_map.121), channel_id=1, replica_groups=mesh['tm_0'=2,'tm_1'=4,'lat_0'=8,'lat_1'=2,'ens'=2] {'tm_0','tm_1','lat_..., dimensions={0} | all-to-all | bytes 131072 | tf_op jit(solution)/shard_map/all_to_all | solution.py:551
  73.6 0.1 shard_map.122.sum_ref
  73.8 2.0 %collective-permute-start.7 = (f32[8,128]{1,0:T(8,128)S(1)}, f32[8,128]{1,0:T(8,128)S(1)}, u32[]{:S(2)}, u32[]{:S(2)}) collective-permute-start(f32[8,128]{1,0:T(8,128)S(1)} %shard_map.122.sum_ref), channel_id=1, source_target_pairs={{0,1},{1,0},{2,3},{3,2},{4,5},{5,4},{6,7},{7,6},{8,9},{9,8},{10,11... | collective-permute-start | bytes 12296 | tf_op jit(solution)/shard_map/ppermute | solution.py:553
  75.8 0.8 %collective-permute-done.7.other_sum_ref = f32[8,128]{1,0:T(8,128)S(1)} collective-permute-done((f32[8,128]{1,0:T(8,128)S(1)}, f32[8,128]{1,0:T(8,128)S(1)}, u32[]{:S(2)}, u32[]{:S(2)}) %collective-permute-start.7) | collective-permute-done | bytes 4128 | tf_op jit(solution)/shard_map/ppermute | solution.py:553
  76.6 1.4 %shard_map.124 = (f32[1,16,1440]{2,1,0:T(8,128)}, f32[1,8,16,1440]{3,2,1,0:T(8,128)}) custom-call(f32[8,128]{1,0:T(8,128)S(1)} %shard_map.122.sum_ref, f32[8,128]{1,0:T(8,128)S(1)} %collective-permute-done.7.other_sum_ref, f32[16,1,16,1440]{3,2,1,0:T(8,128)S(1)} %copy-done, f32[16,1,16,1440]{3,2,1,0:T(8,128)S(1)} %collective-permute-done.6.other_ref, ...), custom_call_target="tpu_custom_call" | custom-call | tf_op jit(solution)/shard_map/pallas_call | solution.py:554
  (14 shorter events, 0.0 us)
Async XLA Ops:
  0.6 8.0 %copy-start.1 = (f32[1,8,16,1440]{3,2,1,0:T(8,128)S(1)}, f32[1,8,16,1440]{3,2,1,0:T(8,128)}, u32[]{:S(2)}) copy-start(f32[1,8,16,1440]{3,2,1,0:T(8,128)} %inc_hbm.1) | copy-start | bytes 2211844
  0.6 10.8 %copy-start.2 = (f32[1,32,16]{1,2,0:T(8,128)S(1)}, f32[1,32,16]{1,2,0:T(8,128)}, u32[]{:S(2)}) copy-start(f32[1,32,16]{1,2,0:T(8,128)} %param.18) | copy-start | bytes 6148
  0.7 10.8 %copy-start.5 = (f32[8]{0:T(128)S(1)}, f32[8]{0:T(128)}, u32[]{:S(2)}) copy-start(f32[8]{0:T(128)} %prec_ref.1) | copy-start | bytes 100
  0.7 10.8 %copy-start.4 = (s32[1,32]{1,0:T(1,128)S(1)}, s32[1,32]{1,0:T(1,128)}, u32[]{:S(2)}) copy-start(s32[1,32]{1,0:T(1,128)} %rows_hbm.1) | copy-start | bytes 388
  0.7 10.8 %copy-start.6 = (s32[1,32]{1,0:T(1,128)S(1)}, s32[1,32]{1,0:T(1,128)}, u32[]{:S(2)}) copy-start(s32[1,32]{1,0:T(1,128)} %counts_ref.1) | copy-start | bytes 388
  0.7 46.0 %collective-permute-start.6 = (f32[16,1,16,1440]{3,2,1,0:T(8,128)}, f32[16,1,16,1440]{3,2,1,0:T(8,128)S(1)}, u32[]{:S(2)}, u32[]{:S(2)}) collective-permute-start(f32[16,1,16,1440]{3,2,1,0:T(8,128)} %own_ref.3), channel_id=1, source_target_pairs={{0,1},{1,0},{2,3},{3,2},{4,5},{5,4},{6,7},{7,6},{8,9},{9,8},{10,11... | collective-permute-start | bytes 4423688 | tf_op jit(solution)/shard_map/ppermute | solution.py:516
  5.6 10.9 %copy-start.3 = (f32[1,32,16]{1,2,0:T(8,128)S(1)}, f32[1,32,16]{1,2,0:T(8,128)}, u32[]{:S(2)}) copy-start(f32[1,32,16]{1,2,0:T(8,128)} %param.17) | copy-start | bytes 6148
  5.6 10.9 %collective-permute-start = (f32[7,8,1536]{2,1,0:T(8,128)S(1)}, f32[7,8,1536]{2,1,0:T(8,128)S(1)}, u32[]{:S(2)}, u32[]{:S(2)}) collective-permute-start(f32[7,8,1536]{2,1,0:T(8,128)S(1)} %shard_map.115), channel_id=1, source_target_pairs={{1,2},{2,1},{3,4},{4,3},{5,6},{6,5},{7,8},{8,7},{9,10},{10,9},{11,... | collective-permute-start | bytes 1032200 | tf_op jit(solution)/shard_map/ppermute | solution.py:503
  8.8 9.7 %collective-permute-start.1 = (f32[4,8,1536]{2,1,0:T(8,128)S(1)}, f32[4,8,1536]{2,1,0:T(8,128)S(1)}, u32[]{:S(2)}, u32[]{:S(2)}) collective-permute-start(f32[4,8,1536]{2,1,0:T(8,128)S(1)} %get-tuple-element.37.near_ref), channel_id=1, source_target_pairs={{32,0},{64,32},{96,64},{128,96},{160,128},{192,160},{224,192},{33,... | collective-permute-start | bytes 589832 | tf_op jit(solution)/shard_map/ppermute | solution.py:506
  10.1 9.7 %collective-permute-start.3 = (f32[4,8,1536]{2,1,0:T(8,128)S(1)}, f32[4,8,1536]{2,1,0:T(8,128)S(1)}, u32[]{:S(2)}, u32[]{:S(2)}) collective-permute-start(f32[4,8,1536]{2,1,0:T(8,128)S(1)} %get-tuple-element.42.far_ref), channel_id=1, source_target_pairs={{32,0},{64,32},{96,64},{128,96},{160,128},{192,160},{224,192},{33,... | collective-permute-start | bytes 589832 | tf_op jit(solution)/shard_map/ppermute | solution.py:507
  20.0 8.8 %collective-permute-start.4 = (f32[4,8,1536]{2,1,0:T(8,128)S(1)}, f32[4,8,1536]{2,1,0:T(8,128)S(1)}, u32[]{:S(2)}, u32[]{:S(2)}) collective-permute-start(f32[4,8,1536]{2,1,0:T(8,128)S(1)} %get-tuple-element.44), channel_id=1, source_target_pairs={{0,1},{1,0},{2,3},{3,2},{4,5},{5,4},{6,7},{7,6},{8,9},{9,8},{10,11... | collective-permute-start | bytes 589832 | tf_op jit(solution)/shard_map/ppermute | solution.py:532
  20.4 10.5 %collective-permute-start.2 = (f32[4,8,1536]{2,1,0:T(8,128)S(1)}, f32[4,8,1536]{2,1,0:T(8,128)S(1)}, u32[]{:S(2)}, u32[]{:S(2)}) collective-permute-start(f32[4,8,1536]{2,1,0:T(8,128)S(1)} %get-tuple-element.40), channel_id=1, source_target_pairs={{1,2},{2,1},{3,4},{4,3},{5,6},{6,5},{7,8},{8,7},{9,10},{10,9},{11,... | collective-permute-start | bytes 589832 | tf_op jit(solution)/shard_map/ppermute | solution.py:528
  26.1 20.8 %collective-permute-start.5 = (f32[8,8,1536]{2,1,0:T(8,128)S(1)}, f32[8,8,1536]{2,1,0:T(8,128)S(1)}, u32[]{:S(2)}, u32[]{:S(2)}) collective-permute-start(f32[8,8,1536]{2,1,0:T(8,128)S(1)} %get-tuple-element.49), channel_id=1, source_target_pairs={{0,32},{32,64},{64,96},{96,128},{128,160},{160,192},{192,224},{1,3... | collective-permute-start | bytes 1179656 | tf_op jit(solution)/shard_map/ppermute | solution.py:533
  29.7 17.0 %copy-start = (f32[16,1,16,1440]{3,2,1,0:T(8,128)S(1)}, f32[16,1,16,1440]{3,2,1,0:T(8,128)}, u32[]{:S(2)}) copy-start(f32[16,1,16,1440]{3,2,1,0:T(8,128)} %own_ref.3) | copy-start | bytes 4423684
  47.0 29.6 %collective-permute-start.8 = (f32[8,8,1536]{2,1,0:T(8,128)S(1)}, f32[8,8,1536]{2,1,0:T(8,128)S(1)}, u32[]{:S(2)}, u32[]{:S(2)}) collective-permute-start(f32[8,8,1536]{2,1,0:T(8,128)S(1)} %shard_map.123.own_grad_ref), channel_id=1, source_target_pairs={{0,1},{1,0},{2,3},{3,2},{4,5},{5,4},{6,7},{7,6},{8,9},{9,8},{10,11... | collective-permute-start | bytes 1179656 | tf_op jit(solution)/shard_map/ppermute | solution.py:550
  73.8 2.8 %collective-permute-start.7 = (f32[8,128]{1,0:T(8,128)S(1)}, f32[8,128]{1,0:T(8,128)S(1)}, u32[]{:S(2)}, u32[]{:S(2)}) collective-permute-start(f32[8,128]{1,0:T(8,128)S(1)} %shard_map.122.sum_ref), channel_id=1, source_target_pairs={{0,1},{1,0},{2,3},{3,2},{4,5},{5,4},{6,7},{7,6},{8,9},{9,8},{10,11... | collective-permute-start | bytes 12296 | tf_op jit(solution)/shard_map/ppermute | solution.py:553

commit v7 on v6

--- a/solution.py
+++ b/solution.py
@@ -34,31 +34,29 @@
     )
 
 
-def fetch(source, first, size, target, sem):
-    return pltpu.make_async_copy(source.at[0, :, pl.ds(first, size), :], target, sem)
-
-
 def edge_kernel(inc_hbm, lon_hbm, lat_hbm, out_ref, inc, lon, lat, x0, x1, coef, sems):
     core = lax.axis_index("ens")
     lons = inc.shape[-1]
 
-    def rows(first, at, sign):
-        copies = [
-            fetch(source, first, HALF, target, sems.at[i])
-            for i, (source, target) in enumerate(((inc_hbm, inc), (lon_hbm, lon), (lat_hbm, lat)))
-        ]
+    def rows(at, sign):
+        first = 0 if at(0) == 0 else HALF
+        copies = []
+        for part, start in enumerate((first, HALF - first)):
+            for i, (source, target) in enumerate(((inc_hbm, inc), (lon_hbm, lon), (lat_hbm, lat))):
+                where = (0, slice(None), pl.ds(start, HALF), slice(None))
+                copies.append(pltpu.make_async_copy(source.at[where], target.at[where], sems.at[3 * part + i]))
         for copy in copies:
             copy.start()
         copies[0].wait()
         for r in range(4):
-            x0[r, :, 0:lons] = inc[:, at(r), :]
+            x0[r, :, 0:lons] = inc[0, :, at(r), :]
             wrap(x0.at[r], lons)
         copies[1].wait()
         copies[2].wait()
         for r in range(3):
-            coef[1, r, :, 0:lons] = lon[:, at(r), :]
+            coef[1, r, :, 0:lons] = lon[0, :, at(r), :]
             wrap(coef.at[1, r], lons)
-            coef[4, r, :, 0:lons] = sign * lat[:, at(r), :]
+            coef[4, r, :, 0:lons] = sign * lat[0, :, at(r), :]
             wrap(coef.at[4, r], lons)
             c, e = coef[1, r], coef[4, r]
             if r == 0:
@@ -75,14 +73,16 @@
                 value = coef[0, r] * f + coef[1, r] * east(f) + coef[2, r] * west(f) + coef[3, r] * src[r + 1]
                 dst[r] = value + coef[4, r] * src[r - 1] if r else value
             out_ref[s] = dst[0]
+        for copy in copies[3:]:
+            copy.wait()
 
     @pl.when(core == 0)
     def _():
-        rows(0, lambda r: r, 1.0)
+        rows(lambda r: r, 1.0)
 
     @pl.when(core == 1)
     def _():
-        rows(HALF, lambda r: 7 - r, -1.0)
+        rows(lambda r: 15 - r, -1.0)
 
 
 def own_kernel(inc_ref, near_ref, far_ref, field_ref):
@@ -185,19 +185,13 @@
 
 
 def prepare_kernel(
-    lon_hbm, lat_hbm, jac_hbm, field_ref, prec_ref, rows_ref, counts_ref, oprec_ref,
-    coef_ref, prec_out, weight_ref, joint_ref, end_ref, jac_ref, lon, lat, x0, x1, sems,
+    lon_ref, lat_ref, jac_hbm, field_ref, prec_ref, rows_ref, counts_ref, oprec_ref,
+    coef_ref, prec_out, weight_ref, joint_ref, end_ref, jac_ref, x0, x1, sem,
 ):
     core = lax.axis_index("ens")
-    lons = lon.shape[-1]
-    levels = lon.shape[0]
-    copies = [
-        fetch(source, 0, 2 * HALF, target, sems.at[i])
-        for i, (source, target) in enumerate(((lon_hbm, lon), (lat_hbm, lat)))
-    ]
-    for copy in copies:
-        copy.start()
-    jac_copy = pltpu.make_async_copy(jac_hbm.at[0], jac_ref, sems.at[2])
+    lons = lon_ref.shape[-1]
+    levels = prec_out.shape[0]
+    jac_copy = pltpu.make_async_copy(jac_hbm.at[0], jac_ref, sem)
     jac_copy.start()
     level = lax.broadcasted_iota(jnp.int32, prec_out.shape, 0)
     prec = jnp.zeros(prec_out.shape, jnp.float32)
@@ -207,14 +201,12 @@
     slot = lax.broadcasted_iota(jnp.int32, weight_ref.shape, 0)
     mine = (rows_ref[...] % 16) // HALF == core
     weight_ref[...] = jnp.where((slot < counts_ref[...]) & mine, oprec_ref[...], 0.0)
-    for copy in copies:
-        copy.wait()
 
     def rows(at, sign):
         for r in range(12):
-            coef_ref[1, r, :, 0:lons] = lon[:, at(r), :]
+            coef_ref[1, r, :, 0:lons] = lon_ref[0, :, at(r), :]
             wrap(coef_ref.at[1, r], lons)
-            coef_ref[4, r, :, 0:lons] = sign * lat[:, at(r), :]
+            coef_ref[4, r, :, 0:lons] = sign * lat_ref[0, :, at(r), :]
             wrap(coef_ref.at[4, r], lons)
             store_coefficients(coef_ref, r, coef_ref[1, r], coef_ref[4, r])
 
@@ -403,8 +395,7 @@
     out_ref[...] = jnp.broadcast_to(vec, out_ref.shape)
 
 
-def final_kernel(sum_ref, other_sum_ref, own_ref, other_ref, own_grad_ref, other_grad_ref, out_ref, grad_ref):
-    store_gradient(own_grad_ref, other_grad_ref, grad_ref)
+def step_kernel(sum_ref, other_sum_ref, own_ref, other_ref, out_ref):
     members = own_ref.shape[0]
     lane = lax.broadcasted_iota(jnp.int32, (HALF, LANES), 1)
     theirs = other_sum_ref[...]
@@ -422,7 +413,7 @@
         out_ref[0, rows, :] = total
 
 
-def store_gradient(own_ref, other_ref, out_ref):
+def gradient_kernel(own_ref, other_ref, out_ref):
     core = lax.axis_index("ens")
     lons = out_ref.shape[-1]
 
@@ -490,18 +481,17 @@
     own = (HALF, levels, wide)
     quarter = (4, levels, wide)
     fields = (increment, wind_lon, wind_lat)
-    piece = buf(levels, HALF, lons)
-    whole = buf(levels, band_rows, lons)
 
     row = buf(4, levels, wide)
-    (outgoing,) = call(
+    whole = (1, levels, band_rows, lons)
+    outgoing, inc_band, lon_band, lat_band = call(
         edge_kernel,
         [HBM] * 3,
-        [(7, levels, wide)],
-        [piece, piece, piece, row, row, buf(5, 3, levels, wide), pltpu.SemaphoreType.DMA((3,))],
+        [(7, levels, wide), whole, whole, whole],
+        [row, row, buf(5, 3, levels, wide), pltpu.SemaphoreType.DMA((6,))],
     )(*(in_hbm(field) for field in fields))
     halo = lax.ppermute(outgoing, band, trade)
-    near_rows, far_rows, field = call(own_kernel, [VMEM], [quarter, quarter, (12, levels, wide)])(increment)
+    near_rows, far_rows, field = call(own_kernel, [VMEM], [quarter, quarter, (12, levels, wide)])(inc_band)
     earlier = [(i + 1, i) for i in range(count_t - 1)]
     next_near = lax.ppermute(near_rows, TM, earlier)
     next_far = lax.ppermute(far_rows, TM, earlier)
@@ -509,10 +499,10 @@
     joint = (STEPS - 1, 2, levels, wide)
     coefs, prec, weight, joint_rows, far, jacobian = call(
         prepare_kernel,
-        [HBM] * 3 + [VMEM, SMEM] + [VMEM] * 3,
+        [VMEM, VMEM, HBM, VMEM, SMEM] + [VMEM] * 3,
         [(5, 12, levels, wide), (levels, wide), (slots, blocks), joint, quarter, (blocks, slots, lons)],
-        [whole, whole, working, working, pltpu.SemaphoreType.DMA((3,))],
-    )(in_hbm(wind_lon), in_hbm(wind_lat), in_hbm(obs_jacobian), field, model_precision, obs_rows, obs_counts, obs_precision[0].T)
+        [working, working, pltpu.SemaphoreType.DMA],
+    )(lon_band, lat_band, in_hbm(obs_jacobian), field, model_precision, obs_rows, obs_counts, obs_precision[0].T)
     other_pert = lax.ppermute(perturbations, "ens", partner)
 
     end, force, edges = call(
@@ -551,9 +541,10 @@
     sums = lax.all_to_all(products, TM_LAT, 0, 0, tiled=True)
     (total,) = call(sum_kernel, [VMEM], [(HALF, LANES)])(sums)
     other_total = lax.ppermute(total, "ens", partner)
-    forcing_step, grad_state = call(
-        final_kernel, [VMEM] * 6, [(1, band_rows, lons), (1, levels, band_rows, lons)]
-    )(total, other_total, perturbations, other_pert, own_grad, other_grad)
+    (grad_state,) = call(gradient_kernel, [VMEM] * 2, [whole])(own_grad, other_grad)
+    (forcing_step,) = call(step_kernel, [VMEM] * 4, [(1, band_rows, lons)])(
+        total, other_total, perturbations, other_pert
+    )
     return (grad_state, forcing_step)
 
 

time: 78.3 us -> 79.2 us (1.011)
    ppermute x1, waiting for transfers between devices: 1.53 us -> 2.54 us  [on_device(): halo = lax.ppermute(outgoing, band, trade)]
    pallas_call x4 -> x5, Pallas kernels: 6.69 us -> 6.43 us  [the longest x1 2.44 us: on_device(): call(prepare_kernel, [VMEM, VMEM, HBM, VMEM, SMEM] + [VMEM] * 3, [(5, 12,...]
where the time goes in v7:
time: 79.2 us; the launch traced here: 78.8 us
  blocking collectives  41.8 us (53%)
  starting transfers between devices  19.6 us (25%)
  Pallas kernels  10.9 us (14%)
  waiting for transfers between devices  5.58 us (7%)
  between operations  0.85 us (1%)
    all_to_all x1, blocking collectives, on_device(): sums = lax.all_to_all(products, TM_LAT, 0, 0, tiled=True)  26.5 us
    all_to_all x1, blocking collectives, on_device(): pieces = lax.all_to_all(forcing, TM, 0, 0, tiled=True)  15.2 us
    ppermute x1, starting transfers between devices, on_device(): outer = lax.ppermute(outer, band, trade)  5.76 us
    ppermute x1, starting transfers between devices, on_device(): other_pert = lax.ppermute(perturbations, 'ens', partner)  3.29 us
    ppermute x1, starting transfers between devices, on_device(): halo = lax.ppermute(outgoing, band, trade)  2.85 us
    ppermute x1, starting transfers between devices, on_device(): mismatch = lax.ppermute(later, TM, [(i, i + 1) for i in range(count_t - 1)])  2.76 us
    ppermute x1, waiting for transfers between devices, on_device(): halo = lax.ppermute(outgoing, band, trade)  2.54 us
    pallas_call x1, Pallas kernels, on_device(): call(prepare_kernel, [VMEM, VMEM, HBM, VMEM, SMEM] + [VMEM] * 3, [(5, 12,...  2.44 us
  transfers between devices with their start and end apart: 9, of which 4 were waited for; matrix products, arithmetic and copies ran while one was open for 0% of the time, Pallas kernels for 12%

profile of v7, /device:TPU:1, one launch (start us, length us, event | category | flops | bytes accessed | tf_op | source)
XLA Modules:
  0.0 78.8 jit_solution(5043085527313589931)
XLA Ops:
  0.7 0.0 copy-start.3
  0.7 3.3 %collective-permute-start.6 = (f32[16,1,16,1440]{3,2,1,0:T(8,128)}, f32[16,1,16,1440]{3,2,1,0:T(8,128)S(1)}, u32[]{:S(2)}, u32[]{:S(2)}) collective-permute-start(f32[16,1,16,1440]{3,2,1,0:T(8,128)} %own_ref.3), channel_id=1, source_target_pairs={{0,1},{1,0},{2,3},{3,2},{4,5},{5,4},{6,7},{7,6},{8,9},{9,8},{10,11... | collective-permute-start | bytes 4423688 | tf_op jit(solution)/shard_map/ppermute | solution.py:506
  4.0 1.7 %shard_map.113 = (f32[7,8,1536]{2,1,0:T(8,128)S(1)}, f32[1,8,16,1440]{3,2,1,0:T(8,128)S(1)}, f32[1,8,16,1440]{3,2,1,0:T(8,128)S(1)}, f32[1,8,16,1440]{3,2,1,0:T(8,128)S(1)}) custom-call(f32[1,8,16,1440]{3,2,1,0:T(8,128)} %inc_hbm.1, f32[1,8,16,1440]{3,2,1,0:T(8,128)} %lon_hbm.1, f32[1,8,16,1440]{3,2,1,0:T(8,128)} %lat_hbm.1), custom_call_target="tpu_custom_call" | custom-call | tf_op jit(solution)/shard_map/pallas_call | solution.py:487
  5.6 2.9 %collective-permute-start = (f32[7,8,1536]{2,1,0:T(8,128)S(1)}, f32[7,8,1536]{2,1,0:T(8,128)S(1)}, u32[]{:S(2)}, u32[]{:S(2)}) collective-permute-start(f32[7,8,1536]{2,1,0:T(8,128)S(1)} %get-tuple-element.38), channel_id=1, source_target_pairs={{1,2},{2,1},{3,4},{4,3},{5,6},{6,5},{7,8},{8,7},{9,10},{10,9},{11,... | collective-permute-start | bytes 1032200 | tf_op jit(solution)/shard_map/ppermute | solution.py:493
  8.5 0.0 copy-start.2
  8.5 0.2 shard_map.114
  8.7 1.3 %collective-permute-start.1 = (f32[4,8,1536]{2,1,0:T(8,128)S(1)}, f32[4,8,1536]{2,1,0:T(8,128)S(1)}, u32[]{:S(2)}, u32[]{:S(2)}) collective-permute-start(f32[4,8,1536]{2,1,0:T(8,128)S(1)} %get-tuple-element.43.near_ref), channel_id=1, source_target_pairs={{32,0},{64,32},{96,64},{128,96},{160,128},{192,160},{224,192},{33,... | collective-permute-start | bytes 589832 | tf_op jit(solution)/shard_map/ppermute | solution.py:496
  10.0 1.3 %collective-permute-start.3 = (f32[4,8,1536]{2,1,0:T(8,128)S(1)}, f32[4,8,1536]{2,1,0:T(8,128)S(1)}, u32[]{:S(2)}, u32[]{:S(2)}) collective-permute-start(f32[4,8,1536]{2,1,0:T(8,128)S(1)} %get-tuple-element.48.far_ref), channel_id=1, source_target_pairs={{32,0},{64,32},{96,64},{128,96},{160,128},{192,160},{224,192},{33,... | collective-permute-start | bytes 589832 | tf_op jit(solution)/shard_map/ppermute | solution.py:497
  11.4 2.4 %shard_map.115 = (f32[5,12,8,1536]{3,2,1,0:T(8,128)S(1)}, f32[8,1536]{1,0:T(8,128)S(1)}, f32[16,32]{1,0:T(8,128)S(1)}, f32[3,2,8,1536]{3,2,1,0:T(8,128)S(1)}, f3...) custom-call(f32[1,8,16,1440]{3,2,1,0:T(8,128)S(1)} %get-tuple-element.33.lon_ref, ...), custom_call_target="tpu_custom_call" | custom-call | tf_op jit(solution)/shard_map/pallas_call | solution.py:500
  13.8 2.5 %collective-permute-done.halo_ref = f32[7,8,1536]{2,1,0:T(8,128)S(1)} collective-permute-done((f32[7,8,1536]{2,1,0:T(8,128)S(1)}, f32[7,8,1536]{2,1,0:T(8,128)S(1)}, u32[]{:S(2)}, u32[]{:S(2)}) %collective-permute-start) | collective-permute-done | bytes 344096 | tf_op jit(solution)/shard_map/ppermute | solution.py:493
  16.4 2.0 %shard_map.116 = (f32[8,8,1536]{2,1,0:T(8,128)S(1)}, f32[8,8,1536]{2,1,0:T(8,128)S(1)}, f32[5,2,8,1536]{3,2,1,0:T(8,128)S(1)}) custom-call(f32[12,8,1536]{2,1,0:T(8,128)S(1)} %get-tuple-element.32.field_ref, f32[5,12,8,1536]{3,2,1,0:T(8,128)S(1)} %get-tuple-element.35.coef_ref, f32[3,2,8,1536]{3,2,1,0:T(8,128)S(1)} %get-tuple-element.36.joint_ref, ...), custom_call_target="tpu_custom_call" | custom-call | tf_op jit(solution)/shard_map/pallas_call | solution.py:508
  18.4 0.0 collective-permute-done.1.next_ref.near_ref
  18.4 1.4 %collective-permute-done.3.far_ref = f32[4,8,1536]{2,1,0:T(8,128)S(1)} collective-permute-done((f32[4,8,1536]{2,1,0:T(8,128)S(1)}, f32[4,8,1536]{2,1,0:T(8,128)S(1)}, u32[]{:S(2)}, u32[]{:S(2)}) %collective-permute-start.3) | collective-permute-done | bytes 196640 | tf_op jit(solution)/shard_map/ppermute | solution.py:497
  19.8 0.1 shard_map.118
  19.8 0.1 collective-permute-start.4
  19.9 0.3 shard_map.117
  20.2 5.8 %collective-permute-start.2 = (f32[4,8,1536]{2,1,0:T(8,128)S(1)}, f32[4,8,1536]{2,1,0:T(8,128)S(1)}, u32[]{:S(2)}, u32[]{:S(2)}) collective-permute-start(f32[4,8,1536]{2,1,0:T(8,128)S(1)} %get-tuple-element.46), channel_id=1, source_target_pairs={{1,2},{2,1},{3,4},{4,3},{5,6},{6,5},{7,8},{8,7},{9,10},{10,9},{11,... | collective-permute-start | bytes 589832 | tf_op jit(solution)/shard_map/ppermute | solution.py:518
  26.0 2.8 %collective-permute-start.5 = (f32[8,8,1536]{2,1,0:T(8,128)S(1)}, f32[8,8,1536]{2,1,0:T(8,128)S(1)}, u32[]{:S(2)}, u32[]{:S(2)}) collective-permute-start(f32[8,8,1536]{2,1,0:T(8,128)S(1)} %get-tuple-element.55), channel_id=1, source_target_pairs={{0,32},{32,64},{64,96},{96,128},{128,160},{160,192},{192,224},{1,3... | collective-permute-start | bytes 1179656 | tf_op jit(solution)/shard_map/ppermute | solution.py:523
  28.8 1.1 %shard_map.119 = (f32[3,2,8,1536]{3,2,1,0:T(8,128)S(1)}, f32[4,8,1536]{2,1,0:T(8,128)S(1)}, f32[8,8,1536]{2,1,0:T(8,128)S(1)}) custom-call(f32[4,8,1536]{2,1,0:T(8,128)S(1)} %get-tuple-element.45.near_ref.adj_ref, f32[4,8,1536]{2,1,0:T(8,128)S(1)} %get-tuple-element.49.adj_ref, f32[4,8,1536]{2,1,0:T(8,128)S(1)} %collective-permute-done.4.inner_ref, ...), custom_call_target="tpu_custom_call" | custom-call | tf_op jit(solution)/shard_map/pallas_call | solution.py:524
  29.9 0.0 copy-start
  29.9 0.8 %collective-permute-done.2.outer_ref = f32[4,8,1536]{2,1,0:T(8,128)S(1)} collective-permute-done((f32[4,8,1536]{2,1,0:T(8,128)S(1)}, f32[4,8,1536]{2,1,0:T(8,128)S(1)}, u32[]{:S(2)}, u32[]{:S(2)}) %collective-permute-start.2) | collective-permute-done | bytes 196640 | tf_op jit(solution)/shard_map/ppermute | solution.py:518
  30.7 0.6 shard_map.120
  31.3 15.2 %all_to_all.10.pieces_ref = f32[8,8,1440]{2,1,0:T(8,128)S(1)} all-to-all(f32[8,8,1440]{2,1,0:T(8,128)S(1)} %get-tuple-element.56), channel_id=1, replica_groups=mesh['tm_0'=2,'tm_1'=4,'lat_0'=8,'lat_1'=2,'ens'=2] {'tm_0','tm_1'}, dimensions={0} | all-to-all | bytes 737280 | tf_op jit(solution)/shard_map/all_to_all | solution.py:533
  46.5 0.2 shard_map.121
  46.8 0.1 shard_map.122.own_ref
  46.9 0.3 collective-permute-start.7
  47.2 26.5 %all_to_all.11.sums_ref = f32[128,1,128]{2,1,0:T(1,128)S(1)} all-to-all(f32[128,1,128]{2,1,0:T(1,128)S(1)} %shard_map.121), channel_id=1, replica_groups=mesh['tm_0'=2,'tm_1'=4,'lat_0'=8,'lat_1'=2,'ens'=2] {'tm_0','tm_1','lat_..., dimensions={0} | all-to-all | bytes 131072 | tf_op jit(solution)/shard_map/all_to_all | solution.py:541
  73.7 0.1 shard_map.124.sum_ref
  73.9 2.0 %collective-permute-start.8 = (f32[8,128]{1,0:T(8,128)S(1)}, f32[8,128]{1,0:T(8,128)S(1)}, u32[]{:S(2)}, u32[]{:S(2)}) collective-permute-start(f32[8,128]{1,0:T(8,128)S(1)} %shard_map.124.sum_ref), channel_id=1, source_target_pairs={{0,1},{1,0},{2,3},{3,2},{4,5},{5,4},{6,7},{7,6},{8,9},{9,8},{10,11... | collective-permute-start | bytes 12296 | tf_op jit(solution)/shard_map/ppermute | solution.py:543
  75.8 0.8 %collective-permute-done.8.other_sum_ref = f32[8,128]{1,0:T(8,128)S(1)} collective-permute-done((f32[8,128]{1,0:T(8,128)S(1)}, f32[8,128]{1,0:T(8,128)S(1)}, u32[]{:S(2)}, u32[]{:S(2)}) %collective-permute-start.8) | collective-permute-done | bytes 4128 | tf_op jit(solution)/shard_map/ppermute | solution.py:543
  76.7 1.0 %shard_map.125 = f32[1,16,1440]{2,1,0:T(8,128)} custom-call(f32[8,128]{1,0:T(8,128)S(1)} %shard_map.124.sum_ref, f32[8,128]{1,0:T(8,128)S(1)} %collective-permute-done.8.other_sum_ref, f32[16,1,16,1440]{3,2,1,0:T(8,128)S(1)} %copy-done, f32[16,1,16,1440]{3,2,1,0:T(8,128)S(1)} %collective-permute-done.6.other_ref), custom_call_target="tpu_custom_call" | custom-call | tf_op jit(solution)/shard_map/pallas_call | solution.py:545
  77.7 1.1 %shard_map.123 = f32[1,8,16,1440]{3,2,1,0:T(8,128)} custom-call(f32[8,8,1536]{2,1,0:T(8,128)S(1)} %shard_map.122.own_ref, f32[8,8,1536]{2,1,0:T(8,128)S(1)} %collective-permute-done.7.other_ref), custom_call_target="tpu_custom_call" | custom-call | tf_op jit(solution)/shard_map/pallas_call | solution.py:544
  (13 shorter events, 0.0 us)
Async XLA Ops:
  0.6 10.7 %copy-start.1 = (f32[1,32,16]{1,2,0:T(8,128)S(1)}, f32[1,32,16]{1,2,0:T(8,128)}, u32[]{:S(2)}) copy-start(f32[1,32,16]{1,2,0:T(8,128)} %param.18) | copy-start | bytes 6148
  0.6 10.7 %copy-start.4 = (f32[8]{0:T(128)S(1)}, f32[8]{0:T(128)}, u32[]{:S(2)}) copy-start(f32[8]{0:T(128)} %prec_ref.1) | copy-start | bytes 100
  0.7 10.7 %copy-start.3 = (s32[1,32]{1,0:T(1,128)S(1)}, s32[1,32]{1,0:T(1,128)}, u32[]{:S(2)}) copy-start(s32[1,32]{1,0:T(1,128)} %rows_hbm.1) | copy-start | bytes 388
  0.7 10.7 %copy-start.5 = (s32[1,32]{1,0:T(1,128)S(1)}, s32[1,32]{1,0:T(1,128)}, u32[]{:S(2)}) copy-start(s32[1,32]{1,0:T(1,128)} %counts_ref.1) | copy-start | bytes 388
  0.7 45.9 %collective-permute-start.6 = (f32[16,1,16,1440]{3,2,1,0:T(8,128)}, f32[16,1,16,1440]{3,2,1,0:T(8,128)S(1)}, u32[]{:S(2)}, u32[]{:S(2)}) collective-permute-start(f32[16,1,16,1440]{3,2,1,0:T(8,128)} %own_ref.3), channel_id=1, source_target_pairs={{0,1},{1,0},{2,3},{3,2},{4,5},{5,4},{6,7},{7,6},{8,9},{9,8},{10,11... | collective-permute-start | bytes 4423688 | tf_op jit(solution)/shard_map/ppermute | solution.py:506
  5.6 10.7 %collective-permute-start = (f32[7,8,1536]{2,1,0:T(8,128)S(1)}, f32[7,8,1536]{2,1,0:T(8,128)S(1)}, u32[]{:S(2)}, u32[]{:S(2)}) collective-permute-start(f32[7,8,1536]{2,1,0:T(8,128)S(1)} %get-tuple-element.38), channel_id=1, source_target_pairs={{1,2},{2,1},{3,4},{4,3},{5,6},{6,5},{7,8},{8,7},{9,10},{10,9},{11,... | collective-permute-start | bytes 1032200 | tf_op jit(solution)/shard_map/ppermute | solution.py:493
  8.5 7.9 %copy-start.2 = (f32[1,32,16]{1,2,0:T(8,128)S(1)}, f32[1,32,16]{1,2,0:T(8,128)}, u32[]{:S(2)}) copy-start(f32[1,32,16]{1,2,0:T(8,128)} %param.17) | copy-start | bytes 6148
  8.7 9.7 %collective-permute-start.1 = (f32[4,8,1536]{2,1,0:T(8,128)S(1)}, f32[4,8,1536]{2,1,0:T(8,128)S(1)}, u32[]{:S(2)}, u32[]{:S(2)}) collective-permute-start(f32[4,8,1536]{2,1,0:T(8,128)S(1)} %get-tuple-element.43.near_ref), channel_id=1, source_target_pairs={{32,0},{64,32},{96,64},{128,96},{160,128},{192,160},{224,192},{33,... | collective-permute-start | bytes 589832 | tf_op jit(solution)/shard_map/ppermute | solution.py:496
  10.0 9.7 %collective-permute-start.3 = (f32[4,8,1536]{2,1,0:T(8,128)S(1)}, f32[4,8,1536]{2,1,0:T(8,128)S(1)}, u32[]{:S(2)}, u32[]{:S(2)}) collective-permute-start(f32[4,8,1536]{2,1,0:T(8,128)S(1)} %get-tuple-element.48.far_ref), channel_id=1, source_target_pairs={{32,0},{64,32},{96,64},{128,96},{160,128},{192,160},{224,192},{33,... | collective-permute-start | bytes 589832 | tf_op jit(solution)/shard_map/ppermute | solution.py:497
  19.8 8.9 %collective-permute-start.4 = (f32[4,8,1536]{2,1,0:T(8,128)S(1)}, f32[4,8,1536]{2,1,0:T(8,128)S(1)}, u32[]{:S(2)}, u32[]{:S(2)}) collective-permute-start(f32[4,8,1536]{2,1,0:T(8,128)S(1)} %get-tuple-element.50), channel_id=1, source_target_pairs={{0,1},{1,0},{2,3},{3,2},{4,5},{5,4},{6,7},{7,6},{8,9},{9,8},{10,11... | collective-permute-start | bytes 589832 | tf_op jit(solution)/shard_map/ppermute | solution.py:522
  20.2 10.5 %collective-permute-start.2 = (f32[4,8,1536]{2,1,0:T(8,128)S(1)}, f32[4,8,1536]{2,1,0:T(8,128)S(1)}, u32[]{:S(2)}, u32[]{:S(2)}) collective-permute-start(f32[4,8,1536]{2,1,0:T(8,128)S(1)} %get-tuple-element.46), channel_id=1, source_target_pairs={{1,2},{2,1},{3,4},{4,3},{5,6},{6,5},{7,8},{8,7},{9,10},{10,9},{11,... | collective-permute-start | bytes 589832 | tf_op jit(solution)/shard_map/ppermute | solution.py:518
  26.0 20.8 %collective-permute-start.5 = (f32[8,8,1536]{2,1,0:T(8,128)S(1)}, f32[8,8,1536]{2,1,0:T(8,128)S(1)}, u32[]{:S(2)}, u32[]{:S(2)}) collective-permute-start(f32[8,8,1536]{2,1,0:T(8,128)S(1)} %get-tuple-element.55), channel_id=1, source_target_pairs={{0,32},{32,64},{64,96},{96,128},{128,160},{160,192},{192,224},{1,3... | collective-permute-start | bytes 1179656 | tf_op jit(solution)/shard_map/ppermute | solution.py:523
  29.9 16.7 %copy-start = (f32[16,1,16,1440]{3,2,1,0:T(8,128)S(1)}, f32[16,1,16,1440]{3,2,1,0:T(8,128)}, u32[]{:S(2)}) copy-start(f32[16,1,16,1440]{3,2,1,0:T(8,128)} %own_ref.3) | copy-start | bytes 4423684
  46.9 30.8 %collective-permute-start.7 = (f32[8,8,1536]{2,1,0:T(8,128)S(1)}, f32[8,8,1536]{2,1,0:T(8,128)S(1)}, u32[]{:S(2)}, u32[]{:S(2)}) collective-permute-start(f32[8,8,1536]{2,1,0:T(8,128)S(1)} %shard_map.122.own_ref), channel_id=1, source_target_pairs={{0,1},{1,0},{2,3},{3,2},{4,5},{5,4},{6,7},{7,6},{8,9},{9,8},{10,11... | collective-permute-start | bytes 1179656 | tf_op jit(solution)/shard_map/ppermute | solution.py:540
  73.9 2.8 %collective-permute-start.8 = (f32[8,128]{1,0:T(8,128)S(1)}, f32[8,128]{1,0:T(8,128)S(1)}, u32[]{:S(2)}, u32[]{:S(2)}) collective-permute-start(f32[8,128]{1,0:T(8,128)S(1)} %shard_map.124.sum_ref), channel_id=1, source_target_pairs={{0,1},{1,0},{2,3},{3,2},{4,5},{5,4},{6,7},{7,6},{8,9},{9,8},{10,11... | collective-permute-start | bytes 12296 | tf_op jit(solution)/shard_map/ppermute | solution.py:543

commit v8 on v7

--- a/solution.py
+++ b/solution.py
@@ -12,7 +12,7 @@
 HALF = 8
 TM = ("tm_0", "tm_1")
 LAT = ("lat_0", "lat_1")
-TM_LAT = ("tm_0", "tm_1", "lat_0", "lat_1")
+LAT_TM = ("lat_0", "lat_1", "tm_0", "tm_1")
 
 
 def east(value):
@@ -34,7 +34,39 @@
     )
 
 
-def edge_kernel(inc_hbm, lon_hbm, lat_hbm, out_ref, inc, lon, lat, x0, x1, coef, sems):
+def pack(ref, count, lons, out_ref):
+    full, tail = lons // LANES, lons % LANES
+    share = LANES // tail
+    lane = lax.broadcasted_iota(jnp.int32, (HALF, LANES), 1)
+    for r in range(count):
+        for i in range(full):
+            out_ref[full * r + i] = ref[r, :, LANES * i : LANES * (i + 1)]
+    for first in range(0, count, share):
+        ends = ref[first, :, full * LANES :]
+        for q in range(1, min(share, count - first)):
+            end = pltpu.roll(ref[first + q, :, full * LANES :], tail * q, 1)
+            ends = jnp.where(lane < tail * q, ends, end)
+        out_ref[full * count + first // share] = ends
+
+
+def unpack(in_ref, count, lons, ref):
+    full, tail = lons // LANES, lons % LANES
+    share = LANES // tail
+    for r in range(count):
+        for i in range(full):
+            ref[r, :, LANES * i : LANES * (i + 1)] = in_ref[full * r + i]
+        ends = in_ref[full * count + r // share]
+        q = r % share
+        ref[r, :, full * LANES :] = pltpu.roll(ends, LANES - tail * q, 1) if q else ends
+        wrap(ref.at[r], lons)
+
+
+def tiles(count, levels, lons):
+    share = LANES // (lons % LANES)
+    return (lons // LANES * count + -(-count // share), levels, LANES)
+
+
+def edge_kernel(inc_hbm, lon_hbm, lat_hbm, packed_ref, inc, lon, lat, out_ref, x0, x1, coef, sems):
     core = lax.axis_index("ens")
     lons = inc.shape[-1]
 
@@ -73,6 +105,7 @@
                 value = coef[0, r] * f + coef[1, r] * east(f) + coef[2, r] * west(f) + coef[3, r] * src[r + 1]
                 dst[r] = value + coef[4, r] * src[r - 1] if r else value
             out_ref[s] = dst[0]
+        pack(out_ref, 7, lons, packed_ref)
         for copy in copies[3:]:
             copy.wait()
 
@@ -85,7 +118,7 @@
         rows(lambda r: 15 - r, -1.0)
 
 
-def own_kernel(inc_ref, near_ref, far_ref, field_ref):
+def own_kernel(inc_ref, near_ref, far_ref, near_packed, far_packed, field_ref):
     core = lax.axis_index("ens")
     lons = inc_ref.shape[-1]
 
@@ -103,6 +136,9 @@
     @pl.when(core == 1)
     def _():
         rows(lambda r: 15 - r)
+
+    pack(near_ref, 4, lons, near_packed)
+    pack(far_ref, 4, lons, far_packed)
 
 
 class Rows:
@@ -240,13 +276,14 @@
 
 
 def forward_kernel(
-    field_ref, coef_ref, joint_ref, far_ref, halo_ref, jac, rows_hbm, val_ref, weight_ref,
-    end_ref, force_ref, edge_ref, x0, x1, pk, wgt, rows, sem,
+    field_ref, coef_ref, joint_ref, far_ref, packed_ref, jac, rows_hbm, val_ref, weight_ref,
+    end_ref, force_ref, edge_ref, halo_ref, x0, x1, pk, wgt, rows, sem,
 ):
     core = lax.axis_index("ens")
     blocks, slots, lons = jac.shape
     rows_copy = pltpu.make_async_copy(rows_hbm, rows, sem)
     rows_copy.start()
+    unpack(packed_ref, 7, lons, halo_ref)
     x0[3] = halo_ref[0]
     x0[4:6] = field_ref[0:2]
     store_coefficients(edge_ref, 1, halo_ref[4], halo_ref[5])
@@ -289,10 +326,14 @@
     return (lax.axis_index(TM) < lax.axis_size(TM) - 1).astype(jnp.float32)
 
 
-def near_kernel(force_ref, end_ref, next_ref, prec_ref, coef_ref, adj_ref, flux_ref, x0, x1):
+def near_kernel(force_ref, end_ref, packed_ref, prec_ref, coef_ref, adj_ref, flux_packed, later_ref, next_ref, flux_ref, x0, x1):
+    lons = 1440
+    unpack(packed_ref, 4, lons, next_ref)
     prec = prec_ref[...] * with_next()
     for r in range(4):
-        adj = force_ref[r] - prec * (next_ref[r] - end_ref[r])
+        later = prec * (next_ref[r] - end_ref[r])
+        later_ref[r] = later
+        adj = force_ref[r] - later
         adj_ref[r] = adj
         x0[r] = adj
     center, plon, mlon, plat, mlat = (coef_ref.at[i] for i in range(5))
@@ -304,13 +345,15 @@
             value = center[r] * g + west(plon[r] * g) + east(mlon[r] * g) + mlat[r + 1] * src[r + 1]
             dst[r] = value + plat[r - 1] * src[r - 1] if r else value
         flux_ref[s] = mlat[0] * dst[0]
-
-
-def far_kernel(force_ref, end_ref, near_ref, far_ref, prec_ref, later_ref, adj_ref, inner_ref):
+    pack(flux_ref, 4, lons, flux_packed)
+
+
+def far_kernel(force_ref, end_ref, near_ref, packed_ref, prec_ref, later_ref, adj_ref, inner_ref, next_ref):
+    unpack(packed_ref, 4, 1440, next_ref)
     prec = prec_ref[...] * with_next()
     for r in range(4):
-        later_ref[r] = prec * (near_ref[r] - end_ref[r])
-        later = prec * (far_ref[r] - end_ref[4 + r])
+        later_ref[r] = near_ref[r]
+        later = prec * (next_ref[r] - end_ref[4 + r])
         later_ref[4 + r] = later
         adj = force_ref[4 + r] - later
         adj_ref[r] = adj
@@ -336,10 +379,11 @@
 
 
 def adjoint_kernel(
-    adj_ref, outer_ref, edge_ref, coef_ref, joint_ref, far_ref, total_ref, forcing_ref, start_ref, g0, g1, sums
+    adj_ref, packed_ref, edge_ref, coef_ref, joint_ref, far_ref, total_ref, forcing_ref, start_ref, outer_ref, g0, g1, sums
 ):
     core = lax.axis_index("ens")
     lons = forcing_ref.shape[-1]
+    unpack(packed_ref, 4, lons, outer_ref)
     g0[4:6] = adj_ref[0:2]
     coefs = [Rows(edge_ref, coef_ref, i) for i in range(5)]
     sums[...] = total_ref[0:3]
@@ -487,14 +531,16 @@
     outgoing, inc_band, lon_band, lat_band = call(
         edge_kernel,
         [HBM] * 3,
-        [(7, levels, wide), whole, whole, whole],
-        [row, row, buf(5, 3, levels, wide), pltpu.SemaphoreType.DMA((6,))],
+        [tiles(7, levels, lons), whole, whole, whole],
+        [buf(7, levels, wide), row, row, buf(5, 3, levels, wide), pltpu.SemaphoreType.DMA((6,))],
     )(*(in_hbm(field) for field in fields))
     halo = lax.ppermute(outgoing, band, trade)
-    near_rows, far_rows, field = call(own_kernel, [VMEM], [quarter, quarter, (12, levels, wide)])(inc_band)
+    packed = tiles(4, levels, lons)
+    near_rows, far_rows, near_packed, far_packed, field = call(
+        own_kernel, [VMEM], [quarter, quarter, packed, packed, (12, levels, wide)]
+    )(inc_band)
     earlier = [(i + 1, i) for i in range(count_t - 1)]
-    next_near = lax.ppermute(near_rows, TM, earlier)
-    next_far = lax.ppermute(far_rows, TM, earlier)
+    next_near = lax.ppermute(near_packed, TM, earlier)
     working = buf(16, levels, wide)
     joint = (STEPS - 1, 2, levels, wide)
     coefs, prec, weight, joint_rows, far, jacobian = call(
@@ -505,19 +551,21 @@
     )(lon_band, lat_band, in_hbm(obs_jacobian), field, model_precision, obs_rows, obs_counts, obs_precision[0].T)
     other_pert = lax.ppermute(perturbations, "ens", partner)
 
+    far_packed, far = lax.optimization_barrier((far_packed, far))
+    next_far = lax.ppermute(far_packed, TM, earlier)
     end, force, edges = call(
         forward_kernel,
         [VMEM] * 6 + [HBM] + [VMEM] * 2,
         [own, own, (5, 2, levels, wide)],
         [
-            working, working, buf(blocks, wide), buf(slots, blocks),
+            buf(7, levels, wide), working, working, buf(blocks, wide), buf(slots, blocks),
             pltpu.SMEM((1, blocks), jnp.int32), pltpu.SemaphoreType.DMA,
         ],
     )(field, coefs, joint_rows, far, halo, jacobian, in_hbm(obs_rows), obs_values[0].T, weight)
-    near, outer = call(near_kernel, [VMEM] * 5, [quarter, quarter], [buf(*quarter), buf(*quarter)])(force, end, next_near, prec, coefs)
+    near, outer, later = call(near_kernel, [VMEM] * 5, [quarter, packed, quarter], [buf(*quarter)] * 4)(force, end, next_near, prec, coefs)
     outer = lax.ppermute(outer, band, trade)
-    later, adj, inner = call(far_kernel, [VMEM] * 5, [own, quarter, quarter])(
-        force, end, next_near, next_far, prec
+    later, adj, inner = call(far_kernel, [VMEM] * 5, [own, quarter, quarter], [buf(*quarter)])(
+        force, end, later, next_far, prec
     )
     inner = lax.ppermute(inner, "ens", partner)
     mismatch = lax.ppermute(later, TM, [(i, i + 1) for i in range(count_t - 1)])
@@ -528,7 +576,7 @@
         adjoint_kernel,
         [VMEM] * 7,
         [(levels, HALF, lons), own],
-        [working, working, buf(3, levels, wide)],
+        [buf(*quarter), working, working, buf(3, levels, wide)],
     )(near, outer, edges, coefs, joint_rows, far, total)
     pieces = lax.all_to_all(forcing, TM, 0, 0, tiled=True)
 
@@ -538,7 +586,7 @@
     start, mismatch, products = lax.optimization_barrier((start, mismatch, products))
     (own_grad,) = call(mismatch_kernel, [VMEM] * 5, [own])(start, mismatch, near_rows, far_rows, prec)
     other_grad = lax.ppermute(own_grad, "ens", partner)
-    sums = lax.all_to_all(products, TM_LAT, 0, 0, tiled=True)
+    sums = lax.all_to_all(products, LAT_TM, 0, 0, tiled=True)
     (total,) = call(sum_kernel, [VMEM], [(HALF, LANES)])(sums)
     other_total = lax.ppermute(total, "ens", partner)
     (grad_state,) = call(gradient_kernel, [VMEM] * 2, [whole])(own_grad, other_grad)

time: 79.2 us -> 78 us (0.985)
  waiting for transfers between devices: 5.58 us -> 4.31 us
    ppermute x1, waiting for transfers between devices: 0.84 us -> 0.01 us  [on_device(): outer = lax.ppermute(outer, band, trade)]
  transfers between devices with their start and end apart: 9 -> 9, of which waited for: 4 -> 3; matrix products, arithmetic and copies ran while one was open for 0% -> 0% of each run, Pallas kernels for 12% -> 13%
where the time goes in v8:
time: 78 us; the launch traced here: 77.7 us
  blocking collectives  41.7 us (53%)
  starting transfers between devices  19.5 us (25%)
  Pallas kernels  11.2 us (14%)
  waiting for transfers between devices  4.31 us (6%)
  between operations  0.85 us (1%)
    all_to_all x1, blocking collectives, on_device(): sums = lax.all_to_all(products, LAT_TM, 0, 0, tiled=True)  26.7 us
    all_to_all x1, blocking collectives, on_device(): pieces = lax.all_to_all(forcing, TM, 0, 0, tiled=True)  14.9 us
    ppermute x1, starting transfers between devices, on_device(): outer = lax.ppermute(outer, band, trade)  5.76 us
    ppermute x1, starting transfers between devices, on_device(): mismatch = lax.ppermute(later, TM, [(i, i + 1) for i in range(count_t - 1)])  3.38 us
    ppermute x1, starting transfers between devices, on_device(): other_pert = lax.ppermute(perturbations, 'ens', partner)  3.29 us
    ppermute x1, starting transfers between devices, on_device(): halo = lax.ppermute(outgoing, band, trade)  2.85 us
    pallas_call x1, Pallas kernels, on_device(): call(prepare_kernel, [VMEM, VMEM, HBM, VMEM, SMEM] + [VMEM] * 3, [(5, 12,...  2.44 us
    ppermute x1, waiting for transfers between devices, on_device(): halo = lax.ppermute(outgoing, band, trade)  2.03 us
  transfers between devices with their start and end apart: 9, of which 3 were waited for; matrix products, arithmetic and copies ran while one was open for 0% of the time, Pallas kernels for 13%

profile of v8, /device:TPU:1, one launch (start us, length us, event | category | flops | bytes accessed | tf_op | source)
XLA Modules:
  0.0 77.7 jit_solution(11245979653747701481)
XLA Ops:
  0.7 0.0 copy-start.3
  0.7 3.3 %collective-permute-start.6 = (f32[16,1,16,1440]{3,2,1,0:T(8,128)}, f32[16,1,16,1440]{3,2,1,0:T(8,128)S(1)}, u32[]{:S(2)}, u32[]{:S(2)}) collective-permute-start(f32[16,1,16,1440]{3,2,1,0:T(8,128)} %own_ref.3), channel_id=1, source_target_pairs={{0,1},{1,0},{2,3},{3,2},{4,5},{5,4},{6,7},{7,6},{8,9},{9,8},{10,11... | collective-permute-start | bytes 4423688 | tf_op jit(solution)/shard_map/ppermute | solution.py:552
  4.0 1.7 %shard_map.113 = (f32[79,8,128]{2,1,0:T(8,128)S(1)}, f32[1,8,16,1440]{3,2,1,0:T(8,128)S(1)}, f32[1,8,16,1440]{3,2,1,0:T(8,128)S(1)}, f32[1,8,16,1440]{3,2,1,0:T(8,128)S(1)}) custom-call(f32[1,8,16,1440]{3,2,1,0:T(8,128)} %inc_hbm.1, f32[1,8,16,1440]{3,2,1,0:T(8,128)} %lon_hbm.1, f32[1,8,16,1440]{3,2,1,0:T(8,128)} %lat_hbm.1), custom_call_target="tpu_custom_call" | custom-call | tf_op jit(solution)/shard_map/pallas_call | solution.py:531
  5.7 2.9 %collective-permute-start = (f32[79,8,128]{2,1,0:T(8,128)S(1)}, f32[79,8,128]{2,1,0:T(8,128)S(1)}, u32[]{:S(2)}, u32[]{:S(2)}) collective-permute-start(f32[79,8,128]{2,1,0:T(8,128)S(1)} %get-tuple-element.45), channel_id=1, source_target_pairs={{1,2},{2,1},{3,4},{4,3},{5,6},{6,5},{7,8},{8,7},{9,10},{10,9},{11,... | collective-permute-start | bytes 970760 | tf_op jit(solution)/shard_map/ppermute | solution.py:537
  8.5 0.0 copy-start.2
  8.6 0.3 shard_map.114
  8.8 1.3 %collective-permute-start.1 = (f32[45,8,128]{2,1,0:T(8,128)S(1)}, f32[45,8,128]{2,1,0:T(8,128)S(1)}, u32[]{:S(2)}, u32[]{:S(2)}) collective-permute-start(f32[45,8,128]{2,1,0:T(8,128)S(1)} %get-tuple-element.50), channel_id=1, source_target_pairs={{32,0},{64,32},{96,64},{128,96},{160,128},{192,160},{224,192},{33,... | collective-permute-start | bytes 552968 | tf_op jit(solution)/shard_map/ppermute | solution.py:543
  10.2 2.4 %shard_map.115 = (f32[5,12,8,1536]{3,2,1,0:T(8,128)S(1)}, f32[8,1536]{1,0:T(8,128)S(1)}, f32[16,32]{1,0:T(8,128)S(1)}, f32[3,2,8,1536]{3,2,1,0:T(8,128)S(1)}, f3...) custom-call(f32[1,8,16,1440]{3,2,1,0:T(8,128)S(1)} %get-tuple-element.38.lon_ref, ...), custom_call_target="tpu_custom_call" | custom-call | tf_op jit(solution)/shard_map/pallas_call | solution.py:546
  12.6 1.3 %collective-permute-start.3 = (f32[45,8,128]{2,1,0:T(8,128)S(1)}, f32[45,8,128]{2,1,0:T(8,128)S(1)}, u32[]{:S(2)}, u32[]{:S(2)}) collective-permute-start(f32[45,8,128]{2,1,0:T(8,128)S(1)} %get-tuple-element.56), channel_id=1, source_target_pairs={{32,0},{64,32},{96,64},{128,96},{160,128},{192,160},{224,192},{33,... | collective-permute-start | bytes 552968 | tf_op jit(solution)/shard_map/ppermute | solution.py:555
  13.9 2.0 %collective-permute-done.packed_ref = f32[79,8,128]{2,1,0:T(8,128)S(1)} collective-permute-done((f32[79,8,128]{2,1,0:T(8,128)S(1)}, f32[79,8,128]{2,1,0:T(8,128)S(1)}, u32[]{:S(2)}, u32[]{:S(2)}) %collective-permute-start) | collective-permute-done | bytes 323616 | tf_op jit(solution)/shard_map/ppermute | solution.py:537
  16.0 2.0 %shard_map.116 = (f32[8,8,1536]{2,1,0:T(8,128)S(1)}, f32[8,8,1536]{2,1,0:T(8,128)S(1)}, f32[5,2,8,1536]{3,2,1,0:T(8,128)S(1)}) custom-call(f32[12,8,1536]{2,1,0:T(8,128)S(1)} %get-tuple-element.37.field_ref, f32[5,12,8,1536]{3,2,1,0:T(8,128)S(1)} %get-tuple-element.40.coef_ref, f32[3,2,8,1536]{3,2,1,0:T(8,128)S(1)} %get-tuple-element.41.joint_ref, ...), custom_call_target="tpu_custom_call" | custom-call | tf_op jit(solution)/shard_map/pallas_call | solution.py:556
  18.0 0.0 collective-permute-done.1.packed_ref
  18.0 0.4 shard_map.117
  18.4 1.4 %collective-permute-done.3.packed_ref = f32[45,8,128]{2,1,0:T(8,128)S(1)} collective-permute-done((f32[45,8,128]{2,1,0:T(8,128)S(1)}, f32[45,8,128]{2,1,0:T(8,128)S(1)}, u32[]{:S(2)}, u32[]{:S(2)}) %collective-permute-start.3) | collective-permute-done | bytes 184352 | tf_op jit(solution)/shard_map/ppermute | solution.py:555
  19.8 0.1 shard_map.118
  19.9 0.1 collective-permute-start.4
  20.0 5.8 %collective-permute-start.2 = (f32[45,8,128]{2,1,0:T(8,128)S(1)}, f32[45,8,128]{2,1,0:T(8,128)S(1)}, u32[]{:S(2)}, u32[]{:S(2)}) collective-permute-start(f32[45,8,128]{2,1,0:T(8,128)S(1)} %get-tuple-element.53), channel_id=1, source_target_pairs={{1,2},{2,1},{3,4},{4,3},{5,6},{6,5},{7,8},{8,7},{9,10},{10,9},{11,... | collective-permute-start | bytes 552968 | tf_op jit(solution)/shard_map/ppermute | solution.py:566
  25.8 3.4 %collective-permute-start.5 = (f32[8,8,1536]{2,1,0:T(8,128)S(1)}, f32[8,8,1536]{2,1,0:T(8,128)S(1)}, u32[]{:S(2)}, u32[]{:S(2)}) collective-permute-start(f32[8,8,1536]{2,1,0:T(8,128)S(1)} %get-tuple-element.63), channel_id=1, source_target_pairs={{0,32},{32,64},{64,96},{96,128},{128,160},{160,192},{192,224},{1,3... | collective-permute-start | bytes 1179656 | tf_op jit(solution)/shard_map/ppermute | solution.py:571
  29.2 0.0 collective-permute-done.4.inner_ref
  29.2 1.1 %shard_map.119 = (f32[3,2,8,1536]{3,2,1,0:T(8,128)S(1)}, f32[4,8,1536]{2,1,0:T(8,128)S(1)}, f32[8,8,1536]{2,1,0:T(8,128)S(1)}) custom-call(f32[4,8,1536]{2,1,0:T(8,128)S(1)} %get-tuple-element.52.near_ref.adj_ref, f32[4,8,1536]{2,1,0:T(8,128)S(1)} %get-tuple-element.57.adj_ref, f32[4,8,1536]{2,1,0:T(8,128)S(1)} %collective-permute-done.4.inner_ref, ...), custom_call_target="tpu_custom_call" | custom-call | tf_op jit(solution)/shard_map/pallas_call | solution.py:572
  30.3 0.0 copy-start
  30.3 0.6 shard_map.120
  30.9 14.9 %all_to_all.10.pieces_ref = f32[8,8,1440]{2,1,0:T(8,128)S(1)} all-to-all(f32[8,8,1440]{2,1,0:T(8,128)S(1)} %get-tuple-element.64), channel_id=1, replica_groups=mesh['tm_0'=2,'tm_1'=4,'lat_0'=8,'lat_1'=2,'ens'=2] {'tm_0','tm_1'}, dimensions={0} | all-to-all | bytes 737280 | tf_op jit(solution)/shard_map/all_to_all | solution.py:581
  45.9 0.2 shard_map.121
  46.1 0.1 shard_map.122.own_ref
  46.2 0.1 collective-permute-start.7
  46.3 26.7 %all_to_all.11.sums_ref = f32[128,1,128]{2,1,0:T(1,128)S(1)} all-to-all(f32[128,1,128]{2,1,0:T(1,128)S(1)} %shard_map.121), channel_id=1, replica_groups=mesh['tm_0'=2,'tm_1'=4,'lat_0'=8,'lat_1'=2,'ens'=2] {'lat_0','lat_1','tm..., dimensions={0} | all-to-all | bytes 131072 | tf_op jit(solution)/shard_map/all_to_all | solution.py:589
  73.1 0.1 shard_map.124.sum_ref
  73.2 1.5 %collective-permute-start.8 = (f32[8,128]{1,0:T(8,128)S(1)}, f32[8,128]{1,0:T(8,128)S(1)}, u32[]{:S(2)}, u32[]{:S(2)}) collective-permute-start(f32[8,128]{1,0:T(8,128)S(1)} %shard_map.124.sum_ref), channel_id=1, source_target_pairs={{0,1},{1,0},{2,3},{3,2},{4,5},{5,4},{6,7},{7,6},{8,9},{9,8},{10,11... | collective-permute-start | bytes 12296 | tf_op jit(solution)/shard_map/ppermute | solution.py:591
  74.7 0.8 %collective-permute-done.8.other_sum_ref = f32[8,128]{1,0:T(8,128)S(1)} collective-permute-done((f32[8,128]{1,0:T(8,128)S(1)}, f32[8,128]{1,0:T(8,128)S(1)}, u32[]{:S(2)}, u32[]{:S(2)}) %collective-permute-start.8) | collective-permute-done | bytes 4128 | tf_op jit(solution)/shard_map/ppermute | solution.py:591
  75.5 1.0 %shard_map.125 = f32[1,16,1440]{2,1,0:T(8,128)} custom-call(f32[8,128]{1,0:T(8,128)S(1)} %shard_map.124.sum_ref, f32[8,128]{1,0:T(8,128)S(1)} %collective-permute-done.8.other_sum_ref, f32[16,1,16,1440]{3,2,1,0:T(8,128)S(1)} %copy-done, f32[16,1,16,1440]{3,2,1,0:T(8,128)S(1)} %collective-permute-done.6.other_ref), custom_call_target="tpu_custom_call" | custom-call | tf_op jit(solution)/shard_map/pallas_call | solution.py:593
  76.6 1.1 %shard_map.123 = f32[1,8,16,1440]{3,2,1,0:T(8,128)} custom-call(f32[8,8,1536]{2,1,0:T(8,128)S(1)} %shard_map.122.own_ref, f32[8,8,1536]{2,1,0:T(8,128)S(1)} %collective-permute-done.7.other_ref), custom_call_target="tpu_custom_call" | custom-call | tf_op jit(solution)/shard_map/pallas_call | solution.py:592
  (13 shorter events, 0.0 us)
Async XLA Ops:
  0.6 9.5 %copy-start.1 = (f32[1,32,16]{1,2,0:T(8,128)S(1)}, f32[1,32,16]{1,2,0:T(8,128)}, u32[]{:S(2)}) copy-start(f32[1,32,16]{1,2,0:T(8,128)} %param.18) | copy-start | bytes 6148
  0.6 9.5 %copy-start.4 = (f32[8]{0:T(128)S(1)}, f32[8]{0:T(128)}, u32[]{:S(2)}) copy-start(f32[8]{0:T(128)} %prec_ref.1) | copy-start | bytes 100
  0.7 9.5 %copy-start.3 = (s32[1,32]{1,0:T(1,128)S(1)}, s32[1,32]{1,0:T(1,128)}, u32[]{:S(2)}) copy-start(s32[1,32]{1,0:T(1,128)} %rows_hbm.1) | copy-start | bytes 388
  0.7 9.5 %copy-start.5 = (s32[1,32]{1,0:T(1,128)S(1)}, s32[1,32]{1,0:T(1,128)}, u32[]{:S(2)}) copy-start(s32[1,32]{1,0:T(1,128)} %counts_ref.1) | copy-start | bytes 388
  0.7 45.2 %collective-permute-start.6 = (f32[16,1,16,1440]{3,2,1,0:T(8,128)}, f32[16,1,16,1440]{3,2,1,0:T(8,128)S(1)}, u32[]{:S(2)}, u32[]{:S(2)}) collective-permute-start(f32[16,1,16,1440]{3,2,1,0:T(8,128)} %own_ref.3), channel_id=1, source_target_pairs={{0,1},{1,0},{2,3},{3,2},{4,5},{5,4},{6,7},{7,6},{8,9},{9,8},{10,11... | collective-permute-start | bytes 4423688 | tf_op jit(solution)/shard_map/ppermute | solution.py:552
  5.7 10.3 %collective-permute-start = (f32[79,8,128]{2,1,0:T(8,128)S(1)}, f32[79,8,128]{2,1,0:T(8,128)S(1)}, u32[]{:S(2)}, u32[]{:S(2)}) collective-permute-start(f32[79,8,128]{2,1,0:T(8,128)S(1)} %get-tuple-element.45), channel_id=1, source_target_pairs={{1,2},{2,1},{3,4},{4,3},{5,6},{6,5},{7,8},{8,7},{9,10},{10,9},{11,... | collective-permute-start | bytes 970760 | tf_op jit(solution)/shard_map/ppermute | solution.py:537
  8.5 7.4 %copy-start.2 = (f32[1,32,16]{1,2,0:T(8,128)S(1)}, f32[1,32,16]{1,2,0:T(8,128)}, u32[]{:S(2)}) copy-start(f32[1,32,16]{1,2,0:T(8,128)} %param.17) | copy-start | bytes 6148
  8.8 9.2 %collective-permute-start.1 = (f32[45,8,128]{2,1,0:T(8,128)S(1)}, f32[45,8,128]{2,1,0:T(8,128)S(1)}, u32[]{:S(2)}, u32[]{:S(2)}) collective-permute-start(f32[45,8,128]{2,1,0:T(8,128)S(1)} %get-tuple-element.50), channel_id=1, source_target_pairs={{32,0},{64,32},{96,64},{128,96},{160,128},{192,160},{224,192},{33,... | collective-permute-start | bytes 552968 | tf_op jit(solution)/shard_map/ppermute | solution.py:543
  12.6 7.2 %collective-permute-start.3 = (f32[45,8,128]{2,1,0:T(8,128)S(1)}, f32[45,8,128]{2,1,0:T(8,128)S(1)}, u32[]{:S(2)}, u32[]{:S(2)}) collective-permute-start(f32[45,8,128]{2,1,0:T(8,128)S(1)} %get-tuple-element.56), channel_id=1, source_target_pairs={{32,0},{64,32},{96,64},{128,96},{160,128},{192,160},{224,192},{33,... | collective-permute-start | bytes 552968 | tf_op jit(solution)/shard_map/ppermute | solution.py:555
  19.9 9.2 %collective-permute-start.4 = (f32[4,8,1536]{2,1,0:T(8,128)S(1)}, f32[4,8,1536]{2,1,0:T(8,128)S(1)}, u32[]{:S(2)}, u32[]{:S(2)}) collective-permute-start(f32[4,8,1536]{2,1,0:T(8,128)S(1)} %get-tuple-element.58), channel_id=1, source_target_pairs={{0,1},{1,0},{2,3},{3,2},{4,5},{5,4},{6,7},{7,6},{8,9},{9,8},{10,11... | collective-permute-start | bytes 589832 | tf_op jit(solution)/shard_map/ppermute | solution.py:570
  20.0 10.2 %collective-permute-start.2 = (f32[45,8,128]{2,1,0:T(8,128)S(1)}, f32[45,8,128]{2,1,0:T(8,128)S(1)}, u32[]{:S(2)}, u32[]{:S(2)}) collective-permute-start(f32[45,8,128]{2,1,0:T(8,128)S(1)} %get-tuple-element.53), channel_id=1, source_target_pairs={{1,2},{2,1},{3,4},{4,3},{5,6},{6,5},{7,8},{8,7},{9,10},{10,9},{11,... | collective-permute-start | bytes 552968 | tf_op jit(solution)/shard_map/ppermute | solution.py:566
  25.8 20.3 %collective-permute-start.5 = (f32[8,8,1536]{2,1,0:T(8,128)S(1)}, f32[8,8,1536]{2,1,0:T(8,128)S(1)}, u32[]{:S(2)}, u32[]{:S(2)}) collective-permute-start(f32[8,8,1536]{2,1,0:T(8,128)S(1)} %get-tuple-element.63), channel_id=1, source_target_pairs={{0,32},{32,64},{64,96},{96,128},{128,160},{160,192},{192,224},{1,3... | collective-permute-start | bytes 1179656 | tf_op jit(solution)/shard_map/ppermute | solution.py:571
  30.3 15.6 %copy-start = (f32[16,1,16,1440]{3,2,1,0:T(8,128)S(1)}, f32[16,1,16,1440]{3,2,1,0:T(8,128)}, u32[]{:S(2)}) copy-start(f32[16,1,16,1440]{3,2,1,0:T(8,128)} %own_ref.3) | copy-start | bytes 4423684
  46.2 30.3 %collective-permute-start.7 = (f32[8,8,1536]{2,1,0:T(8,128)S(1)}, f32[8,8,1536]{2,1,0:T(8,128)S(1)}, u32[]{:S(2)}, u32[]{:S(2)}) collective-permute-start(f32[8,8,1536]{2,1,0:T(8,128)S(1)} %shard_map.122.own_ref), channel_id=1, source_target_pairs={{0,1},{1,0},{2,3},{3,2},{4,5},{5,4},{6,7},{7,6},{8,9},{9,8},{10,11... | collective-permute-start | bytes 1179656 | tf_op jit(solution)/shard_map/ppermute | solution.py:588
  73.2 2.3 %collective-permute-start.8 = (f32[8,128]{1,0:T(8,128)S(1)}, f32[8,128]{1,0:T(8,128)S(1)}, u32[]{:S(2)}, u32[]{:S(2)}) collective-permute-start(f32[8,128]{1,0:T(8,128)S(1)} %shard_map.124.sum_ref), channel_id=1, source_target_pairs={{0,1},{1,0},{2,3},{3,2},{4,5},{5,4},{6,7},{7,6},{8,9},{9,8},{10,11... | collective-permute-start | bytes 12296 | tf_op jit(solution)/shard_map/ppermute | solution.py:591
